TPU v7x, 32 devices: a 4x4x1 block of a 4x4x8 slice. The times are simulated.
32 devices in a mesh: sweep: 1 (over z), ent: 32 (over y, x, core).
Axes of the slice: x: 4, y: 4, z: 1, core: 2. Of those that a mesh axis runs over, the one named last changes fastest.
The devices are a block of a 4x4x8 slice.
Arguments:
- ent_emb: float32 [262144, 200], P(('sweep', 'ent'))
- ent_ada: float32 [262144], P(('sweep', 'ent'))
- rel_emb: float32 [237, 200], P('sweep')
- rel_ada: float32 [237], P('sweep')
- head_idx: int32 [32, 16, 2048], P(('sweep', 'ent'))
- tail_idx: int32 [32, 16, 2048], P(('sweep', 'ent'))
- rel_idx: int32 [32, 16, 2048], P(('sweep', 'ent'))
- edge_mask: int32 [32, 16, 2048], P(('sweep', 'ent'))
- neg_idx: int32 [16, 500], P('sweep')
Outputs:
- output 1: float32 [262144, 200], P(('sweep', 'ent'))
- output 2: float32 [262144], P(('sweep', 'ent'))
- output 3: float32 [237, 200], P('sweep')
- output 4: float32 [237], P('sweep')
- output 5: float32 [32, 16], P(('sweep', 'ent'))
All inputs are finite; a program needn't handle non-finite values.
Results may differ from a plain program's by a relative error of at most 0.001.
Values are sent between devices in bfloat16 or wider.
A program may use at most 768 MiB of HBM per device.

v0:
```python
import jax
import jax.numpy as jnp
from jax import lax
from jax.sharding import PartitionSpec as P

LEARN_RATE = 0.05
ADA_EPS = 1e-10


def bucket_grads(head_rows, tail_rows, neg_rows, rel_rows, edge_w):
    half = head_rows.shape[-1] // 2
    head_f = head_rows.astype(jnp.float32)
    h_re = head_f[:, :half]
    h_im = head_f[:, half:]
    r_re = rel_rows[:, :half]
    r_im = rel_rows[:, half:]
    query = jnp.concatenate([h_re * r_re - h_im * r_im, h_re * r_im + h_im * r_re], axis=1)
    query_bf = query.astype(jnp.bfloat16)
    tail_f = tail_rows.astype(jnp.float32)
    pos_score = jnp.sum(query * tail_f, axis=1)
    neg_score = jnp.einsum('bd,nd->bn', query_bf, neg_rows, preferred_element_type=jnp.float32)
    top_score = jnp.maximum(pos_score, jnp.max(neg_score, axis=1))
    pos_exp = jnp.exp(pos_score - top_score)
    neg_exp = jnp.exp(neg_score - top_score[:, None])
    norm_sum = pos_exp + jnp.sum(neg_exp, axis=1)
    log_norm = top_score + jnp.log(norm_sum)
    loss = jnp.sum(edge_w * (log_norm - pos_score)) / edge_w.shape[0]
    pos_grad = edge_w * (pos_exp / norm_sum - 1.0)
    neg_grad = (edge_w[:, None] * neg_exp / norm_sum[:, None]).astype(jnp.bfloat16)
    query_grad = pos_grad[:, None] * tail_f + jnp.einsum('bn,nd->bd', neg_grad, neg_rows, preferred_element_type=jnp.float32)
    tail_grad = pos_grad[:, None] * query
    negrow_grad = jnp.einsum('bn,bd->nd', neg_grad, query_bf, preferred_element_type=jnp.float32)
    g_re = query_grad[:, :half]
    g_im = query_grad[:, half:]
    head_grad = jnp.concatenate([g_re * r_re + g_im * r_im, g_im * r_re - g_re * r_im], axis=1)
    relrow_grad = jnp.concatenate([g_re * h_re + g_im * h_im, g_im * h_re - g_re * h_im], axis=1)
    return loss, head_grad, tail_grad, negrow_grad, relrow_grad


def adagrad_rows(table, state, grad):
    new_state = state + jnp.mean(grad * grad, axis=1)
    return table - LEARN_RATE * grad / jnp.sqrt(new_state + ADA_EPS)[:, None], new_state


def solution(mesh):
    ent_size = mesh.shape['ent']
    row_spec = P(('sweep', 'ent'), None)
    flat_spec = P(('sweep', 'ent'))
    rel_spec = P('sweep', None)
    state_spec = P('sweep')
    edge_spec = P(('sweep', 'ent'), None, None)

    def device_fn(ent_emb, ent_ada, rel_emb, rel_ada, head_idx, tail_idx, rel_idx, edge_mask, neg_idx):
        part_rows = ent_emb.shape[0]
        num_rel = rel_emb.shape[0]
        rounds = head_idx.shape[1]
        my_dev = lax.axis_index('ent')
        table, state, rel_tab, rel_state = ent_emb, ent_ada, rel_emb, rel_ada
        losses = []
        for round_no in range(rounds):
            table_bf = table.astype(jnp.bfloat16)
            if round_no == 0:
                tail_tab = table_bf
            else:
                tail_tab = lax.ppermute(table_bf, 'ent', [(sender, (sender - round_no) % ent_size) for sender in range(ent_size)])
            neg_ids = neg_idx[round_no]
            neg_local = neg_ids % part_rows
            owned = (neg_ids // part_rows) == my_dev
            neg_mine = jnp.where(owned[:, None], jnp.take(table_bf, neg_local, axis=0), jnp.zeros((), jnp.bfloat16))
            neg_rows = lax.psum(neg_mine, 'ent')
            head_ids = head_idx[0, round_no]
            tail_ids = tail_idx[0, round_no]
            rel_ids = rel_idx[0, round_no]
            edge_w = edge_mask[0, round_no].astype(jnp.float32)
            loss, head_grad, tail_grad, negrow_grad, relrow_grad = bucket_grads(
                jnp.take(table_bf, head_ids, axis=0), jnp.take(tail_tab, tail_ids, axis=0),
                neg_rows, jnp.take(rel_tab, rel_ids, axis=0), edge_w)
            losses.append(loss)
            if round_no == 0:
                back_grad, back_ids = tail_grad, tail_ids
            else:
                back_grad, back_ids = lax.ppermute((tail_grad, tail_ids), 'ent', [(sender, (sender + round_no) % ent_size) for sender in range(ent_size)])
            neg_sum = lax.psum(negrow_grad, 'ent')
            rel_sum = lax.psum(jax.ops.segment_sum(relrow_grad, rel_ids, num_segments=num_rel), 'ent')
            row_grads = jnp.concatenate([head_grad, back_grad, jnp.where(owned[:, None], neg_sum, 0.0)], axis=0)
            row_ids = jnp.concatenate([head_ids, back_ids, neg_local], axis=0)
            grad_ent = jax.ops.segment_sum(row_grads, row_ids, num_segments=part_rows)
            table, state = adagrad_rows(table, state, grad_ent)
            rel_tab, rel_state = adagrad_rows(rel_tab, rel_state, rel_sum)
        return table, state, rel_tab, rel_state, jnp.stack(losses)[None, :]

    return jax.shard_map(device_fn, mesh=mesh,
                         in_specs=(row_spec, flat_spec, rel_spec, state_spec, edge_spec, edge_spec, edge_spec, edge_spec, rel_spec),
                         out_specs=(row_spec, flat_spec, rel_spec, state_spec, row_spec), check_vma=False)
```

profile of v0, /device:TPU:97, one launch (start us, length us, event | category | flops | bytes accessed | tf_op | source)
XLA Modules:
  0.0 5568.4 jit_solution(13913981121954914292)
XLA Ops:
  145.2 12.6 scatter_custom_fusion.1
  159.5 93.7 %all-reduce.111.cloned.1.call-done = (f32[500,200]{0,1:T(8,128)}, f32[237,200]{1,0:T(8,128)}) async-done(((f32[500,200]{0,1:T(8,128)}, f32[237,200]{1,0:T(8,128)}), (f32[500,200]{0,1:T(8,128)}, f32[237,200]{1,0:T(8,128)})) %all-reduce.111.cloned.1.call-update) | async-done | bytes 589616 | tf_op jit(solution)/shard_map/psum | solution.py:83
  263.7 27.0 scatter_custom_fusion
  342.0 91.3 %all-reduce.51.cloned.1.call-done = bf16[500,200]{0,1:T(8,128)(2,1)} async-done(((bf16[500,200]{0,1:T(8,128)(2,1)}), bf16[500,200]{0,1:T(8,128)(2,1)}) %all-reduce.51.cloned.1.call-update) | async-done | bytes 200016 | tf_op jit(solution)/shard_map/psum | solution.py:70
  471.3 12.6 scatter_custom_fusion.3
  488.4 91.2 %all-reduce.109.cloned.1.call-done = (f32[500,200]{0,1:T(8,128)}, f32[237,200]{1,0:T(8,128)}) async-done(((f32[500,200]{0,1:T(8,128)}, f32[237,200]{1,0:T(8,128)}), (f32[500,200]{0,1:T(8,128)}, f32[237,200]{1,0:T(8,128)})) %all-reduce.109.cloned.1.call-update) | async-done | bytes 589616 | tf_op jit(solution)/shard_map/psum | solution.py:83
  590.1 27.0 scatter_custom_fusion.2
  675.9 106.4 %all-reduce.53.cloned.1.call-done = bf16[500,200]{0,1:T(8,128)(2,1)} async-done(((bf16[500,200]{0,1:T(8,128)(2,1)}), bf16[500,200]{0,1:T(8,128)(2,1)}) %all-reduce.53.cloned.1.call-update) | async-done | bytes 200016 | tf_op jit(solution)/shard_map/psum | solution.py:70
  822.3 12.7 scatter_custom_fusion.5
  841.2 91.0 %all-reduce.107.cloned.1.call-done = (f32[500,200]{0,1:T(8,128)}, f32[237,200]{1,0:T(8,128)}) async-done(((f32[500,200]{0,1:T(8,128)}, f32[237,200]{1,0:T(8,128)}), (f32[500,200]{0,1:T(8,128)}, f32[237,200]{1,0:T(8,128)})) %all-reduce.107.cloned.1.call-update) | async-done | bytes 589616 | tf_op jit(solution)/shard_map/psum | solution.py:83
  942.6 27.0 scatter_custom_fusion.4
  1022.5 105.6 %all-reduce.55.cloned.1.call-done = bf16[500,200]{0,1:T(8,128)(2,1)} async-done(((bf16[500,200]{0,1:T(8,128)(2,1)}), bf16[500,200]{0,1:T(8,128)(2,1)}) %all-reduce.55.cloned.1.call-update) | async-done | bytes 200016 | tf_op jit(solution)/shard_map/psum | solution.py:70
  1168.0 12.6 scatter_custom_fusion.7
  1184.5 92.3 %all-reduce.105.cloned.1.call-done = (f32[500,200]{0,1:T(8,128)}, f32[237,200]{1,0:T(8,128)}) async-done(((f32[500,200]{0,1:T(8,128)}, f32[237,200]{1,0:T(8,128)}), (f32[500,200]{0,1:T(8,128)}, f32[237,200]{1,0:T(8,128)})) %all-reduce.105.cloned.1.call-update) | async-done | bytes 589616 | tf_op jit(solution)/shard_map/psum | solution.py:83
  1287.3 27.0 scatter_custom_fusion.6
  1373.1 113.4 %all-reduce.57.cloned.1.call-done = bf16[500,200]{0,1:T(8,128)(2,1)} async-done(((bf16[500,200]{0,1:T(8,128)(2,1)}), bf16[500,200]{0,1:T(8,128)(2,1)}) %all-reduce.57.cloned.1.call-update) | async-done | bytes 200016 | tf_op jit(solution)/shard_map/psum | solution.py:70
  1525.7 12.6 scatter_custom_fusion.9
  1542.5 95.0 %all-reduce.103.cloned.1.call-done = (f32[500,200]{0,1:T(8,128)}, f32[237,200]{1,0:T(8,128)}) async-done(((f32[500,200]{0,1:T(8,128)}, f32[237,200]{1,0:T(8,128)}), (f32[500,200]{0,1:T(8,128)}, f32[237,200]{1,0:T(8,128)})) %all-reduce.103.cloned.1.call-update) | async-done | bytes 589616 | tf_op jit(solution)/shard_map/psum | solution.py:83
  1647.9 27.0 scatter_custom_fusion.8
  1728.4 122.5 %all-reduce.59.cloned.1.call-done = bf16[500,200]{0,1:T(8,128)(2,1)} async-done(((bf16[500,200]{0,1:T(8,128)(2,1)}), bf16[500,200]{0,1:T(8,128)(2,1)}) %all-reduce.59.cloned.1.call-update) | async-done | bytes 200016 | tf_op jit(solution)/shard_map/psum | solution.py:70
  1889.4 12.6 scatter_custom_fusion.11
  1907.7 93.7 %all-reduce.101.cloned.1.call-done = (f32[500,200]{0,1:T(8,128)}, f32[237,200]{1,0:T(8,128)}) async-done(((f32[500,200]{0,1:T(8,128)}, f32[237,200]{1,0:T(8,128)}), (f32[500,200]{0,1:T(8,128)}, f32[237,200]{1,0:T(8,128)})) %all-reduce.101.cloned.1.call-update) | async-done | bytes 589616 | tf_op jit(solution)/shard_map/psum | solution.py:83
  2011.8 27.0 scatter_custom_fusion.10
  2097.2 110.2 %all-reduce.61.cloned.1.call-done = bf16[500,200]{0,1:T(8,128)(2,1)} async-done(((bf16[500,200]{0,1:T(8,128)(2,1)}), bf16[500,200]{0,1:T(8,128)(2,1)}) %all-reduce.61.cloned.1.call-update) | async-done | bytes 200016 | tf_op jit(solution)/shard_map/psum | solution.py:70
  2245.6 12.7 scatter_custom_fusion.13
  2263.4 93.2 %all-reduce.99.cloned.1.call-done = (f32[500,200]{0,1:T(8,128)}, f32[237,200]{1,0:T(8,128)}) async-done(((f32[500,200]{0,1:T(8,128)}, f32[237,200]{1,0:T(8,128)}), (f32[500,200]{0,1:T(8,128)}, f32[237,200]{1,0:T(8,128)})) %all-reduce.99.cloned.1.call-update) | async-done | bytes 589616 | tf_op jit(solution)/shard_map/psum | solution.py:83
  2367.0 27.0 scatter_custom_fusion.12
  2447.5 90.8 %all-reduce.63.cloned.1.call-done = bf16[500,200]{0,1:T(8,128)(2,1)} async-done(((bf16[500,200]{0,1:T(8,128)(2,1)}), bf16[500,200]{0,1:T(8,128)(2,1)}) %all-reduce.63.cloned.1.call-update) | async-done | bytes 200016 | tf_op jit(solution)/shard_map/psum | solution.py:70
  2576.0 12.6 scatter_custom_fusion.15
  2595.1 91.3 %all-reduce.97.cloned.1.call-done = (f32[500,200]{0,1:T(8,128)}, f32[237,200]{1,0:T(8,128)}) async-done(((f32[500,200]{0,1:T(8,128)}, f32[237,200]{1,0:T(8,128)}), (f32[500,200]{0,1:T(8,128)}, f32[237,200]{1,0:T(8,128)})) %all-reduce.97.cloned.1.call-update) | async-done | bytes 589616 | tf_op jit(solution)/shard_map/psum | solution.py:83
  2696.8 27.0 scatter_custom_fusion.14
  2782.0 91.8 %all-reduce.65.cloned.1.call-done = bf16[500,200]{0,1:T(8,128)(2,1)} async-done(((bf16[500,200]{0,1:T(8,128)(2,1)}), bf16[500,200]{0,1:T(8,128)(2,1)}) %all-reduce.65.cloned.1.call-update) | async-done | bytes 200016 | tf_op jit(solution)/shard_map/psum | solution.py:70
  2911.6 12.6 scatter_custom_fusion.17
  2930.4 90.9 %all-reduce.95.cloned.1.call-done = (f32[500,200]{0,1:T(8,128)}, f32[237,200]{1,0:T(8,128)}) async-done(((f32[500,200]{0,1:T(8,128)}, f32[237,200]{1,0:T(8,128)}), (f32[500,200]{0,1:T(8,128)}, f32[237,200]{1,0:T(8,128)})) %all-reduce.95.cloned.1.call-update) | async-done | bytes 589616 | tf_op jit(solution)/shard_map/psum | solution.py:83
  3031.8 27.0 scatter_custom_fusion.16
  3110.7 93.5 %all-reduce.67.cloned.1.call-done = bf16[500,200]{0,1:T(8,128)(2,1)} async-done(((bf16[500,200]{0,1:T(8,128)(2,1)}), bf16[500,200]{0,1:T(8,128)(2,1)}) %all-reduce.67.cloned.1.call-update) | async-done | bytes 200016 | tf_op jit(solution)/shard_map/psum | solution.py:70
  3242.5 12.6 scatter_custom_fusion.19
  3261.1 90.1 %all-reduce.93.cloned.1.call-done = (f32[500,200]{0,1:T(8,128)}, f32[237,200]{1,0:T(8,128)}) async-done(((f32[500,200]{0,1:T(8,128)}, f32[237,200]{1,0:T(8,128)}), (f32[500,200]{0,1:T(8,128)}, f32[237,200]{1,0:T(8,128)})) %all-reduce.93.cloned.1.call-update) | async-done | bytes 589616 | tf_op jit(solution)/shard_map/psum | solution.py:83
  3361.7 27.0 scatter_custom_fusion.18
  3445.7 108.4 %all-reduce.69.cloned.1.call-done = bf16[500,200]{0,1:T(8,128)(2,1)} async-done(((bf16[500,200]{0,1:T(8,128)(2,1)}), bf16[500,200]{0,1:T(8,128)(2,1)}) %all-reduce.69.cloned.1.call-update) | async-done | bytes 200016 | tf_op jit(solution)/shard_map/psum | solution.py:70
  3591.4 12.7 scatter_custom_fusion.21
  3612.3 91.5 %all-reduce.91.cloned.1.call-done = (f32[500,200]{0,1:T(8,128)}, f32[237,200]{1,0:T(8,128)}) async-done(((f32[500,200]{0,1:T(8,128)}, f32[237,200]{1,0:T(8,128)}), (f32[500,200]{0,1:T(8,128)}, f32[237,200]{1,0:T(8,128)})) %all-reduce.91.cloned.1.call-update) | async-done | bytes 589616 | tf_op jit(solution)/shard_map/psum | solution.py:83
  3714.2 27.0 scatter_custom_fusion.20
  3792.1 122.0 %all-reduce.71.cloned.1.call-done = bf16[500,200]{0,1:T(8,128)(2,1)} async-done(((bf16[500,200]{0,1:T(8,128)(2,1)}), bf16[500,200]{0,1:T(8,128)(2,1)}) %all-reduce.71.cloned.1.call-update) | async-done | bytes 200016 | tf_op jit(solution)/shard_map/psum | solution.py:70
  3952.6 12.6 scatter_custom_fusion.23
  3969.0 96.1 %all-reduce.89.cloned.1.call-done = (f32[500,200]{0,1:T(8,128)}, f32[237,200]{1,0:T(8,128)}) async-done(((f32[500,200]{0,1:T(8,128)}, f32[237,200]{1,0:T(8,128)}), (f32[500,200]{0,1:T(8,128)}, f32[237,200]{1,0:T(8,128)})) %all-reduce.89.cloned.1.call-update) | async-done | bytes 589616 | tf_op jit(solution)/shard_map/psum | solution.py:83
  4075.6 27.0 scatter_custom_fusion.22
  4158.5 117.1 %all-reduce.73.cloned.1.call-done = bf16[500,200]{0,1:T(8,128)(2,1)} async-done(((bf16[500,200]{0,1:T(8,128)(2,1)}), bf16[500,200]{0,1:T(8,128)(2,1)}) %all-reduce.73.cloned.1.call-update) | async-done | bytes 200016 | tf_op jit(solution)/shard_map/psum | solution.py:70
  4313.7 12.6 scatter_custom_fusion.25
  4330.1 96.2 %all-reduce.87.cloned.1.call-done = (f32[500,200]{0,1:T(8,128)}, f32[237,200]{1,0:T(8,128)}) async-done(((f32[500,200]{0,1:T(8,128)}, f32[237,200]{1,0:T(8,128)}), (f32[500,200]{0,1:T(8,128)}, f32[237,200]{1,0:T(8,128)})) %all-reduce.87.cloned.1.call-update) | async-done | bytes 589616 | tf_op jit(solution)/shard_map/psum | solution.py:83
  4436.8 27.0 scatter_custom_fusion.24
  4513.9 124.5 %all-reduce.75.cloned.1.call-done = bf16[500,200]{0,1:T(8,128)(2,1)} async-done(((bf16[500,200]{0,1:T(8,128)(2,1)}), bf16[500,200]{0,1:T(8,128)(2,1)}) %all-reduce.75.cloned.1.call-update) | async-done | bytes 200016 | tf_op jit(solution)/shard_map/psum | solution.py:70
  4676.8 12.6 scatter_custom_fusion.27
  4693.4 96.6 %all-reduce.85.cloned.1.call-done = (f32[500,200]{0,1:T(8,128)}, f32[237,200]{1,0:T(8,128)}) async-done(((f32[500,200]{0,1:T(8,128)}, f32[237,200]{1,0:T(8,128)}), (f32[500,200]{0,1:T(8,128)}, f32[237,200]{1,0:T(8,128)})) %all-reduce.85.cloned.1.call-update) | async-done | bytes 589616 | tf_op jit(solution)/shard_map/psum | solution.py:83
  4800.5 27.0 scatter_custom_fusion.26
  4881.7 114.2 %all-reduce.77.cloned.1.call-done = bf16[500,200]{0,1:T(8,128)(2,1)} async-done(((bf16[500,200]{0,1:T(8,128)(2,1)}), bf16[500,200]{0,1:T(8,128)(2,1)}) %all-reduce.77.cloned.1.call-update) | async-done | bytes 200016 | tf_op jit(solution)/shard_map/psum | solution.py:70
  5035.1 12.6 scatter_custom_fusion.29
  5051.6 94.5 %all-reduce.83.cloned.1.call-done = (f32[500,200]{0,1:T(8,128)}, f32[237,200]{1,0:T(8,128)}) async-done(((f32[500,200]{0,1:T(8,128)}, f32[237,200]{1,0:T(8,128)}), (f32[500,200]{0,1:T(8,128)}, f32[237,200]{1,0:T(8,128)})) %all-reduce.83.cloned.1.call-update) | async-done | bytes 589616 | tf_op jit(solution)/shard_map/psum | solution.py:83
  5156.5 27.0 scatter_custom_fusion.28
  5233.7 110.2 %all-reduce.79.cloned.1.call-done = bf16[500,200]{0,1:T(8,128)(2,1)} async-done(((bf16[500,200]{0,1:T(8,128)(2,1)}), bf16[500,200]{0,1:T(8,128)(2,1)}) %all-reduce.79.cloned.1.call-update) | async-done | bytes 200016 | tf_op jit(solution)/shard_map/psum | solution.py:70
  5383.1 12.6 scatter_custom_fusion.31
  5401.7 14.4 collective-permute-done.42
  5426.8 69.9 %all-reduce.81.cloned.1.call-done = (f32[500,200]{0,1:T(8,128)}, f32[237,200]{1,0:T(8,128)}) async-done(((f32[500,200]{0,1:T(8,128)}, f32[237,200]{1,0:T(8,128)}), (f32[500,200]{0,1:T(8,128)}, f32[237,200]{1,0:T(8,128)})) %all-reduce.81.cloned.1.call-update) | async-done | bytes 589616 | tf_op jit(solution)/shard_map/psum | solution.py:83
  5510.4 27.0 scatter_custom_fusion.30
  (1783 shorter events, 1800.1 us)
Async XLA Ops:
  7.2 124.7 %all-reduce.49.cloned.1.call-start = ((), (), s32[]{:S(2)}) async-start(), calls=%async_computation | async-start | bytes 409600 | tf_op jit(solution)/shard_map/psum | solution.py:70
  29.4 223.9 %all-reduce.111.cloned.1.call-start = ((), (), s32[]{:S(2)}) async-start(), calls=%async_computation.31 | async-start | bytes 1310720 | tf_op jit(solution)/shard_map/psum | solution.py:83
  30.2 456.6 %collective-permute-start = (s32[2048]{0:T(1024)}, s32[2048]{0:T(1024)}, u32[]{:S(2)}, u32[]{:S(2)}) collective-permute-start(s32[2048]{0:T(1024)} %bitcast.6), channel_id=1, source_target_pairs={{0,1},{1,2},{2,3},{3,4},{4,5},{5,6},{6,7},{7,8},{8,9},{9,10},{10,1... | collective-permute-start | bytes 24584 | tf_op jit(solution)/shard_map/ppermute | solution.py:82
  33.0 805.1 %collective-permute-start.3 = (s32[2048]{0:T(1024)}, s32[2048]{0:T(1024)}, u32[]{:S(2)}, u32[]{:S(2)}) collective-permute-start(s32[2048]{0:T(1024)} %bitcast.11), channel_id=1, source_target_pairs={{0,2},{1,3},{2,4},{3,5},{4,6},{5,7},{6,8},{7,9},{8,10},{9,11},{10,... | collective-permute-start | bytes 24584 | tf_op jit(solution)/shard_map/ppermute | solution.py:82
  34.3 1149.2 %collective-permute-start.6 = (s32[2048]{0:T(1024)}, s32[2048]{0:T(1024)}, u32[]{:S(2)}, u32[]{:S(2)}) collective-permute-start(s32[2048]{0:T(1024)} %bitcast.16), channel_id=1, source_target_pairs={{0,3},{1,4},{2,5},{3,6},{4,7},{5,8},{6,9},{7,10},{8,11},{9,12},{10... | collective-permute-start | bytes 24584 | tf_op jit(solution)/shard_map/ppermute | solution.py:82
  36.1 1505.2 %collective-permute-start.9 = (s32[2048]{0:T(1024)}, s32[2048]{0:T(1024)}, u32[]{:S(2)}, u32[]{:S(2)}) collective-permute-start(s32[2048]{0:T(1024)} %bitcast.21), channel_id=1, source_target_pairs={{0,4},{1,5},{2,6},{3,7},{4,8},{5,9},{6,10},{7,11},{8,12},{9,13},{1... | collective-permute-start | bytes 24584 | tf_op jit(solution)/shard_map/ppermute | solution.py:82
  157.9 275.4 %all-reduce.51.cloned.1.call-start = ((), (), s32[]{:S(2)}) async-start(), calls=%async_computation.1 | async-start | bytes 409600 | tf_op jit(solution)/shard_map/psum | solution.py:70
  308.1 128.9 %collective-permute-start.1 = (bf16[8192,200]{0,1:T(8,128)(2,1)}, bf16[8192,200]{0,1:T(8,128)(2,1)}, u32[]{:S(2)}, u32[]{:S(2)}) collective-permute-start(bf16[8192,200]{0,1:T(8,128)(2,1)} %copy.198), channel_id=1, source_target_pairs={{0,31},{1,0},{2,1},{3,2},{4,3},{5,4},{6,5},{7,6},{8,7},{9,8},{10,9... | collective-permute-start | bytes 9830408 | tf_op jit(solution)/shard_map/ppermute | solution.py:65
  338.7 240.9 %all-reduce.109.cloned.1.call-start = ((), (), s32[]{:S(2)}) async-start(), calls=%async_computation.30 | async-start | bytes 1310720 | tf_op jit(solution)/shard_map/psum | solution.py:83
  486.7 295.6 %all-reduce.53.cloned.1.call-start = ((), (), s32[]{:S(2)}) async-start(), calls=%async_computation.2 | async-start | bytes 409600 | tf_op jit(solution)/shard_map/psum | solution.py:70
  486.8 1418.1 %collective-permute-start.12 = (s32[2048]{0:T(1024)}, s32[2048]{0:T(1024)}, u32[]{:S(2)}, u32[]{:S(2)}) collective-permute-start(s32[2048]{0:T(1024)} %bitcast.26), channel_id=1, source_target_pairs={{0,5},{1,6},{2,7},{3,8},{4,9},{5,10},{6,11},{7,12},{8,13},{9,14},{... | collective-permute-start | bytes 24584 | tf_op jit(solution)/shard_map/ppermute | solution.py:82
  639.8 146.5 %collective-permute-start.4 = (bf16[8192,200]{0,1:T(8,128)(2,1)}, bf16[8192,200]{0,1:T(8,128)(2,1)}, u32[]{:S(2)}, u32[]{:S(2)}) collective-permute-start(bf16[8192,200]{0,1:T(8,128)(2,1)} %copy.206), channel_id=1, source_target_pairs={{0,30},{1,31},{2,0},{3,1},{4,2},{5,3},{6,4},{7,5},{8,6},{9,7},{10,... | collective-permute-start | bytes 9830408 | tf_op jit(solution)/shard_map/ppermute | solution.py:65
  673.1 259.1 %all-reduce.107.cloned.1.call-start = ((), (), s32[]{:S(2)}) async-start(), calls=%async_computation.29 | async-start | bytes 1310720 | tf_op jit(solution)/shard_map/psum | solution.py:83
  838.0 290.1 %all-reduce.55.cloned.1.call-start = ((), (), s32[]{:S(2)}) async-start(), calls=%async_computation.3 | async-start | bytes 409600 | tf_op jit(solution)/shard_map/psum | solution.py:70
  838.1 1423.1 %collective-permute-start.15 = (s32[2048]{0:T(1024)}, s32[2048]{0:T(1024)}, u32[]{:S(2)}, u32[]{:S(2)}) collective-permute-start(s32[2048]{0:T(1024)} %bitcast.31), channel_id=1, source_target_pairs={{0,6},{1,7},{2,8},{3,9},{4,10},{5,11},{6,12},{7,13},{8,14},{9,15},... | collective-permute-start | bytes 24584 | tf_op jit(solution)/shard_map/ppermute | solution.py:82
  986.9 145.1 %collective-permute-start.7 = (bf16[8192,200]{0,1:T(8,128)(2,1)}, bf16[8192,200]{0,1:T(8,128)(2,1)}, u32[]{:S(2)}, u32[]{:S(2)}) collective-permute-start(bf16[8192,200]{0,1:T(8,128)(2,1)} %copy.214), channel_id=1, source_target_pairs={{0,29},{1,30},{2,31},{3,0},{4,1},{5,2},{6,3},{7,4},{8,5},{9,6},{10... | collective-permute-start | bytes 9830408 | tf_op jit(solution)/shard_map/ppermute | solution.py:65
  1019.5 257.4 %all-reduce.105.cloned.1.call-start = ((), (), s32[]{:S(2)}) async-start(), calls=%async_computation.28 | async-start | bytes 1310720 | tf_op jit(solution)/shard_map/psum | solution.py:83
  1183.4 303.1 %all-reduce.57.cloned.1.call-start = ((), (), s32[]{:S(2)}) async-start(), calls=%async_computation.4 | async-start | bytes 409600 | tf_op jit(solution)/shard_map/psum | solution.py:70
  1183.5 1408.0 %collective-permute-start.18 = (s32[2048]{0:T(1024)}, s32[2048]{0:T(1024)}, u32[]{:S(2)}, u32[]{:S(2)}) collective-permute-start(s32[2048]{0:T(1024)} %bitcast.36), channel_id=1, source_target_pairs={{0,7},{1,8},{2,9},{3,10},{4,11},{5,12},{6,13},{7,14},{8,15},{9,16}... | collective-permute-start | bytes 24584 | tf_op jit(solution)/shard_map/ppermute | solution.py:82
  1337.0 153.3 %collective-permute-start.10 = (bf16[8192,200]{0,1:T(8,128)(2,1)}, bf16[8192,200]{0,1:T(8,128)(2,1)}, u32[]{:S(2)}, u32[]{:S(2)}) collective-permute-start(bf16[8192,200]{0,1:T(8,128)(2,1)} %copy.222), channel_id=1, source_target_pairs={{0,28},{1,29},{2,30},{3,31},{4,0},{5,1},{6,2},{7,3},{8,4},{9,5},{1... | collective-permute-start | bytes 9830408 | tf_op jit(solution)/shard_map/ppermute | solution.py:65
  1370.2 267.2 %all-reduce.103.cloned.1.call-start = ((), (), s32[]{:S(2)}) async-start(), calls=%async_computation.27 | async-start | bytes 1310720 | tf_op jit(solution)/shard_map/psum | solution.py:83
  1541.1 309.8 %all-reduce.59.cloned.1.call-start = ((), (), s32[]{:S(2)}) async-start(), calls=%async_computation.5 | async-start | bytes 409600 | tf_op jit(solution)/shard_map/psum | solution.py:70
  1541.2 1385.9 %collective-permute-start.21 = (s32[2048]{0:T(1024)}, s32[2048]{0:T(1024)}, u32[]{:S(2)}, u32[]{:S(2)}) collective-permute-start(s32[2048]{0:T(1024)} %bitcast.41), channel_id=1, source_target_pairs={{0,8},{1,9},{2,10},{3,11},{4,12},{5,13},{6,14},{7,15},{8,16},{9,17... | collective-permute-start | bytes 24584 | tf_op jit(solution)/shard_map/ppermute | solution.py:82
  1692.3 162.5 %collective-permute-start.13 = (bf16[8192,200]{0,1:T(8,128)(2,1)}, bf16[8192,200]{0,1:T(8,128)(2,1)}, u32[]{:S(2)}, u32[]{:S(2)}) collective-permute-start(bf16[8192,200]{0,1:T(8,128)(2,1)} %copy.230), channel_id=1, source_target_pairs={{0,27},{1,28},{2,29},{3,30},{4,31},{5,0},{6,1},{7,2},{8,3},{9,4},{... | collective-permute-start | bytes 9830408 | tf_op jit(solution)/shard_map/ppermute | solution.py:65
  1725.6 275.7 %all-reduce.101.cloned.1.call-start = ((), (), s32[]{:S(2)}) async-start(), calls=%async_computation.26 | async-start | bytes 1310720 | tf_op jit(solution)/shard_map/psum | solution.py:83
  1904.9 302.5 %all-reduce.61.cloned.1.call-start = ((), (), s32[]{:S(2)}) async-start(), calls=%async_computation.6 | async-start | bytes 409600 | tf_op jit(solution)/shard_map/psum | solution.py:70
  1905.0 1353.1 %collective-permute-start.24 = (s32[2048]{0:T(1024)}, s32[2048]{0:T(1024)}, u32[]{:S(2)}, u32[]{:S(2)}) collective-permute-start(s32[2048]{0:T(1024)} %bitcast.46), channel_id=1, source_target_pairs={{0,9},{1,10},{2,11},{3,12},{4,13},{5,14},{6,15},{7,16},{8,17},{9,1... | collective-permute-start | bytes 24584 | tf_op jit(solution)/shard_map/ppermute | solution.py:82
  2061.6 149.7 %collective-permute-start.16 = (bf16[8192,200]{0,1:T(8,128)(2,1)}, bf16[8192,200]{0,1:T(8,128)(2,1)}, u32[]{:S(2)}, u32[]{:S(2)}) collective-permute-start(bf16[8192,200]{0,1:T(8,128)(2,1)} %copy.238), channel_id=1, source_target_pairs={{0,26},{1,27},{2,28},{3,29},{4,30},{5,31},{6,0},{7,1},{8,2},{9,3},... | collective-permute-start | bytes 9830408 | tf_op jit(solution)/shard_map/ppermute | solution.py:65
  2094.1 262.5 %all-reduce.99.cloned.1.call-start = ((), (), s32[]{:S(2)}) async-start(), calls=%async_computation.25 | async-start | bytes 1310720 | tf_op jit(solution)/shard_map/psum | solution.py:83
  2261.1 277.2 %all-reduce.63.cloned.1.call-start = ((), (), s32[]{:S(2)}) async-start(), calls=%async_computation.7 | async-start | bytes 409600 | tf_op jit(solution)/shard_map/psum | solution.py:70
  2261.2 1345.7 %collective-permute-start.27 = (s32[2048]{0:T(1024)}, s32[2048]{0:T(1024)}, u32[]{:S(2)}, u32[]{:S(2)}) collective-permute-start(s32[2048]{0:T(1024)} %bitcast.51), channel_id=1, source_target_pairs={{0,10},{1,11},{2,12},{3,13},{4,14},{5,15},{6,16},{7,17},{8,18},{9,... | collective-permute-start | bytes 24584 | tf_op jit(solution)/shard_map/ppermute | solution.py:82
  2411.4 130.8 %collective-permute-start.19 = (bf16[8192,200]{0,1:T(8,128)(2,1)}, bf16[8192,200]{0,1:T(8,128)(2,1)}, u32[]{:S(2)}, u32[]{:S(2)}) collective-permute-start(bf16[8192,200]{0,1:T(8,128)(2,1)} %copy.246), channel_id=1, source_target_pairs={{0,25},{1,26},{2,27},{3,28},{4,29},{5,30},{6,31},{7,0},{8,1},{9,2}... | collective-permute-start | bytes 9830408 | tf_op jit(solution)/shard_map/ppermute | solution.py:65
  2444.6 241.7 %all-reduce.97.cloned.1.call-start = ((), (), s32[]{:S(2)}) async-start(), calls=%async_computation.24 | async-start | bytes 1310720 | tf_op jit(solution)/shard_map/psum | solution.py:83
  2591.5 282.3 %all-reduce.65.cloned.1.call-start = ((), (), s32[]{:S(2)}) async-start(), calls=%async_computation.8 | async-start | bytes 409600 | tf_op jit(solution)/shard_map/psum | solution.py:70
  2591.6 1376.7 %collective-permute-start.30 = (s32[2048]{0:T(1024)}, s32[2048]{0:T(1024)}, u32[]{:S(2)}, u32[]{:S(2)}) collective-permute-start(s32[2048]{0:T(1024)} %bitcast.56), channel_id=1, source_target_pairs={{0,11},{1,12},{2,13},{3,14},{4,15},{5,16},{6,17},{7,18},{8,19},{9,... | collective-permute-start | bytes 24584 | tf_op jit(solution)/shard_map/ppermute | solution.py:82
  2746.6 131.1 %collective-permute-start.22 = (bf16[8192,200]{0,1:T(8,128)(2,1)}, bf16[8192,200]{0,1:T(8,128)(2,1)}, u32[]{:S(2)}, u32[]{:S(2)}) collective-permute-start(bf16[8192,200]{0,1:T(8,128)(2,1)} %copy.254), channel_id=1, source_target_pairs={{0,24},{1,25},{2,26},{3,27},{4,28},{5,29},{6,30},{7,31},{8,0},{9,1... | collective-permute-start | bytes 9830408 | tf_op jit(solution)/shard_map/ppermute | solution.py:65
  2779.2 242.2 %all-reduce.95.cloned.1.call-start = ((), (), s32[]{:S(2)}) async-start(), calls=%async_computation.23 | async-start | bytes 1310720 | tf_op jit(solution)/shard_map/psum | solution.py:83
  2927.0 277.2 %all-reduce.67.cloned.1.call-start = ((), (), s32[]{:S(2)}) async-start(), calls=%async_computation.9 | async-start | bytes 409600 | tf_op jit(solution)/shard_map/psum | solution.py:70
  2927.1 1402.3 %collective-permute-start.33 = (s32[2048]{0:T(1024)}, s32[2048]{0:T(1024)}, u32[]{:S(2)}, u32[]{:S(2)}) collective-permute-start(s32[2048]{0:T(1024)} %bitcast.61), channel_id=1, source_target_pairs={{0,12},{1,13},{2,14},{3,15},{4,16},{5,17},{6,18},{7,19},{8,20},{9,... | collective-permute-start | bytes 24584 | tf_op jit(solution)/shard_map/ppermute | solution.py:82
  3076.2 131.8 %collective-permute-start.25 = (bf16[8192,200]{0,1:T(8,128)(2,1)}, bf16[8192,200]{0,1:T(8,128)(2,1)}, u32[]{:S(2)}, u32[]{:S(2)}) collective-permute-start(bf16[8192,200]{0,1:T(8,128)(2,1)} %copy.262), channel_id=1, source_target_pairs={{0,23},{1,24},{2,25},{3,26},{4,27},{5,28},{6,29},{7,30},{8,31},{9,... | collective-permute-start | bytes 9830408 | tf_op jit(solution)/shard_map/ppermute | solution.py:65
  3107.7 243.5 %all-reduce.93.cloned.1.call-start = ((), (), s32[]{:S(2)}) async-start(), calls=%async_computation.22 | async-start | bytes 1310720 | tf_op jit(solution)/shard_map/psum | solution.py:83
  3257.9 296.1 %all-reduce.69.cloned.1.call-start = ((), (), s32[]{:S(2)}) async-start(), calls=%async_computation.10 | async-start | bytes 409600 | tf_op jit(solution)/shard_map/psum | solution.py:70
  3258.0 1434.7 %collective-permute-start.36 = (s32[2048]{0:T(1024)}, s32[2048]{0:T(1024)}, u32[]{:S(2)}, u32[]{:S(2)}) collective-permute-start(s32[2048]{0:T(1024)} %bitcast.66), channel_id=1, source_target_pairs={{0,13},{1,14},{2,15},{3,16},{4,17},{5,18},{6,19},{7,20},{8,21},{9,... | collective-permute-start | bytes 24584 | tf_op jit(solution)/shard_map/ppermute | solution.py:82
  3411.4 146.5 %collective-permute-start.28 = (bf16[8192,200]{0,1:T(8,128)(2,1)}, bf16[8192,200]{0,1:T(8,128)(2,1)}, u32[]{:S(2)}, u32[]{:S(2)}) collective-permute-start(bf16[8192,200]{0,1:T(8,128)(2,1)} %copy.270), channel_id=1, source_target_pairs={{0,22},{1,23},{2,24},{3,25},{4,26},{5,27},{6,28},{7,29},{8,30},{9,... | collective-permute-start | bytes 9830408 | tf_op jit(solution)/shard_map/ppermute | solution.py:65
  3442.7 261.0 %all-reduce.91.cloned.1.call-start = ((), (), s32[]{:S(2)}) async-start(), calls=%async_computation.21 | async-start | bytes 1310720 | tf_op jit(solution)/shard_map/psum | solution.py:83
  3606.8 307.3 %all-reduce.71.cloned.1.call-start = ((), (), s32[]{:S(2)}) async-start(), calls=%async_computation.11 | async-start | bytes 409600 | tf_op jit(solution)/shard_map/psum | solution.py:70
  3606.9 1443.9 %collective-permute-start.39 = (s32[2048]{0:T(1024)}, s32[2048]{0:T(1024)}, u32[]{:S(2)}, u32[]{:S(2)}) collective-permute-start(s32[2048]{0:T(1024)} %bitcast.71), channel_id=1, source_target_pairs={{0,14},{1,15},{2,16},{3,17},{4,18},{5,19},{6,20},{7,21},{8,22},{9,... | collective-permute-start | bytes 24584 | tf_op jit(solution)/shard_map/ppermute | solution.py:82
  3758.5 159.5 %collective-permute-start.31 = (bf16[8192,200]{0,1:T(8,128)(2,1)}, bf16[8192,200]{0,1:T(8,128)(2,1)}, u32[]{:S(2)}, u32[]{:S(2)}) collective-permute-start(bf16[8192,200]{0,1:T(8,128)(2,1)} %copy.278), channel_id=1, source_target_pairs={{0,21},{1,22},{2,23},{3,24},{4,25},{5,26},{6,27},{7,28},{8,29},{9,... | collective-permute-start | bytes 9830408 | tf_op jit(solution)/shard_map/ppermute | solution.py:65
  3789.3 275.8 %all-reduce.89.cloned.1.call-start = ((), (), s32[]{:S(2)}) async-start(), calls=%async_computation.20 | async-start | bytes 1310720 | tf_op jit(solution)/shard_map/psum | solution.py:83
  3942.0 124.1 %collective-permute-start.32 = (f32[2048,200]{0,1:T(8,128)}, f32[2048,200]{0,1:T(8,128)}, u32[]{:S(2)}, u32[]{:S(2)}) collective-permute-start(f32[2048,200]{0,1:T(8,128)} %fusion.72), channel_id=1, source_target_pairs={{0,11},{1,12},{2,13},{3,14},{4,15},{5,16},{6,17},{7,18},{8,19},{9,... | collective-permute-start | bytes 4915208 | tf_op jit(solution)/shard_map/ppermute | solution.py:82
  3968.0 307.6 %all-reduce.73.cloned.1.call-start = ((), (), s32[]{:S(2)}) async-start(), calls=%async_computation.12 | async-start | bytes 409600 | tf_op jit(solution)/shard_map/psum | solution.py:70
  4125.4 154.1 %collective-permute-start.34 = (bf16[8192,200]{0,1:T(8,128)(2,1)}, bf16[8192,200]{0,1:T(8,128)(2,1)}, u32[]{:S(2)}, u32[]{:S(2)}) collective-permute-start(bf16[8192,200]{0,1:T(8,128)(2,1)} %copy.286), channel_id=1, source_target_pairs={{0,20},{1,21},{2,22},{3,23},{4,24},{5,25},{6,26},{7,27},{8,28},{9,... | collective-permute-start | bytes 9830408 | tf_op jit(solution)/shard_map/ppermute | solution.py:65
  4155.4 270.9 %all-reduce.87.cloned.1.call-start = ((), (), s32[]{:S(2)}) async-start(), calls=%async_computation.19 | async-start | bytes 1310720 | tf_op jit(solution)/shard_map/psum | solution.py:83
  4329.2 309.2 %all-reduce.75.cloned.1.call-start = ((), (), s32[]{:S(2)}) async-start(), calls=%async_computation.13 | async-start | bytes 409600 | tf_op jit(solution)/shard_map/psum | solution.py:70
  4481.1 161.1 %collective-permute-start.37 = (bf16[8192,200]{0,1:T(8,128)(2,1)}, bf16[8192,200]{0,1:T(8,128)(2,1)}, u32[]{:S(2)}, u32[]{:S(2)}) collective-permute-start(bf16[8192,200]{0,1:T(8,128)(2,1)} %copy.294), channel_id=1, source_target_pairs={{0,19},{1,20},{2,21},{3,22},{4,23},{5,24},{6,25},{7,26},{8,27},{9,... | collective-permute-start | bytes 9830408 | tf_op jit(solution)/shard_map/ppermute | solution.py:65
  4511.0 279.0 %all-reduce.85.cloned.1.call-start = ((), (), s32[]{:S(2)}) async-start(), calls=%async_computation.18 | async-start | bytes 1310720 | tf_op jit(solution)/shard_map/psum | solution.py:83
  4666.3 124.7 %collective-permute-start.38 = (f32[2048,200]{0,1:T(8,128)}, f32[2048,200]{0,1:T(8,128)}, u32[]{:S(2)}, u32[]{:S(2)}) collective-permute-start(f32[2048,200]{0,1:T(8,128)} %fusion.68), channel_id=1, source_target_pairs={{0,13},{1,14},{2,15},{3,16},{4,17},{5,18},{6,19},{7,20},{8,21},{9,... | collective-permute-start | bytes 4915208 | tf_op jit(solution)/shard_map/ppermute | solution.py:82
  4692.2 303.7 %all-reduce.77.cloned.1.call-start = ((), (), s32[]{:S(2)}) async-start(), calls=%async_computation.14 | async-start | bytes 409600 | tf_op jit(solution)/shard_map/psum | solution.py:70
  4850.2 149.5 %collective-permute-start.40 = (bf16[8192,200]{0,1:T(8,128)(2,1)}, bf16[8192,200]{0,1:T(8,128)(2,1)}, u32[]{:S(2)}, u32[]{:S(2)}) collective-permute-start(bf16[8192,200]{0,1:T(8,128)(2,1)} %copy.302), channel_id=1, source_target_pairs={{0,18},{1,19},{2,20},{3,21},{4,22},{5,23},{6,24},{7,25},{8,26},{9,... | collective-permute-start | bytes 9830408 | tf_op jit(solution)/shard_map/ppermute | solution.py:65
  4878.9 267.2 %all-reduce.83.cloned.1.call-start = ((), (), s32[]{:S(2)}) async-start(), calls=%async_computation.17 | async-start | bytes 1310720 | tf_op jit(solution)/shard_map/psum | solution.py:83
  5050.5 293.3 %all-reduce.79.cloned.1.call-start = ((), (), s32[]{:S(2)}) async-start(), calls=%async_computation.15 | async-start | bytes 409600 | tf_op jit(solution)/shard_map/psum | solution.py:70
  5200.9 146.9 %collective-permute-start.43 = (bf16[8192,200]{0,1:T(8,128)(2,1)}, bf16[8192,200]{0,1:T(8,128)(2,1)}, u32[]{:S(2)}, u32[]{:S(2)}) collective-permute-start(bf16[8192,200]{0,1:T(8,128)(2,1)} %copy.310), channel_id=1, source_target_pairs={{0,17},{1,18},{2,19},{3,20},{4,21},{5,22},{6,23},{7,24},{8,25},{9,... | collective-permute-start | bytes 9830408 | tf_op jit(solution)/shard_map/ppermute | solution.py:65
  5230.6 266.1 %all-reduce.81.cloned.1.call-start = ((), (), s32[]{:S(2)}) async-start(), calls=%async_computation.16 | async-start | bytes 1310720 | tf_op jit(solution)/shard_map/psum | solution.py:83
  5376.8 124.4 %collective-permute-start.44 = (f32[2048,200]{0,1:T(8,128)}, f32[2048,200]{0,1:T(8,128)}, u32[]{:S(2)}, u32[]{:S(2)}) collective-permute-start(f32[2048,200]{0,1:T(8,128)} %fusion.64), channel_id=1, source_target_pairs={{0,15},{1,16},{2,17},{3,18},{4,19},{5,20},{6,21},{7,22},{8,23},{9,... | collective-permute-start | bytes 4915208 | tf_op jit(solution)/shard_map/ppermute | solution.py:82
  (463 other events, 10049.0 us)
Sparse Core Ops, SparseCore 0:
  29.5 96.3 all-reduce.48
  158.0 95.2 all-reduce.110
  338.8 94.4 all-reduce.50
  486.9 92.6 all-reduce.108
  673.2 109.1 all-reduce.52
  838.1 93.9 all-reduce.106
  1019.6 108.4 all-reduce.54
  1183.6 93.2 all-reduce.104
  1370.4 116.0 all-reduce.56
  1541.3 96.1 all-reduce.102
  1725.7 125.1 all-reduce.58
  1905.0 96.3 all-reduce.100
  2094.2 113.1 all-reduce.60
  2261.2 95.3 all-reduce.98
  2444.8 93.5 all-reduce.62
  2591.6 94.7 all-reduce.96
  2779.3 94.4 all-reduce.64
  2927.1 94.1 all-reduce.94
  3107.8 96.3 all-reduce.66
  3258.1 93.0 all-reduce.92
  3442.9 111.1 all-reduce.68
  3606.9 96.7 all-reduce.90
  3789.4 124.6 all-reduce.70
  3968.1 96.9 all-reduce.88
  4155.6 119.9 all-reduce.72
  4329.3 96.9 all-reduce.86
  4511.1 127.1 all-reduce.74
  4692.3 97.6 all-reduce.84
  4879.0 116.8 all-reduce.76
  5050.7 95.3 all-reduce.82
  5230.7 113.0 all-reduce.78
  5398.6 97.9 all-reduce.80
where the time goes:
time: 5580 us; the launch traced here: 5570 us
  waiting for transfers between devices  3110 us (56%)
  other arithmetic  1220 us (22%)
  local copies, waits for them, and re-layouts  991 us (18%)
  starting transfers between devices  114 us (2%)
  matrix products  112 us (2%)
    psum x16, waiting for transfers between devices, device_fn(): neg_rows = lax.psum(neg_mine, 'ent')  1620 us
    psum x16, waiting for transfers between devices, device_fn(): neg_sum = lax.psum(negrow_grad, 'ent')  1470 us
    scatter-add x16, other arithmetic, device_fn(): grad_ent = jax.ops.segment_sum(row_grads, row_ids, num_segments=part_rows)  432 us
    scatter-add x16, other arithmetic, device_fn(): jax.ops.segment_sum(relrow_grad, rel_ids, num_segments=num_rel)  202 us
    gather x32, local copies, waits for them, and re-layouts, device_fn(): jnp.take(tail_tab, tail_ids, axis=0)  202 us
    gather x32, local copies, waits for them, and re-layouts, device_fn(): jnp.take(table_bf, head_ids, axis=0)  178 us
    gather x32, local copies, waits for them, and re-layouts, device_fn(): jnp.take(rel_tab, rel_ids, axis=0)  134 us
    convert_element_type x16, other arithmetic, device_fn(): table_bf = table.astype(jnp.bfloat16)  125 us
  transfers between devices with their start and end apart: 77, of which 32 were waited for; matrix products, arithmetic and copies ran while one was open for 38% of the time, Pallas kernels for 0%

commit v1 on v0

v1 whole, which is shorter than its diff:
```python
import functools

import jax
import jax.numpy as jnp
from jax import lax
from jax.experimental import pallas as pl
from jax.experimental.pallas import tpu as pltpu
from jax.sharding import PartitionSpec as P

LEARN_RATE = 0.05
ADA_EPS = 1e-10
LANES = 128
CHUNK = 256
PACK_ROWS = 1024
F32, BF16, I32 = jnp.float32, jnp.bfloat16, jnp.int32
MESH = pl.DeviceIdType.MESH
VMEM = pltpu.VMEM


def round_up(value, multiple):
    return -(-value // multiple) * multiple


class Dims:
    def __init__(self, mesh, ent_emb, rel_emb, head_idx, neg_idx):
        self.ent = mesh.shape['ent']
        self.chips = self.ent // 2
        self.rows, self.dim = ent_emb.shape
        self.half = self.dim // 2
        self.hp = round_up(self.half, 8)
        self.dc = 2 * self.hp
        self.num_rel = rel_emb.shape[0]
        self.relp = round_up(self.num_rel, LANES)
        self.rounds, self.edges = head_idx.shape[1:]
        self.nch = self.edges // CHUNK
        self.neg = neg_idx.shape[1]
        self.negp = round_up(self.neg, self.ent * 16)
        self.negc = self.negp // self.ent
        self.cols = (self.relp + self.negp) // LANES
        self.tiles = self.dc // 8 * self.cols
        self.tpd = -(-self.tiles // self.ent)
        self.trows = 2 * self.rows + 16


def nt_dot(lhs, rhs):
    return lax.dot_general(lhs, rhs, (((1,), (1,)), ((), ())), preferred_element_type=F32)


def nn_dot(lhs, rhs):
    return jnp.dot(lhs, rhs, preferred_element_type=F32)


def split3(x):
    hi = x.astype(BF16)
    rest = x - hi.astype(F32)
    mid = rest.astype(BF16)
    lo = (rest - mid.astype(F32)).astype(BF16)
    return hi, mid, lo


def iota(shape, dim):
    return lax.broadcasted_iota(I32, shape, dim)


def eye(n):
    return jnp.where(iota((n, n), 0) == iota((n, n), 1), 1.0, 0.0).astype(BF16)


def compact_sel(dims, out_rows):
    c = iota((out_rows, 2 * LANES), 0)
    lane = iota((out_rows, 2 * LANES), 1)
    src = jnp.where(c < dims.hp, c, c - dims.hp + LANES)
    return jnp.where((lane == src) & (c < dims.dc), 1.0, 0.0).astype(BF16)


def pack_kernel(half, last, e_ref, g_ref, o_ref):
    step = pl.program_id(0)
    lane = iota((LANES, LANES), 1)

    @pl.when(step < last)
    def _():
        g_cols = jnp.transpose(g_ref[...])
        for i in range(PACK_ROWS // LANES):
            rows = pl.ds(i * LANES, LANES)
            lo = e_ref[rows, :LANES]
            hi = e_ref[rows, LANES:]
            shift = LANES - half
            im = jnp.where(lane < shift, pltpu.roll(lo, shift, 1), pltpu.roll(hi, shift, 1))
            im = jnp.where(lane < half, im, 0.0)
            im = jnp.where(lane == LANES - 1, g_cols[:, i:i + 1], im)
            o_ref[pl.ds(2 * i * LANES, LANES, stride=2), :] = jnp.where(lane < half, lo, 0.0)
            o_ref[pl.ds(2 * i * LANES + 1, LANES, stride=2), :] = im

    @pl.when(step == last)
    def _():
        o_ref[...] = jnp.zeros_like(o_ref)


def pack(dims, emb, ada):
    blocks = dims.rows // PACK_ROWS
    return pl.pallas_call(
        functools.partial(pack_kernel, dims.half, blocks),
        grid=(blocks + 1,),
        out_shape=jax.ShapeDtypeStruct((dims.trows, LANES), F32),
        in_specs=[pl.BlockSpec((PACK_ROWS, 2 * LANES), lambda i: (jnp.minimum(i, blocks - 1), 0)),
                  pl.BlockSpec((PACK_ROWS // LANES, LANES), lambda i: (jnp.minimum(i, blocks - 1), 0))],
        out_specs=pl.BlockSpec((2 * PACK_ROWS, LANES), lambda i: (i, 0)),
        name='pack')(emb, ada.reshape(dims.rows // LANES, LANES))


def unpack_kernel(half, t_ref, e_ref, g_ref):
    lane = iota((LANES, LANES), 1)
    g_cols = jnp.zeros((LANES, LANES), F32)
    for i in range(PACK_ROWS // LANES):
        rows = pl.ds(i * LANES, LANES)
        re = t_ref[pl.ds(2 * i * LANES, LANES, stride=2), :]
        im = t_ref[pl.ds(2 * i * LANES + 1, LANES, stride=2), :]
        im_hi = pltpu.roll(im, half, 1)
        e_ref[rows, :LANES] = jnp.where(lane < half, re, im_hi)
        e_ref[rows, LANES:] = im_hi
        g_cols = jnp.where(lane == i, im[:, LANES - 1:], g_cols)
    g_ref[...] = jnp.transpose(g_cols)[:PACK_ROWS // LANES, :]


def unpack(dims, table):
    blocks = dims.rows // PACK_ROWS
    emb, ada = pl.pallas_call(
        functools.partial(unpack_kernel, dims.half),
        grid=(blocks,),
        out_shape=[jax.ShapeDtypeStruct((dims.rows, dims.dim), F32),
                   jax.ShapeDtypeStruct((dims.rows // LANES, LANES), F32)],
        in_specs=[pl.BlockSpec((2 * PACK_ROWS, LANES), lambda i: (i, 0))],
        out_specs=[pl.BlockSpec((PACK_ROWS, 2 * LANES), lambda i: (i, 0)),
                   pl.BlockSpec((PACK_ROWS // LANES, LANES), lambda i: (i, 0))],
        name='unpack')(table)
    return emb, ada.reshape(dims.rows)


def index_kernel(dims, x_ref, o_ref, send_sem, recv_sem):
    me = lax.axis_index('ent')
    barrier = pltpu.get_barrier_semaphore()
    for s in range(1, dims.rounds):
        pl.semaphore_signal(barrier, inc=1, device_id={'ent': lax.rem(me + dims.ent - s, dims.ent)}, device_id_type=MESH)
    pl.semaphore_wait(barrier, dims.rounds - 1)
    copies = [pltpu.make_async_remote_copy(
        src_ref=x_ref.at[s], dst_ref=o_ref.at[s], send_sem=send_sem.at[s], recv_sem=recv_sem.at[s],
        device_id={'ent': lax.rem(me + s, dims.ent)}, device_id_type=MESH) for s in range(1, dims.rounds)]
    for copy in copies:
        copy.start()
    o_ref[0] = x_ref[0]
    for copy in copies:
        copy.wait()


def exchange_indices(dims, both):
    return pl.pallas_call(
        functools.partial(index_kernel, dims),
        out_shape=jax.ShapeDtypeStruct(both.shape, I32),
        in_specs=[pl.BlockSpec(memory_space=VMEM)], out_specs=pl.BlockSpec(memory_space=VMEM),
        scratch_shapes=[pltpu.SemaphoreType.DMA((dims.rounds,))] * 2,
        name='index_exchange',
        compiler_params=pltpu.CompilerParams(collective_id=0, has_side_effects=True))(both)


UNROLL_SCATTER = 16
UNROLL_GATHER = 64
UPDATE_ROWS = 64


def table_kernel(dims, old, new, head_ids, tail_ids, neg_ids, *refs):
    refs = list(refs)
    if old is not None:
        head_g, tail_g, neg_g = refs[:3]
        refs = refs[3:]
    table_in = refs.pop(0)
    if old is not None:
        table = refs.pop(0)
    else:
        table = table_in
    if new is not None:
        head_out, tail_out, neg_out = refs[:3]
        refs = refs[3:]
    ids, sem = refs[:2]
    refs = refs[2:]
    if old is not None:
        acc_a, acc_b = refs[:2]
        refs = refs[2:]
    if new is not None:
        stage, = refs

    edges, negp = dims.edges, dims.negp
    copies = []
    for base, step in ((0, old), (1, new)):
        if step is not None:
            for k, (src, size) in enumerate(((head_ids, edges), (tail_ids, edges), (neg_ids, negp))):
                copies.append(pltpu.make_async_copy(src.at[pl.ds(step * size, size)], ids[3 * base + k], sem.at[3 * base + k]))
    for copy in copies:
        copy.start()

    if old is not None:
        def zero(c, _):
            rows = pl.ds(pl.multiple_of(c * 128, 128), 128)
            acc_a[rows, :] = jnp.zeros((128, LANES), F32)
            acc_b[rows, :] = jnp.zeros((128, LANES), F32)
            return 0
        lax.fori_loop(0, 2 * dims.rows // 128, zero, 0)
    for copy in copies:
        copy.wait()

    def pair(k):
        return pl.ds(pl.multiple_of(2 * k, 2), 2)

    def at(ref, k):
        return pl.ds(pl.multiple_of(ref[k], 2), 2)

    if old is not None:
        old_h, old_t, old_n = ids[:3]

        def scatter(c, _):
            for u in range(UNROLL_SCATTER):
                k = c * UNROLL_SCATTER + u
                h, t = at(old_h, k), at(old_t, k)
                new_a = acc_a[h, :] + head_g[pair(k), :]
                new_b = acc_b[t, :] + tail_g[pair(k), :]
                acc_a[h, :] = new_a
                acc_b[t, :] = new_b
            return 0
        lax.fori_loop(0, edges // UNROLL_SCATTER, scatter, 0)

        def scatter_neg(c, _):
            for u in range(UNROLL_SCATTER // 2):
                k = c * UNROLL_SCATTER + 2 * u
                h, t = at(old_n, k), at(old_n, k + 1)
                new_a = acc_a[h, :] + neg_g[pair(k), :]
                new_b = acc_b[t, :] + neg_g[pair(k + 1), :]
                acc_a[h, :] = new_a
                acc_b[t, :] = new_b
            return 0
        lax.fori_loop(0, negp // UNROLL_SCATTER, scatter_neg, 0)

        lane = iota((UPDATE_ROWS, LANES), 1)

        def update(c, _):
            re = pl.ds(pl.multiple_of(c * 2 * UPDATE_ROWS, 2 * UPDATE_ROWS), UPDATE_ROWS, stride=2)
            im = pl.ds(pl.multiple_of(c * 2 * UPDATE_ROWS, 2 * UPDATE_ROWS) + 1, UPDATE_ROWS, stride=2)
            g_re = acc_a[re, :] + acc_b[re, :]
            g_im = acc_a[im, :] + acc_b[im, :]
            e_re, e_im = table_in[re, :], table_in[im, :]
            part = (g_re * g_re + g_im * g_im) * (1.0 / dims.dim)
            part = jnp.where(lane == LANES - 1, e_im, part)
            state = jnp.sum(part, axis=1, keepdims=True)
            rate = LEARN_RATE / jnp.sqrt(state + ADA_EPS)
            table[re, :] = e_re - rate * g_re
            table[im, :] = jnp.where(lane == LANES - 1, state, e_im - rate * g_im)
            return 0
        lax.fori_loop(0, dims.rows // UPDATE_ROWS, update, 0)
        table[pl.ds(2 * dims.rows, 16), :] = jnp.zeros((16, LANES), F32)

    if new is not None:
        new_h, new_t, new_n = ids[3:]
        sel = compact_sel(dims, 2 * LANES)

        def gather(ref, count):
            def body(c, _):
                for u in range(UNROLL_GATHER):
                    k = c * UNROLL_GATHER + u
                    stage[pair(k), :] = table[at(ref, k), :]
                return 0
            lax.fori_loop(0, count // UNROLL_GATHER, body, 0)

        def staged(c):
            re = stage[pl.ds(pl.multiple_of(c * 2 * CHUNK, 2 * CHUNK), CHUNK, stride=2), :]
            im = stage[pl.ds(pl.multiple_of(c * 2 * CHUNK, 2 * CHUNK) + 1, CHUNK, stride=2), :]
            return jnp.concatenate([re.astype(BF16), im.astype(BF16)], axis=1)

        for ref, out in ((new_t, tail_out), (new_h, head_out)):
            gather(ref, edges)

            def convert(c, _):
                out[c] = nt_dot(sel[:dims.dc], staged(c)).astype(BF16)
                return 0
            lax.fori_loop(0, dims.nch, convert, 0)
        gather(new_n, negp)
        for c in range(negp // CHUNK):
            rows = nt_dot(staged(c), sel).astype(BF16)
            neg_out[pl.ds(c * CHUNK, CHUNK), :] = rows


def table_step(dims, old, new, ids, grads, table):
    vm = pl.BlockSpec(memory_space=VMEM)
    anys = pl.BlockSpec(memory_space=pl.ANY)
    in_specs = [anys] * 3
    operands = list(ids)
    outs, aliases = [], {}
    smem = lambda n: pltpu.SMEM((n,), I32)
    sizes = (dims.edges, dims.edges, dims.negp)
    if old is not None:
        in_specs += [vm] * 3
        operands += list(grads)
        aliases = {len(operands): 0}
        outs.append(jax.ShapeDtypeStruct((dims.trows, LANES), F32))
    in_specs.append(vm)
    operands.append(table)
    if new is not None:
        outs += [jax.ShapeDtypeStruct((dims.nch, dims.dc, CHUNK), BF16)] * 2
        outs.append(jax.ShapeDtypeStruct((dims.negp, 2 * LANES), BF16))
    id_scratch = [smem(n) for n in sizes] * 2
    scratch = [pltpu.SemaphoreType.DMA((6,))]
    if old is not None:
        scratch += [VMEM((dims.trows, LANES), F32)] * 2
    if new is not None:
        scratch += [VMEM((2 * dims.edges, LANES), F32)]

    def body(*refs):
        n = len(operands) + len(outs)
        table_kernel(dims, old, new, *refs[:n], refs[n:n + 6], *refs[n + 6:])

    res = pl.pallas_call(
        body, out_shape=outs, in_specs=in_specs, out_specs=[vm] * len(outs),
        scratch_shapes=id_scratch + scratch, input_output_aliases=aliases,
        name=f'table_{"x" if old is None else "u"}{"x" if new is None else "g"}',
        compiler_params=pltpu.CompilerParams(vmem_limit_bytes=34 << 20))(*operands)
    return res


def bucket_kernel(dims, s, head, tail, neg, rel_t, rel_state, rel_ids, rel_ids_p, weight,
                  head_g, tail_g, neg_g, rel_t_out, rel_state_out, loss,
                  tail_r, head_r, dp_s, dp_r, splits, qb, dsb, neg_p, neg_half, neg_buf, neg_acc, neg_all, neg_t,
                  acc_rel, acc_neg, head_c, x_ar, p_ar, half_ar, buf_ar, acc_ar, o_ar,
                  tail_ss, tail_rs, head_ss, head_rs, one_s, one_r, rs_s, rs_r, ag_s, ag_r, rs2_s, rs2_r, ag2_s, ag2_r):
    ent, chips, hp, dc, nch = dims.ent, dims.chips, dims.hp, dims.dc, dims.nch
    me = lax.axis_index('ent')
    core, chip = lax.rem(me, 2), me // 2
    partner = me + 1 - 2 * core
    dst_t = lax.rem(me + ent - s, ent)
    dst_h = lax.rem(me + s, ent)

    def dev(d):
        return {'ent': d}

    def peer(k):
        return lax.rem(chip + k, chips) * 2 + core

    def remote(src, dst, ss, rs, d):
        return pltpu.make_async_remote_copy(src_ref=src, dst_ref=dst, send_sem=ss, recv_sem=rs, device_id=dev(d), device_id_type=MESH)

    barrier = pltpu.get_barrier_semaphore()

    def signal(k, _):
        pl.semaphore_signal(barrier, inc=1, device_id=dev(peer(k)), device_id_type=MESH)
        return 0
    pl.semaphore_signal(barrier, inc=1, device_id=dev(partner), device_id_type=MESH)
    if s:
        pl.semaphore_signal(barrier, inc=1, device_id=dev(dst_t), device_id_type=MESH)
        pl.semaphore_signal(barrier, inc=1, device_id=dev(dst_h), device_id_type=MESH)
    lax.fori_loop(1, chips, signal, 0)

    for i, part in enumerate(split3(rel_t[...])):
        splits[pl.ds(i * dc, dc), :] = part
    qb[pl.ds(dc, 2 * LANES - dc), :] = jnp.zeros((2 * LANES - dc, CHUNK), BF16)
    acc_rel[...] = jnp.zeros_like(acc_rel)
    acc_neg[...] = jnp.zeros_like(acc_neg)
    loss[...] = jnp.zeros_like(loss)
    ident = eye(CHUNK)

    pl.semaphore_wait(barrier, chips + (2 if s else 0))

    def tail_copy(c):
        return remote(tail.at[c], tail_r.at[c], tail_ss.at[c], tail_rs.at[c], dst_t)

    def head_copy(c):
        return remote(head.at[c], head_r.at[c], head_ss.at[c], head_rs.at[c], dst_h)

    def loop(lo, hi, fn):
        def body(k, _):
            fn(k)
            return 0
        lax.fori_loop(lo, hi, body, 0)

    neg_pair = remote(neg.at[1 - core], neg_p, one_s.at[0], one_r.at[0], partner)
    neg_pair.start()
    if s:
        loop(0, nch, lambda c: tail_copy(c).start())
        loop(0, nch, lambda c: head_copy(c).start())
        tail_in, head_in, dp_in = tail_r, head_r, dp_r
    else:
        tail_in, head_in, dp_in = tail, head, dp_s

    neg_pair.wait_recv()
    neg_half[...] = neg[core] + neg_p[...]

    def rs_neg(k):
        return remote(neg_half.at[lax.rem(chip + k, chips)], neg_buf.at[k], rs_s.at[k], rs_r.at[k], peer(k))
    loop(1, chips, lambda k: rs_neg(k).start())
    neg_acc[...] = neg_half[chip]

    def take_neg(k):
        rs_neg(k).wait_recv()
        neg_acc[...] = neg_acc[...] + neg_buf[k]
    loop(1, chips, take_neg)

    def ag_neg(k):
        return remote(neg_acc, neg_all.at[core, chip], ag_s.at[k], ag_r.at[k], peer(k))
    loop(1, chips, lambda k: ag_neg(k).start())
    neg_all[core, chip] = neg_acc[...]
    loop(1, chips, lambda k: ag_neg(k).wait_recv())
    neg_pair2 = remote(neg_all.at[core], neg_all.at[core], one_s.at[1], one_r.at[1], partner)
    neg_pair2.start()
    neg_pair2.wait_recv()
    neg_rows = neg_all[...].reshape(dims.negp, 2 * LANES)
    neg_t[...] = nt_dot(eye(2 * LANES), neg_rows).astype(BF16)

    def one_hot(ids_ref, c):
        ids = ids_ref[pl.ds(s * nch + c, 1), :]
        return jnp.where(iota((dims.relp, CHUNK), 0) == ids, 1.0, 0.0).astype(BF16)

    def rel_rows(hot):
        r = nn_dot(splits[...], hot)
        r = (r[:dc] + r[dc:2 * dc]) + r[2 * dc:]
        return r[:hp], r[hp:]

    def queries(rows, r_re, r_im):
        x = rows.astype(F32)
        h_re, h_im = x[:hp], x[hp:]
        return h_re, h_im, h_re * r_re - h_im * r_im, h_re * r_im + h_im * r_re

    def head_side(c):
        hot = one_hot(rel_ids, c)
        r_re, r_im = rel_rows(hot)
        h_re, h_im, q_re, q_im = queries(head[c], r_re, r_im)
        qb[pl.ds(0, dc), :] = jnp.concatenate([q_re, q_im], axis=0).astype(BF16)
        scores = nn_dot(neg_all[...].reshape(dims.negp, 2 * LANES), qb[...])
        scores = jnp.where(iota((dims.negp, CHUNK), 0) < dims.neg, scores, -1e30)
        if s:
            tail_copy(c).wait_recv()
        t = tail_in[c].astype(F32)
        t_re, t_im = t[:hp], t[hp:]
        pos = jnp.sum(q_re * t_re + q_im * t_im, axis=0, keepdims=True)
        top = jnp.maximum(pos, jnp.max(scores, axis=0, keepdims=True))
        pos_exp = jnp.exp(pos - top)
        neg_exp = jnp.exp(scores - top)
        norm = pos_exp + jnp.sum(neg_exp, axis=0, keepdims=True)
        w = weight[pl.ds(s * nch + c, 1), :]
        loss[pl.ds(0, 1), :] += w * (top + jnp.log(norm) - pos)
        dp = w * (pos_exp / norm - 1.0)
        dp_s[pl.ds(c, 1), :] = dp
        dsb[...] = (neg_exp * (w / norm)).astype(BF16)
        mix = nn_dot(neg_t[pl.ds(0, dc), :], dsb[...])
        g_re = dp * t_re + mix[:hp]
        g_im = dp * t_im + mix[hp:]
        acc_neg[...] += nt_dot(qb[pl.ds(0, dc), :], dsb[...])
        head_c[c] = jnp.concatenate([g_re * r_re + g_im * r_im, g_im * r_re - g_re * r_im], axis=0)
        rel_g = jnp.concatenate([g_re * h_re + g_im * h_im, g_im * h_re - g_re * h_im], axis=0)
        acc_rel[...] += nt_dot(jnp.concatenate(split3(rel_g), axis=1), jnp.concatenate([hot] * 3, axis=1))
    loop(0, nch, head_side)

    if s:
        dp_copy = remote(dp_s, dp_r, one_s.at[2], one_r.at[2], dst_h)
        dp_copy.start()

    def tile_place(t):
        d, j = t // dims.tpd, t % dims.tpd
        return d // chips, d % chips, j
    rel_cols = dims.relp // LANES
    for t in range(dims.tpd * ent):
        i, j = t // dims.cols, t % dims.cols
        if t >= dims.tiles:
            x_ar[tile_place(t)] = jnp.zeros((8, LANES), F32)
        elif j < rel_cols:
            x_ar[tile_place(t)] = acc_rel[pl.ds(8 * i, 8), pl.ds(j * LANES, LANES)]
        else:
            x_ar[tile_place(t)] = acc_neg[pl.ds(8 * i, 8), pl.ds((j - rel_cols) * LANES, LANES)]

    ar_pair = remote(x_ar.at[1 - core], p_ar, one_s.at[3], one_r.at[3], partner)
    ar_pair.start()

    def rows_of(cols):
        gap = jnp.zeros((LANES - hp, CHUNK), F32)
        x = jnp.concatenate([cols[:hp], gap, cols[hp:], gap], axis=0)
        return nt_dot(jnp.concatenate([ident] * 3, axis=1), jnp.concatenate(split3(x), axis=1))

    def put_rows(out, c, rows):
        base = pl.multiple_of(c * 2 * CHUNK, 2 * CHUNK)
        out[pl.ds(base, CHUNK, stride=2), :] = rows[:, :LANES]
        out[pl.ds(base + 1, CHUNK, stride=2), :] = rows[:, LANES:]

    def head_rows(c):
        put_rows(head_g, c, rows_of(head_c[c]))

    def tail_side(c):
        if s:
            head_copy(c).wait_recv()
        r_re, r_im = rel_rows(one_hot(rel_ids_p, c))
        _, _, q_re, q_im = queries(head_in[c], r_re, r_im)
        put_rows(tail_g, c, rows_of(dp_in[pl.ds(c, 1), :] * jnp.concatenate([q_re, q_im], axis=0)))

    ar_pair.wait_recv()
    half_ar[...] = x_ar[core] + p_ar[...]

    def rs_ar(k):
        return remote(half_ar.at[lax.rem(chip + k, chips)], buf_ar.at[k], rs2_s.at[k], rs2_r.at[k], peer(k))
    loop(1, chips, lambda k: rs_ar(k).start())
    loop(0, nch, head_rows)
    acc_ar[...] = half_ar[chip]

    def take_ar(k):
        rs_ar(k).wait_recv()
        acc_ar[...] += buf_ar[k]
    loop(1, chips, take_ar)

    def ag_ar(k):
        return remote(acc_ar, o_ar.at[core, chip], ag2_s.at[k], ag2_r.at[k], peer(k))
    loop(1, chips, lambda k: ag_ar(k).start())
    o_ar[core, chip] = acc_ar[...]
    if s:
        dp_copy.wait_recv()
    loop(0, nch, tail_side)
    loop(1, chips, lambda k: ag_ar(k).wait_recv())
    ar_pair2 = remote(o_ar.at[core], o_ar.at[core], one_s.at[4], one_r.at[4], partner)
    ar_pair2.start()
    ar_pair2.wait_recv()

    for t in range(dims.tiles):
        i, j = t // dims.cols, t % dims.cols
        if j < rel_cols:
            acc_rel[pl.ds(8 * i, 8), pl.ds(j * LANES, LANES)] = o_ar[tile_place(t)]
        else:
            acc_neg[pl.ds(8 * i, 8), pl.ds((j - rel_cols) * LANES, LANES)] = o_ar[tile_place(t)]
    g = acc_rel[...]
    state = rel_state[...] + jnp.sum(g * g, axis=0, keepdims=True) * (1.0 / dims.dim)
    rel_state_out[...] = state
    rel_t_out[...] = rel_t[...] - LEARN_RATE * g / jnp.sqrt(state[:1] + ADA_EPS)
    for c in range(dims.negp // CHUNK):
        put_rows(neg_g, c, rows_of(acc_neg[:, pl.ds(c * CHUNK, CHUNK)]))

    neg_pair.wait_send()
    neg_pair2.wait_send()
    ar_pair.wait_send()
    ar_pair2.wait_send()
    if s:
        dp_copy.wait_send()

        def sent(c):
            tail_copy(c).wait_send()
            head_copy(c).wait_send()
        loop(0, nch, sent)

    def sent_peers(k):
        rs_neg(k).wait_send()
        ag_neg(k).wait_send()
        rs_ar(k).wait_send()
        ag_ar(k).wait_send()
    loop(1, chips, sent_peers)


def bucket_step(dims, s, head, tail, neg, rel_t, rel_state, rel_ids, rel_ids_p, weight):
    d = dims
    vm = pl.BlockSpec(memory_space=VMEM)
    sds = jax.ShapeDtypeStruct
    dma = pltpu.SemaphoreType.DMA
    outs = [sds((2 * d.edges, LANES), F32), sds((2 * d.edges, LANES), F32), sds((2 * d.negp, LANES), F32),
            sds((d.dc, d.relp), F32), sds((8, d.relp), F32), sds((8, CHUNK), F32)]
    rows = VMEM((d.nch, d.dc, CHUNK), BF16)
    neg_part = VMEM((d.chips, d.negc, 2 * LANES), BF16)
    ar_part = VMEM((d.chips, d.tpd, 8, LANES), F32)
    scratch = [rows, rows, VMEM((d.nch, CHUNK), F32), VMEM((d.nch, CHUNK), F32),
               VMEM((3 * d.dc, d.relp), BF16), VMEM((2 * LANES, CHUNK), BF16), VMEM((d.negp, CHUNK), BF16),
               neg_part, neg_part, neg_part, VMEM((d.negc, 2 * LANES), BF16),
               VMEM((2, d.chips, d.negc, 2 * LANES), BF16), VMEM((2 * LANES, d.negp), BF16),
               VMEM((d.dc, d.relp), F32), VMEM((d.dc, d.negp), F32), VMEM((d.nch, d.dc, CHUNK), F32),
               VMEM((2, d.chips, d.tpd, 8, LANES), F32), ar_part, ar_part, ar_part,
               VMEM((d.tpd, 8, LANES), F32), VMEM((2, d.chips, d.tpd, 8, LANES), F32),
               dma((d.nch,)), dma((d.nch,)), dma((d.nch,)), dma((d.nch,)), dma((5,)), dma((5,))]
    scratch += [dma((d.chips,))] * 8
    return pl.pallas_call(
        functools.partial(bucket_kernel, d, s), out_shape=outs, in_specs=[vm] * 8, out_specs=[vm] * 6,
        scratch_shapes=scratch, name=f'bucket_{s}',
        compiler_params=pltpu.CompilerParams(collective_id=1 + s, has_side_effects=True, vmem_limit_bytes=30 << 20),
    )(head, tail, neg.reshape(2, d.chips, d.negc, 2 * LANES), rel_t, rel_state, rel_ids, rel_ids_p, weight)


def solution(mesh):
    row_spec = P(('sweep', 'ent'), None)
    flat_spec = P(('sweep', 'ent'))
    rel_spec = P('sweep', None)
    state_spec = P('sweep')
    edge_spec = P(('sweep', 'ent'), None, None)

    def device_fn(ent_emb, ent_ada, rel_emb, rel_ada, head_idx, tail_idx, rel_idx, edge_mask, neg_idx):
        d = Dims(mesh, ent_emb, rel_emb, head_idx, neg_idx)
        me = lax.axis_index('ent')
        table = pack(d, ent_emb, ent_ada)
        rel = jnp.pad(rel_emb.reshape(d.num_rel, 2, d.half), ((0, d.relp - d.num_rel), (0, 0), (0, d.hp - d.half)))
        rel_t = rel.reshape(d.relp, d.dc).T
        rel_state = jnp.broadcast_to(jnp.pad(rel_ada, (0, d.relp - d.num_rel), constant_values=1.0), (8, d.relp))

        both = jnp.stack([tail_idx[0], rel_idx[0]], axis=1).reshape(d.rounds, 2 * d.edges // LANES, LANES)
        both = exchange_indices(d, both).reshape(d.rounds, 2, d.edges)
        head_ids = (head_idx[0] * 2).reshape(-1)
        tail_ids = (both[:, 0] * 2).reshape(-1)
        local = neg_idx - me * d.rows
        owned = (local >= 0) & (local < d.rows)
        neg_ids = jnp.where(owned, local, d.rows) * 2
        neg_ids = jnp.pad(neg_ids, ((0, 0), (0, d.negp - d.neg)), constant_values=2 * d.rows).reshape(-1)
        ids = (head_ids, tail_ids, neg_ids)
        rel_ids = rel_idx[0].reshape(d.rounds * d.nch, CHUNK)
        rel_ids_p = both[:, 1].reshape(d.rounds * d.nch, CHUNK)
        weight = edge_mask[0].astype(F32).reshape(d.rounds * d.nch, CHUNK)

        head, tail, neg = table_step(d, None, 0, ids, None, table)
        losses = []
        for s in range(d.rounds):
            hg, tg, ng, rel_t, rel_state, loss = bucket_step(d, s, head, tail, neg, rel_t, rel_state, rel_ids, rel_ids_p, weight)
            losses.append(loss[0])
            last = s == d.rounds - 1
            res = table_step(d, s, None if last else s + 1, ids, (hg, tg, ng), table)
            table = res[0]
            if not last:
                head, tail, neg = res[1:]
        loss = jnp.sum(jnp.stack(losses), axis=1) / d.edges
        emb, ada = unpack(d, table)
        rel_out = rel_t.T.reshape(d.relp, 2, d.hp)[:d.num_rel, :, :d.half].reshape(d.num_rel, d.dim)
        return emb, ada, rel_out, rel_state[0, :d.num_rel], loss[None, :]

    return jax.shard_map(device_fn, mesh=mesh,
                         in_specs=(row_spec, flat_spec, rel_spec, state_spec, edge_spec, edge_spec, edge_spec, edge_spec, rel_spec),
                         out_specs=(row_spec, flat_spec, rel_spec, state_spec, row_spec), check_vma=False)
```

time: 5580 us -> 1780 us (0.32)
  waiting for transfers between devices: 3110 us -> 0 us
  Pallas kernels: 0 us -> 1730 us
  other arithmetic: 1220 us -> 3.7 us
  local copies, waits for them, and re-layouts: 991 us -> 30.3 us
  starting transfers between devices: 114 us -> 0 us
  matrix products: 112 us -> 0 us
    psum x32 -> x0, waiting for transfers between devices: 3090 us -> none  [the longest x16 1620 us: device_fn(): neg_rows = lax.psum(neg_mine, 'ent')]
    pallas_call x0 -> x36, Pallas kernels: none -> 1730 us  [the longest x16 1130 us: bucket_step(): pl.pallas_call(functools.partial(bucket_kernel, d, s), out_shape=outs, in...]
    scatter-add x32 -> x0, other arithmetic: 634 us -> none  [the longest x16 432 us: device_fn(): grad_ent = jax.ops.segment_sum(row_grads, row_ids, num_segments=part_rows)]
    gather x128 -> x0, local copies, waits for them, and re-layouts: 588 us -> none  [the longest x32 202 us: device_fn(): jnp.take(tail_tab, tail_ids, axis=0)]
    convert_element_type x49 -> x1, other arithmetic: 140 us -> 0.92 us  [device_fn(): weight = edge_mask[0].astype(F32).reshape(d.rounds * d.nch, CHUNK)]
    reduce_sum x80 -> x1, other arithmetic: 139 us -> 0.12 us  [device_fn(): loss = jnp.sum(jnp.stack(losses), axis=1) / d.edges]
    concatenate x32 -> x0, local copies, waits for them, and re-layouts: 134 us -> none  [the longest x16 89 us: device_fn(): jnp.concatenate([head_grad, back_grad, jnp.where(owned[:, None], neg_sum,...]
    dot_general x48 -> x0, matrix products: 112 us -> none  [the longest x16 60.1 us: bucket_grads(): jnp.einsum('bd,nd->bn', query_bf, neg_rows, preferred_element_type=jnp.fl...]
  transfers between devices with their start and end apart: 77 -> 0, of which waited for: 32 -> 0; matrix products, arithmetic and copies ran while one was open for 38% -> 0% of each run, Pallas kernels for 0% -> 0%
where the time goes in v1:
time: 1780 us; the launch traced here: 1760 us
  Pallas kernels  1730 us (97%)
  local copies, waits for them, and re-layouts  30.3 us (2%)
    pallas_call x16, Pallas kernels, bucket_step(): pl.pallas_call(functools.partial(bucket_kernel, d, s), out_shape=outs, in...  1130 us
    pallas_call x17, Pallas kernels, table_step(): pl.pallas_call(body, out_shape=outs, in_specs=in_specs, out_specs=[vm] *...  558 us

profile of v1, /device:TPU:97, one launch (start us, length us, event | category | flops | bytes accessed | tf_op | source)
XLA Modules:
  0.0 1764.3 jit_solution(8423314416612687421)
XLA Ops:
  0.6 0.0 copy-start.3
  0.6 0.0 copy-start.4
  0.7 0.7 pad.14
  1.4 0.8 select_multiply_fusion
  2.2 0.9 reshape_squeeze.6.rel_ids
  3.1 0.9 multiply_bitcast_fusion
  4.1 0.9 convert_element_type.9
  5.0 1.0 reshape.110
  6.0 0.0 copy-done.3
  6.0 0.0 copy-done.4
  6.1 0.2 copy.34
  6.3 0.9 reshape.105.x_ref
  7.2 17.0 index_exchange.1
  24.2 1.1 reshape.106
  25.3 0.4 slice_reduce_fusion
  25.8 8.6 copy.35.e_ref
  34.3 10.8 pack.1.refs_3_.refs_6_
  45.1 0.0 copy-start
  45.1 3.4 copy-done
  48.5 0.0 copy-start.1
  48.5 8.7 table_xg.1
  57.2 42.7 %bucket_0.1 = (f32[4096,128]{1,0:T(8,128)S(1)}, f32[4096,128]{1,0:T(8,128)S(1)}, f32[1024,128]{1,0:T(8,128)S(1)}, f32[208,256]{1,0:T(8,128)S(1)}, f32[8,256]{1,0:T(8,128)S(1)}, /*index=5*/f32[8,256]{1,0:T(8,128)S(1)}) custom-call(bf16[8,208,256]{2,1,0:T(8,128)(2,1)S(1)} %get-tuple-element.166.head, bf16[8,208,256]{2,1,0:T(8,128)(2,1)S(1)} %get-tuple-element.167.tail, ...), custom_call_target="tpu_custom_call" | custom-call | tf_op jit(solution)/shard_map/bucket_0/pallas_call | solution.py:575
  99.9 0.0 copy-done.1
  99.9 34.9 %table_ug.15 = (f32[16400,128]{1,0:T(8,128)S(1)}, bf16[8,208,256]{2,1,0:T(8,128)(2,1)S(1)}, bf16[8,208,256]{2,1,0:T(8,128)(2,1)S(1)}, bf16[512,256]{1,0:T(8,128)(2,1)S(1)}) custom-call(s32[32768]{0:T(1024)S(1)} %bitcast.42, s32[32768]{0:T(1024)S(1)} %bitcast.59, s32[8192]{0:T(1024)S(1)} %bitcast.76, ...), custom_call_target="tpu_custom_call", output_to_operand_aliasing={{0}: (6, {})} | custom-call | tf_op jit(solution)/shard_map/table_ug/pallas_call | solution.py:318
  134.8 51.6 %bucket_1.1 = (f32[4096,128]{1,0:T(8,128)S(1)}, f32[4096,128]{1,0:T(8,128)S(1)}, f32[1024,128]{1,0:T(8,128)S(1)}, f32[208,256]{1,0:T(8,128)S(1)}, f32[8,256]{1,0:T(8,128)S(1)}, /*index=5*/f32[8,256]{1,0:T(8,128)S(1)}) custom-call(bf16[8,208,256]{2,1,0:T(8,128)(2,1)S(1)} %get-tuple-element.172.head, bf16[8,208,256]{2,1,0:T(8,128)(2,1)S(1)} %get-tuple-element.173.tail, ...), custom_call_target="tpu_custom_call" | custom-call | tf_op jit(solution)/shard_map/bucket_1/pallas_call | solution.py:575
  186.3 34.8 %table_ug.16 = (f32[16400,128]{1,0:T(8,128)S(1)}, bf16[8,208,256]{2,1,0:T(8,128)(2,1)S(1)}, bf16[8,208,256]{2,1,0:T(8,128)(2,1)S(1)}, bf16[512,256]{1,0:T(8,128)(2,1)S(1)}) custom-call(s32[32768]{0:T(1024)S(1)} %bitcast.43, s32[32768]{0:T(1024)S(1)} %bitcast.60, s32[8192]{0:T(1024)S(1)} %bitcast.77, ...), custom_call_target="tpu_custom_call", output_to_operand_aliasing={{0}: (6, {})} | custom-call | tf_op jit(solution)/shard_map/table_ug/pallas_call | solution.py:318
  221.2 60.0 %bucket_2.1 = (f32[4096,128]{1,0:T(8,128)S(1)}, f32[4096,128]{1,0:T(8,128)S(1)}, f32[1024,128]{1,0:T(8,128)S(1)}, f32[208,256]{1,0:T(8,128)S(1)}, f32[8,256]{1,0:T(8,128)S(1)}, /*index=5*/f32[8,256]{1,0:T(8,128)S(1)}) custom-call(bf16[8,208,256]{2,1,0:T(8,128)(2,1)S(1)} %get-tuple-element.181.head, bf16[8,208,256]{2,1,0:T(8,128)(2,1)S(1)} %get-tuple-element.182.tail, ...), custom_call_target="tpu_custom_call" | custom-call | tf_op jit(solution)/shard_map/bucket_2/pallas_call | solution.py:575
  281.2 34.8 %table_ug.17 = (f32[16400,128]{1,0:T(8,128)S(1)}, bf16[8,208,256]{2,1,0:T(8,128)(2,1)S(1)}, bf16[8,208,256]{2,1,0:T(8,128)(2,1)S(1)}, bf16[512,256]{1,0:T(8,128)(2,1)S(1)}) custom-call(s32[32768]{0:T(1024)S(1)} %bitcast.44, s32[32768]{0:T(1024)S(1)} %bitcast.61, s32[8192]{0:T(1024)S(1)} %bitcast.78, ...), custom_call_target="tpu_custom_call", output_to_operand_aliasing={{0}: (6, {})} | custom-call | tf_op jit(solution)/shard_map/table_ug/pallas_call | solution.py:318
  316.1 70.2 %bucket_3.1 = (f32[4096,128]{1,0:T(8,128)S(1)}, f32[4096,128]{1,0:T(8,128)S(1)}, f32[1024,128]{1,0:T(8,128)S(1)}, f32[208,256]{1,0:T(8,128)S(1)}, f32[8,256]{1,0:T(8,128)S(1)}, /*index=5*/f32[8,256]{1,0:T(8,128)S(1)}) custom-call(bf16[8,208,256]{2,1,0:T(8,128)(2,1)S(1)} %get-tuple-element.190.head, bf16[8,208,256]{2,1,0:T(8,128)(2,1)S(1)} %get-tuple-element.191.tail, ...), custom_call_target="tpu_custom_call" | custom-call | tf_op jit(solution)/shard_map/bucket_3/pallas_call | solution.py:575
  386.3 34.8 %table_ug.18 = (f32[16400,128]{1,0:T(8,128)S(1)}, bf16[8,208,256]{2,1,0:T(8,128)(2,1)S(1)}, bf16[8,208,256]{2,1,0:T(8,128)(2,1)S(1)}, bf16[512,256]{1,0:T(8,128)(2,1)S(1)}) custom-call(s32[32768]{0:T(1024)S(1)} %bitcast.45, s32[32768]{0:T(1024)S(1)} %bitcast.62, s32[8192]{0:T(1024)S(1)} %bitcast.79, ...), custom_call_target="tpu_custom_call", output_to_operand_aliasing={{0}: (6, {})} | custom-call | tf_op jit(solution)/shard_map/table_ug/pallas_call | solution.py:318
  421.2 79.1 %bucket_4.1 = (f32[4096,128]{1,0:T(8,128)S(1)}, f32[4096,128]{1,0:T(8,128)S(1)}, f32[1024,128]{1,0:T(8,128)S(1)}, f32[208,256]{1,0:T(8,128)S(1)}, f32[8,256]{1,0:T(8,128)S(1)}, /*index=5*/f32[8,256]{1,0:T(8,128)S(1)}) custom-call(bf16[8,208,256]{2,1,0:T(8,128)(2,1)S(1)} %get-tuple-element.199.head, bf16[8,208,256]{2,1,0:T(8,128)(2,1)S(1)} %get-tuple-element.200.tail, ...), custom_call_target="tpu_custom_call" | custom-call | tf_op jit(solution)/shard_map/bucket_4/pallas_call | solution.py:575
  500.3 34.8 %table_ug.19 = (f32[16400,128]{1,0:T(8,128)S(1)}, bf16[8,208,256]{2,1,0:T(8,128)(2,1)S(1)}, bf16[8,208,256]{2,1,0:T(8,128)(2,1)S(1)}, bf16[512,256]{1,0:T(8,128)(2,1)S(1)}) custom-call(s32[32768]{0:T(1024)S(1)} %bitcast.46, s32[32768]{0:T(1024)S(1)} %bitcast.63, s32[8192]{0:T(1024)S(1)} %bitcast.80, ...), custom_call_target="tpu_custom_call", output_to_operand_aliasing={{0}: (6, {})} | custom-call | tf_op jit(solution)/shard_map/table_ug/pallas_call | solution.py:318
  535.1 78.6 %bucket_5.1 = (f32[4096,128]{1,0:T(8,128)S(1)}, f32[4096,128]{1,0:T(8,128)S(1)}, f32[1024,128]{1,0:T(8,128)S(1)}, f32[208,256]{1,0:T(8,128)S(1)}, f32[8,256]{1,0:T(8,128)S(1)}, /*index=5*/f32[8,256]{1,0:T(8,128)S(1)}) custom-call(bf16[8,208,256]{2,1,0:T(8,128)(2,1)S(1)} %get-tuple-element.208.head, bf16[8,208,256]{2,1,0:T(8,128)(2,1)S(1)} %get-tuple-element.209.tail, ...), custom_call_target="tpu_custom_call" | custom-call | tf_op jit(solution)/shard_map/bucket_5/pallas_call | solution.py:575
  613.7 34.9 %table_ug.20 = (f32[16400,128]{1,0:T(8,128)S(1)}, bf16[8,208,256]{2,1,0:T(8,128)(2,1)S(1)}, bf16[8,208,256]{2,1,0:T(8,128)(2,1)S(1)}, bf16[512,256]{1,0:T(8,128)(2,1)S(1)}) custom-call(s32[32768]{0:T(1024)S(1)} %bitcast.47, s32[32768]{0:T(1024)S(1)} %bitcast.64, s32[8192]{0:T(1024)S(1)} %bitcast.81, ...), custom_call_target="tpu_custom_call", output_to_operand_aliasing={{0}: (6, {})} | custom-call | tf_op jit(solution)/shard_map/table_ug/pallas_call | solution.py:318
  648.6 60.6 %bucket_6.1 = (f32[4096,128]{1,0:T(8,128)S(1)}, f32[4096,128]{1,0:T(8,128)S(1)}, f32[1024,128]{1,0:T(8,128)S(1)}, f32[208,256]{1,0:T(8,128)S(1)}, f32[8,256]{1,0:T(8,128)S(1)}, /*index=5*/f32[8,256]{1,0:T(8,128)S(1)}) custom-call(bf16[8,208,256]{2,1,0:T(8,128)(2,1)S(1)} %get-tuple-element.217.head, bf16[8,208,256]{2,1,0:T(8,128)(2,1)S(1)} %get-tuple-element.218.tail, ...), custom_call_target="tpu_custom_call" | custom-call | tf_op jit(solution)/shard_map/bucket_6/pallas_call | solution.py:575
  709.2 34.9 %table_ug.21 = (f32[16400,128]{1,0:T(8,128)S(1)}, bf16[8,208,256]{2,1,0:T(8,128)(2,1)S(1)}, bf16[8,208,256]{2,1,0:T(8,128)(2,1)S(1)}, bf16[512,256]{1,0:T(8,128)(2,1)S(1)}) custom-call(s32[32768]{0:T(1024)S(1)} %bitcast.48, s32[32768]{0:T(1024)S(1)} %bitcast.65, s32[8192]{0:T(1024)S(1)} %bitcast.82, ...), custom_call_target="tpu_custom_call", output_to_operand_aliasing={{0}: (6, {})} | custom-call | tf_op jit(solution)/shard_map/table_ug/pallas_call | solution.py:318
  744.1 60.0 %bucket_7.1 = (f32[4096,128]{1,0:T(8,128)S(1)}, f32[4096,128]{1,0:T(8,128)S(1)}, f32[1024,128]{1,0:T(8,128)S(1)}, f32[208,256]{1,0:T(8,128)S(1)}, f32[8,256]{1,0:T(8,128)S(1)}, /*index=5*/f32[8,256]{1,0:T(8,128)S(1)}) custom-call(bf16[8,208,256]{2,1,0:T(8,128)(2,1)S(1)} %get-tuple-element.226.head, bf16[8,208,256]{2,1,0:T(8,128)(2,1)S(1)} %get-tuple-element.227.tail, ...), custom_call_target="tpu_custom_call" | custom-call | tf_op jit(solution)/shard_map/bucket_7/pallas_call | solution.py:575
  804.1 34.8 %table_ug.22 = (f32[16400,128]{1,0:T(8,128)S(1)}, bf16[8,208,256]{2,1,0:T(8,128)(2,1)S(1)}, bf16[8,208,256]{2,1,0:T(8,128)(2,1)S(1)}, bf16[512,256]{1,0:T(8,128)(2,1)S(1)}) custom-call(s32[32768]{0:T(1024)S(1)} %bitcast.49, s32[32768]{0:T(1024)S(1)} %bitcast.66, s32[8192]{0:T(1024)S(1)} %bitcast.83, ...), custom_call_target="tpu_custom_call", output_to_operand_aliasing={{0}: (6, {})} | custom-call | tf_op jit(solution)/shard_map/table_ug/pallas_call | solution.py:318
  838.9 59.0 %bucket_8.1 = (f32[4096,128]{1,0:T(8,128)S(1)}, f32[4096,128]{1,0:T(8,128)S(1)}, f32[1024,128]{1,0:T(8,128)S(1)}, f32[208,256]{1,0:T(8,128)S(1)}, f32[8,256]{1,0:T(8,128)S(1)}, /*index=5*/f32[8,256]{1,0:T(8,128)S(1)}) custom-call(bf16[8,208,256]{2,1,0:T(8,128)(2,1)S(1)} %get-tuple-element.235.head, bf16[8,208,256]{2,1,0:T(8,128)(2,1)S(1)} %get-tuple-element.236.tail, ...), custom_call_target="tpu_custom_call" | custom-call | tf_op jit(solution)/shard_map/bucket_8/pallas_call | solution.py:575
  898.0 34.9 %table_ug.23 = (f32[16400,128]{1,0:T(8,128)S(1)}, bf16[8,208,256]{2,1,0:T(8,128)(2,1)S(1)}, bf16[8,208,256]{2,1,0:T(8,128)(2,1)S(1)}, bf16[512,256]{1,0:T(8,128)(2,1)S(1)}) custom-call(s32[32768]{0:T(1024)S(1)} %bitcast.50, s32[32768]{0:T(1024)S(1)} %bitcast.67, s32[8192]{0:T(1024)S(1)} %bitcast.84, ...), custom_call_target="tpu_custom_call", output_to_operand_aliasing={{0}: (6, {})} | custom-call | tf_op jit(solution)/shard_map/table_ug/pallas_call | solution.py:318
  932.8 68.0 %bucket_9.1 = (f32[4096,128]{1,0:T(8,128)S(1)}, f32[4096,128]{1,0:T(8,128)S(1)}, f32[1024,128]{1,0:T(8,128)S(1)}, f32[208,256]{1,0:T(8,128)S(1)}, f32[8,256]{1,0:T(8,128)S(1)}, /*index=5*/f32[8,256]{1,0:T(8,128)S(1)}) custom-call(bf16[8,208,256]{2,1,0:T(8,128)(2,1)S(1)} %get-tuple-element.244.head, bf16[8,208,256]{2,1,0:T(8,128)(2,1)S(1)} %get-tuple-element.245.tail, ...), custom_call_target="tpu_custom_call" | custom-call | tf_op jit(solution)/shard_map/bucket_9/pallas_call | solution.py:575
  1000.8 34.8 %table_ug.24 = (f32[16400,128]{1,0:T(8,128)S(1)}, bf16[8,208,256]{2,1,0:T(8,128)(2,1)S(1)}, bf16[8,208,256]{2,1,0:T(8,128)(2,1)S(1)}, bf16[512,256]{1,0:T(8,128)(2,1)S(1)}) custom-call(s32[32768]{0:T(1024)S(1)} %bitcast.51, s32[32768]{0:T(1024)S(1)} %bitcast.68, s32[8192]{0:T(1024)S(1)} %bitcast.85, ...), custom_call_target="tpu_custom_call", output_to_operand_aliasing={{0}: (6, {})} | custom-call | tf_op jit(solution)/shard_map/table_ug/pallas_call | solution.py:318
  1035.7 78.4 %bucket_10.1 = (f32[4096,128]{1,0:T(8,128)S(1)}, f32[4096,128]{1,0:T(8,128)S(1)}, f32[1024,128]{1,0:T(8,128)S(1)}, f32[208,256]{1,0:T(8,128)S(1)}, f32[8,256]{1,0:T(8,128)S(1)}, /*index=5*/f32[8,256]{1,0:T(8,128)S(1)}) custom-call(bf16[8,208,256]{2,1,0:T(8,128)(2,1)S(1)} %get-tuple-element.253.head, bf16[8,208,256]{2,1,0:T(8,128)(2,1)S(1)} %get-tuple-element.254.tail, ...), custom_call_target="tpu_custom_call" | custom-call | tf_op jit(solution)/shard_map/bucket_10/pallas_call | solution.py:575
  1114.1 34.8 %table_ug.25 = (f32[16400,128]{1,0:T(8,128)S(1)}, bf16[8,208,256]{2,1,0:T(8,128)(2,1)S(1)}, bf16[8,208,256]{2,1,0:T(8,128)(2,1)S(1)}, bf16[512,256]{1,0:T(8,128)(2,1)S(1)}) custom-call(s32[32768]{0:T(1024)S(1)} %bitcast.52, s32[32768]{0:T(1024)S(1)} %bitcast.69, s32[8192]{0:T(1024)S(1)} %bitcast.86, ...), custom_call_target="tpu_custom_call", output_to_operand_aliasing={{0}: (6, {})} | custom-call | tf_op jit(solution)/shard_map/table_ug/pallas_call | solution.py:318
  1149.0 94.6 %bucket_11.1 = (f32[4096,128]{1,0:T(8,128)S(1)}, f32[4096,128]{1,0:T(8,128)S(1)}, f32[1024,128]{1,0:T(8,128)S(1)}, f32[208,256]{1,0:T(8,128)S(1)}, f32[8,256]{1,0:T(8,128)S(1)}, /*index=5*/f32[8,256]{1,0:T(8,128)S(1)}) custom-call(bf16[8,208,256]{2,1,0:T(8,128)(2,1)S(1)} %get-tuple-element.262.head, bf16[8,208,256]{2,1,0:T(8,128)(2,1)S(1)} %get-tuple-element.263.tail, ...), custom_call_target="tpu_custom_call" | custom-call | tf_op jit(solution)/shard_map/bucket_11/pallas_call | solution.py:575
  1243.6 34.8 %table_ug.26 = (f32[16400,128]{1,0:T(8,128)S(1)}, bf16[8,208,256]{2,1,0:T(8,128)(2,1)S(1)}, bf16[8,208,256]{2,1,0:T(8,128)(2,1)S(1)}, bf16[512,256]{1,0:T(8,128)(2,1)S(1)}) custom-call(s32[32768]{0:T(1024)S(1)} %bitcast.53, s32[32768]{0:T(1024)S(1)} %bitcast.70, s32[8192]{0:T(1024)S(1)} %bitcast.87, ...), custom_call_target="tpu_custom_call", output_to_operand_aliasing={{0}: (6, {})} | custom-call | tf_op jit(solution)/shard_map/table_ug/pallas_call | solution.py:318
  1278.4 78.9 %bucket_12.1 = (f32[4096,128]{1,0:T(8,128)S(1)}, f32[4096,128]{1,0:T(8,128)S(1)}, f32[1024,128]{1,0:T(8,128)S(1)}, f32[208,256]{1,0:T(8,128)S(1)}, f32[8,256]{1,0:T(8,128)S(1)}, /*index=5*/f32[8,256]{1,0:T(8,128)S(1)}) custom-call(bf16[8,208,256]{2,1,0:T(8,128)(2,1)S(1)} %get-tuple-element.271.head, bf16[8,208,256]{2,1,0:T(8,128)(2,1)S(1)} %get-tuple-element.272.tail, ...), custom_call_target="tpu_custom_call" | custom-call | tf_op jit(solution)/shard_map/bucket_12/pallas_call | solution.py:575
  1357.3 34.9 %table_ug.27 = (f32[16400,128]{1,0:T(8,128)S(1)}, bf16[8,208,256]{2,1,0:T(8,128)(2,1)S(1)}, bf16[8,208,256]{2,1,0:T(8,128)(2,1)S(1)}, bf16[512,256]{1,0:T(8,128)(2,1)S(1)}) custom-call(s32[32768]{0:T(1024)S(1)} %bitcast.54, s32[32768]{0:T(1024)S(1)} %bitcast.71, s32[8192]{0:T(1024)S(1)} %bitcast.88, ...), custom_call_target="tpu_custom_call", output_to_operand_aliasing={{0}: (6, {})} | custom-call | tf_op jit(solution)/shard_map/table_ug/pallas_call | solution.py:318
  1392.2 95.8 %bucket_13.1 = (f32[4096,128]{1,0:T(8,128)S(1)}, f32[4096,128]{1,0:T(8,128)S(1)}, f32[1024,128]{1,0:T(8,128)S(1)}, f32[208,256]{1,0:T(8,128)S(1)}, f32[8,256]{1,0:T(8,128)S(1)}, /*index=5*/f32[8,256]{1,0:T(8,128)S(1)}) custom-call(bf16[8,208,256]{2,1,0:T(8,128)(2,1)S(1)} %get-tuple-element.280.head, bf16[8,208,256]{2,1,0:T(8,128)(2,1)S(1)} %get-tuple-element.281.tail, ...), custom_call_target="tpu_custom_call" | custom-call | tf_op jit(solution)/shard_map/bucket_13/pallas_call | solution.py:575
  1488.0 34.8 %table_ug.28 = (f32[16400,128]{1,0:T(8,128)S(1)}, bf16[8,208,256]{2,1,0:T(8,128)(2,1)S(1)}, bf16[8,208,256]{2,1,0:T(8,128)(2,1)S(1)}, bf16[512,256]{1,0:T(8,128)(2,1)S(1)}) custom-call(s32[32768]{0:T(1024)S(1)} %bitcast.55, s32[32768]{0:T(1024)S(1)} %bitcast.72, s32[8192]{0:T(1024)S(1)} %bitcast.89, ...), custom_call_target="tpu_custom_call", output_to_operand_aliasing={{0}: (6, {})} | custom-call | tf_op jit(solution)/shard_map/table_ug/pallas_call | solution.py:318
  1522.9 78.1 %bucket_14.1 = (f32[4096,128]{1,0:T(8,128)S(1)}, f32[4096,128]{1,0:T(8,128)S(1)}, f32[1024,128]{1,0:T(8,128)S(1)}, f32[208,256]{1,0:T(8,128)S(1)}, f32[8,256]{1,0:T(8,128)S(1)}, /*index=5*/f32[8,256]{1,0:T(8,128)S(1)}) custom-call(bf16[8,208,256]{2,1,0:T(8,128)(2,1)S(1)} %get-tuple-element.289.head, bf16[8,208,256]{2,1,0:T(8,128)(2,1)S(1)} %get-tuple-element.290.tail, ...), custom_call_target="tpu_custom_call" | custom-call | tf_op jit(solution)/shard_map/bucket_14/pallas_call | solution.py:575
  1601.0 34.8 %table_ug.29 = (f32[16400,128]{1,0:T(8,128)S(1)}, bf16[8,208,256]{2,1,0:T(8,128)(2,1)S(1)}, bf16[8,208,256]{2,1,0:T(8,128)(2,1)S(1)}, bf16[512,256]{1,0:T(8,128)(2,1)S(1)}) custom-call(s32[32768]{0:T(1024)S(1)} %bitcast.56, s32[32768]{0:T(1024)S(1)} %bitcast.73, s32[8192]{0:T(1024)S(1)} %bitcast.90, ...), custom_call_target="tpu_custom_call", output_to_operand_aliasing={{0}: (6, {})} | custom-call | tf_op jit(solution)/shard_map/table_ug/pallas_call | solution.py:318
  1635.9 77.6 %bucket_15.1 = (f32[4096,128]{1,0:T(8,128)S(1)}, f32[4096,128]{1,0:T(8,128)S(1)}, f32[1024,128]{1,0:T(8,128)S(1)}, f32[208,256]{1,0:T(8,128)S(1)}, f32[8,256]{1,0:T(8,128)S(1)}, /*index=5*/f32[8,256]{1,0:T(8,128)S(1)}) custom-call(bf16[8,208,256]{2,1,0:T(8,128)(2,1)S(1)} %get-tuple-element.298.head, bf16[8,208,256]{2,1,0:T(8,128)(2,1)S(1)} %get-tuple-element.299.tail, ...), custom_call_target="tpu_custom_call" | custom-call | tf_op jit(solution)/shard_map/bucket_15/pallas_call | solution.py:575
  1713.5 26.5 %table_ux.1.t_ref = f32[16400,128]{1,0:T(8,128)S(1)} custom-call(s32[32768]{0:T(1024)S(1)} %bitcast.57, s32[32768]{0:T(1024)S(1)} %bitcast.74, s32[8192]{0:T(1024)S(1)} %bitcast.91, f32[4096,128]{1,0:T(8,128)S(1)} %get-tuple-element.303.refs_3_, f32[4096,128]{1,0:T(8,128)S(1)} %get-tuple-element.304.refs_4_, ...), custom_call_target="tpu_custom_call", output_to_operand_aliasing={{}: (6, {})} | custom-call | tf_op jit(solution)/shard_map/table_ux/pallas_call | solution.py:318
  1740.0 0.0 copy-start.2
  1740.0 3.3 copy-done.2
  1743.2 0.6 slice.63
  1743.8 0.1 stack.7
  1743.9 0.1 reduce_sum.9
  1744.0 0.5 multiply_bitcast_fusion.1
  1744.5 9.9 unpack.1
  1754.4 8.8 copy.37
  1763.2 0.7 reshape.129
  (24 shorter events, 0.2 us)
Async XLA Ops:
  0.6 5.4 copy-start.3
  0.6 5.4 copy-start.4
  45.1 3.4 copy-start
  48.5 51.4 %copy-start.1 = (f32[16400,128]{1,0:T(8,128)S(1)}, f32[16400,128]{1,0:T(8,128)}, u32[]{:S(2)}) copy-start(f32[16400,128]{1,0:T(8,128)} %pack.1.refs_3_.refs_6_) | copy-start | bytes 25190404
  1740.0 3.3 copy-start.2

commit v2 on v1

v2 whole, which is shorter than its diff:
```python
import functools

import jax
import jax.numpy as jnp
from jax import lax
from jax.experimental import pallas as pl
from jax.experimental.pallas import tpu as pltpu
from jax.sharding import PartitionSpec as P

LEARN_RATE = 0.05
ADA_EPS = 1e-10
LANES = 128
CHUNK = 256
PACK_ROWS = 1024
QUERY_GROUP, SCORE_GROUP, HEAD_GROUP, ROWS_GROUP, TAIL_GROUP = 2, 2, 2, 4, 2
TAILS_FIRST = 2
AHEAD = 2
HEAD_SENDS = {0: (0, 2, 3, 4, 5, 7, 8), **{k: (4, 8, 8, 8, 8, 8, 8) for k in (1, 2, 3, 6, 7, 8)}}
F32, BF16, I32 = jnp.float32, jnp.bfloat16, jnp.int32
MESH = pl.DeviceIdType.MESH
VMEM = pltpu.VMEM


def round_up(value, multiple):
    return -(-value // multiple) * multiple


class Dims:
    def __init__(self, mesh, ent_emb, rel_emb, head_idx, neg_idx):
        self.ent = mesh.shape['ent']
        self.chips = self.ent // 2
        self.rows, self.dim = ent_emb.shape
        self.half = self.dim // 2
        self.hp = round_up(self.half, 8)
        self.dc = 2 * self.hp
        self.num_rel = rel_emb.shape[0]
        self.relp = round_up(self.num_rel, LANES)
        self.rounds, self.edges = head_idx.shape[1:]
        self.nch = self.edges // CHUNK
        self.neg = neg_idx.shape[1]
        self.negp = round_up(self.neg, self.ent * 16)
        self.negc = self.negp // self.ent
        self.cols = (self.relp + self.negp) // LANES
        self.tiles = self.dc // 8 * self.cols
        self.tpd = -(-self.tiles // self.ent)
        self.trows = 2 * self.rows + 16


def nt_dot(lhs, rhs):
    return lax.dot_general(lhs, rhs, (((1,), (1,)), ((), ())), preferred_element_type=F32)


def nn_dot(lhs, rhs):
    return jnp.dot(lhs, rhs, preferred_element_type=F32)


def split3(x):
    hi = x.astype(BF16)
    rest = x - hi.astype(F32)
    mid = rest.astype(BF16)
    lo = (rest - mid.astype(F32)).astype(BF16)
    return hi, mid, lo


def iota(shape, dim):
    return lax.broadcasted_iota(I32, shape, dim)


def eye(n):
    return jnp.where(iota((n, n), 0) == iota((n, n), 1), 1.0, 0.0).astype(BF16)


def compact_sel(dims, out_rows):
    c = iota((out_rows, 2 * LANES), 0)
    lane = iota((out_rows, 2 * LANES), 1)
    src = jnp.where(c < dims.hp, c, c - dims.hp + LANES)
    return jnp.where((lane == src) & (c < dims.dc), 1.0, 0.0).astype(BF16)


def pack_kernel(half, last, e_ref, g_ref, o_ref):
    step = pl.program_id(0)
    row = iota((LANES, LANES), 0)
    low = half // 8 * 8
    gap = jnp.zeros((LANES - round_up(half, 8), LANES), F32)

    @pl.when(step < last)
    def _():
        for i in range(PACK_ROWS // LANES):
            cols = pl.ds(i * LANES, LANES)
            re = jnp.concatenate([e_ref[pl.ds(0, round_up(half, 8)), cols], gap], axis=0)
            re = jnp.where(row < half, re, 0.0)
            im = jnp.concatenate([e_ref[pl.ds(low, 2 * half - low), cols], jnp.zeros((LANES - (2 * half - low), LANES), F32)], axis=0)
            if half > low:
                im = pltpu.roll(im, LANES - (half - low), 0)
            im = jnp.where(row < half, im, 0.0)
            im = jnp.where(row == LANES - 1, g_ref[pl.ds(i, 1), :], im)
            o_ref[pl.ds(2 * i * LANES, LANES, stride=2), :] = jnp.transpose(re)
            o_ref[pl.ds(2 * i * LANES + 1, LANES, stride=2), :] = jnp.transpose(im)

    @pl.when(step == last)
    def _():
        o_ref[...] = jnp.zeros_like(o_ref)


def pack(dims, emb, ada):
    blocks = dims.rows // PACK_ROWS
    return pl.pallas_call(
        functools.partial(pack_kernel, dims.half, blocks),
        grid=(blocks + 1,),
        out_shape=jax.ShapeDtypeStruct((dims.trows, LANES), F32),
        in_specs=[pl.BlockSpec((dims.dim, PACK_ROWS), lambda i: (0, jnp.minimum(i, blocks - 1))),
                  pl.BlockSpec((PACK_ROWS // LANES, LANES), lambda i: (jnp.minimum(i, blocks - 1), 0))],
        out_specs=pl.BlockSpec((2 * PACK_ROWS, LANES), lambda i: (i, 0)),
        compiler_params=pltpu.CompilerParams(vmem_limit_bytes=16 << 20),
        name='pack')(emb.T, ada.reshape(dims.rows // LANES, LANES))


def unpack_kernel(half, t_ref, e_ref, g_ref):
    low = half // 8 * 8
    high = round_up(half, 8)
    for i in range(PACK_ROWS // LANES):
        cols = pl.ds(i * LANES, LANES)
        re = jnp.transpose(t_ref[pl.ds(2 * i * LANES, LANES, stride=2), :])
        im = jnp.transpose(t_ref[pl.ds(2 * i * LANES + 1, LANES, stride=2), :])
        g_ref[pl.ds(i, 1), :] = im[LANES - 1:]
        e_ref[pl.ds(0, low), cols] = re[:low]
        if half > low:
            im = pltpu.roll(im, half - low, 0)
            e_ref[pl.ds(low, 8), cols] = jnp.where(iota((8, LANES), 0) < half - low, re[low:high], im[:8])
            e_ref[pl.ds(high, 2 * half - high), cols] = im[8:8 + 2 * half - high]
        else:
            e_ref[pl.ds(half, half), cols] = im[:half]


def unpack(dims, table):
    blocks = dims.rows // PACK_ROWS
    emb, ada = pl.pallas_call(
        functools.partial(unpack_kernel, dims.half),
        grid=(blocks,),
        out_shape=[jax.ShapeDtypeStruct((dims.dim, dims.rows), F32),
                   jax.ShapeDtypeStruct((dims.rows // LANES, LANES), F32)],
        in_specs=[pl.BlockSpec((2 * PACK_ROWS, LANES), lambda i: (i, 0))],
        out_specs=[pl.BlockSpec((dims.dim, PACK_ROWS), lambda i: (0, i)),
                   pl.BlockSpec((PACK_ROWS // LANES, LANES), lambda i: (i, 0))],
        compiler_params=pltpu.CompilerParams(vmem_limit_bytes=16 << 20),
        name='unpack')(table)
    return emb.T, ada.reshape(dims.rows)


UNROLL_SCATTER = 16
UNROLL_GATHER = 64
UNROLL_NEG = 8
GATHER_GROUP = 4
UPDATE_ROWS = 512


def table_kernel(dims, update_rows, gather_next, *refs):
    refs = list(refs)

    def take(n):
        taken = refs[:n]
        del refs[:n]
        return taken
    edges, negp = dims.edges, dims.negp
    sources, lists = [], []
    if update_rows:
        old_count, = take(1)
        sources += take(4)
    if gather_next:
        new_count, = take(1)
        sources += take(4)
    if update_rows:
        head_g, tail_g, neg_g = take(3)
    table_in, = take(1)
    table, = take(1) if update_rows else (table_in,)
    if gather_next:
        tail_out, head_out, neg_out = take(3)
    lists = take(len(sources))
    sem, = take(1)
    if update_rows:
        acc_a, acc_b = take(2)
    if gather_next:
        stage, = take(1)
    copies = [pltpu.make_async_copy(src, dst, sem.at[k]) for k, (src, dst) in enumerate(zip(sources, lists))]
    for copy in copies:
        copy.start()
    if update_rows:
        head_i, tail_i, neg_i, src_i = lists[:4]
        table_update(dims, copies, old_count, head_i, tail_i, neg_i, src_i, head_g, tail_g, neg_g, table_in, table, acc_a, acc_b)
    else:
        for copy in copies:
            copy.wait()
    if gather_next:
        head_i, tail_i, neg_i, src_i = lists[-4:]
        sel = compact_sel(dims, 2 * LANES)

        def staged(c):
            base = pl.multiple_of(c * 2 * CHUNK, 2 * CHUNK)
            re = stage[pl.ds(base, CHUNK, stride=2), :]
            im = stage[pl.ds(base + 1, CHUNK, stride=2), :]
            return jnp.concatenate([re.astype(BF16), im.astype(BF16)], axis=1)

        for ids, out in ((tail_i, tail_out), (head_i, head_out)):
            def gather(c, _):
                for u in range(UNROLL_GATHER):
                    k = c * UNROLL_GATHER + u
                    stage[pair(k), :] = table[at(ids, k), :]
                return 0
            lax.fori_loop(0, edges // UNROLL_GATHER, gather, 0)

            def convert(c, _):
                for u in range(GATHER_GROUP):
                    k = c * GATHER_GROUP + u
                    out[k] = nt_dot(sel[:dims.dc], staged(k)).astype(BF16)
                return 0
            lax.fori_loop(0, dims.nch // GATHER_GROUP, convert, 0)

        stage[pl.ds(0, 2 * negp), :] = jnp.zeros((2 * negp, LANES), F32)

        def gather_neg(c, _):
            rows = [table[at(neg_i, c * UNROLL_NEG + u), :] for u in range(UNROLL_NEG)]
            for u in range(UNROLL_NEG):
                stage[at(src_i, c * UNROLL_NEG + u), :] = rows[u]
            return 0
        lax.fori_loop(0, (new_count[0] + UNROLL_NEG - 1) // UNROLL_NEG, gather_neg, 0)
        for c in range(negp // CHUNK):
            neg_out[pl.ds(c * CHUNK, CHUNK), :] = nt_dot(staged(c), sel).astype(BF16)


def table_update(dims, copies, count, head_i, tail_i, neg_i, src_i, head_g, tail_g, neg_g, table_in, table, acc_a, acc_b):
    edges = dims.edges

    def zero(c, _):
        rows = pl.ds(pl.multiple_of(c * 256, 256), 256)
        acc_a[rows, :] = jnp.zeros((256, LANES), F32)
        acc_b[rows, :] = jnp.zeros((256, LANES), F32)
        return 0
    lax.fori_loop(0, 2 * dims.rows // 256, zero, 0)
    for copy in copies:
        copy.wait()

    def scatter(c, _):
        for u in range(0, UNROLL_SCATTER, 2):
            k = c * UNROLL_SCATTER + u
            h0, h1, t0, t1 = at(head_i, k), at(head_i, k + 1), at(tail_i, k), at(tail_i, k + 1)
            a0 = acc_a[h0, :] + head_g[pair(k), :]
            b0 = acc_b[t0, :] + tail_g[pair(k), :]
            a1 = jnp.where(head_i[k] == head_i[k + 1], a0, acc_a[h1, :]) + head_g[pair(k + 1), :]
            b1 = jnp.where(tail_i[k] == tail_i[k + 1], b0, acc_b[t1, :]) + tail_g[pair(k + 1), :]
            acc_a[h0, :] = a0
            acc_b[t0, :] = b0
            acc_a[h1, :] = a1
            acc_b[t1, :] = b1
        return 0
    lax.fori_loop(0, edges // UNROLL_SCATTER, scatter, 0)

    def scatter_neg(c, _):
        for u in range(0, UNROLL_NEG, 2):
            k = c * UNROLL_NEG + u
            h, t = at(neg_i, k), at(neg_i, k + 1)
            new_a = acc_a[h, :] + neg_g[at(src_i, k), :]
            new_b = acc_b[t, :] + neg_g[at(src_i, k + 1), :]
            acc_a[h, :] = new_a
            acc_b[t, :] = new_b
        return 0
    lax.fori_loop(0, (count[0] + UNROLL_NEG - 1) // UNROLL_NEG, scatter_neg, 0)

    lane = iota((UPDATE_ROWS, LANES), 1)

    def update(c, _):
        base = pl.multiple_of(c * 2 * UPDATE_ROWS, 2 * UPDATE_ROWS)
        re = pl.ds(base, UPDATE_ROWS, stride=2)
        im = pl.ds(base + 1, UPDATE_ROWS, stride=2)
        g_re = acc_a[re, :] + acc_b[re, :]
        g_im = acc_a[im, :] + acc_b[im, :]
        e_re, e_im = table_in[re, :], table_in[im, :]
        part = (g_re * g_re + g_im * g_im) * (1.0 / dims.dim)
        part = jnp.where(lane == LANES - 1, e_im, part)
        state = jnp.sum(part, axis=1, keepdims=True)
        rate = LEARN_RATE * lax.rsqrt(state + ADA_EPS)
        table[re, :] = e_re - rate * g_re
        table[im, :] = jnp.where(lane == LANES - 1, state, e_im - rate * g_im)
        return 0
    lax.fori_loop(0, dims.rows // UPDATE_ROWS, update, 0)
    table[pl.ds(2 * dims.rows, 16), :] = jnp.zeros((16, LANES), F32)


def pair(k):
    return pl.ds(pl.multiple_of(2 * k, 2), 2)


def at(ref, k):
    return pl.ds(pl.multiple_of(ref[k], 2), 2)


def table_step(dims, old, new, grads, table):
    vm = pl.BlockSpec(memory_space=VMEM)
    smem = pl.BlockSpec(memory_space=pltpu.SMEM)
    anys = pl.BlockSpec(memory_space=pl.ANY)
    sizes = (dims.edges, dims.edges, dims.negp, dims.negp)
    operands, in_specs, outs, scratch, aliases = [], [], [], [], {}
    for lists in (old, new):
        if lists is not None:
            operands += lists
            in_specs += [smem] + [anys] * 4
            scratch += [pltpu.SMEM((n,), I32) for n in sizes]
    scratch.append(pltpu.SemaphoreType.DMA((len(scratch),)))
    if old is not None:
        operands += grads
        in_specs += [vm] * 3
        aliases = {len(operands): 0}
        outs.append(jax.ShapeDtypeStruct((dims.trows, LANES), F32))
        scratch += [VMEM((dims.trows, LANES), F32)] * 2
    operands.append(table)
    in_specs.append(vm)
    if new is not None:
        outs += [jax.ShapeDtypeStruct((dims.nch, dims.dc, CHUNK), BF16)] * 2
        outs.append(jax.ShapeDtypeStruct((dims.negp, 2 * LANES), BF16))
        scratch.append(VMEM((2 * dims.edges, LANES), F32))
    return pl.pallas_call(
        functools.partial(table_kernel, dims, old is not None, new is not None),
        out_shape=outs, in_specs=in_specs, out_specs=[vm] * len(outs), scratch_shapes=scratch,
        input_output_aliases=aliases, name='table',
        compiler_params=pltpu.CompilerParams(vmem_limit_bytes=24 << 20))(*operands)


def bucket_kernel(dims, s, *refs):
    (head, tail, neg, rel_t, rel_state, rel_ids, rel_ids_p, weight), refs = refs[:8], refs[8:]
    if s == 0:
        (tail_x, rel_x), refs = refs[:2], refs[2:]
    (head_g, tail_g, neg_g, rel_t_out, rel_state_out, loss), refs = refs[:6], refs[6:]
    if s == 0:
        rel_x_out, tail_x_out = refs[0], refs[1:dims.rounds]
        refs = refs[dims.rounds:]
        (x_ss, x_rs), refs = refs[:2], refs[2:]
    (tail_r, head_r, dp_s, dp_r, splits, q_all, r_all, qb, ex, top_s, sum_s, neg_p, neg_half, neg_buf, neg_acc, neg_all, neg_t,
     acc_rel, acc_neg, head_c, x_ar, p_ar, half_ar, buf_ar, acc_ar, o_ar,
     tail_ss, tail_rs, head_ss, head_rs, one_s, one_r, rs_s, rs_r, ag_s, ag_r, rs2_s, rs2_r, ag2_s, ag2_r) = refs
    ent, chips, hp, dc, nch = dims.ent, dims.chips, dims.hp, dims.dc, dims.nch
    me = lax.axis_index('ent')
    core, chip = lax.rem(me, 2), me // 2
    partner = me + 1 - 2 * core
    dst_t = lax.rem(me + ent - s, ent)
    dst_h = lax.rem(me + s, ent)

    def dev(d):
        return {'ent': d}

    def peer(k):
        return lax.rem(chip + k, chips) * 2 + core

    def remote(src, dst, ss, rs, d):
        return pltpu.make_async_remote_copy(src_ref=src, dst_ref=dst, send_sem=ss, recv_sem=rs, device_id=dev(d), device_id_type=MESH)

    def loop(lo, hi, fn):
        def body(k, _):
            fn(k)
            return 0
        lax.fori_loop(lo, hi, body, 0)

    def chunks(group, fn):
        loop(0, nch // group, lambda k: fn([k * group + i for i in range(group)]))

    barrier = pltpu.get_barrier_semaphore()

    def signal(d):
        pl.semaphore_signal(barrier, inc=1, device_id=dev(d), device_id_type=MESH)
    if s:
        signal(dst_t)
        signal(dst_h)
        others = 2
    else:
        loop(1, dims.rounds, lambda k: signal(lax.rem(me + ent - k, ent)))
        others = dims.rounds - 1
    loop(1, chips, lambda k: signal(peer(k)))
    signal(partner)

    def one_hot(ids_ref, c):
        ids = ids_ref[pl.ds(s * nch + c, 1), :]
        return jnp.where(iota((dims.relp, CHUNK), 0) == ids, 1.0, 0.0).astype(BF16)

    def rel_rows(hot):
        r = nn_dot(splits[...], hot)
        return (r[:dc] + r[dc:2 * dc]) + r[2 * dc:]

    def queries(rows, r):
        x = rows.astype(F32)
        h_re, h_im, r_re, r_im = x[:hp], x[hp:], r[:hp], r[hp:]
        return jnp.concatenate([h_re * r_re - h_im * r_im, h_re * r_im + h_im * r_re], axis=0)

    def rel_query(cs):
        for c in cs:
            r_all[c] = rel_rows(one_hot(rel_ids, c))

    def head_query(cs):
        for c in cs:
            q = queries(head[c], r_all[c])
            q_all[c] = q
            qb[c, pl.ds(0, dc), :] = q.astype(BF16)

    ident = eye(CHUNK)
    for c in range(nch):
        qb[c, pl.ds(dc, 2 * LANES - dc), :] = jnp.zeros((2 * LANES - dc, CHUNK), BF16)
    acc_rel[...] = jnp.zeros_like(acc_rel)
    acc_neg[...] = jnp.zeros_like(acc_neg)
    loss[...] = jnp.zeros_like(loss)
    pl.semaphore_wait(barrier, chips + others)

    def tail_copy(c):
        return remote(tail.at[c], tail_r.at[c], tail_ss.at[c], tail_rs.at[c], dst_t)

    def head_copy(c):
        return remote(head.at[c], head_r.at[c], head_ss.at[c], head_rs.at[c], dst_h)

    def send_tails(lo, hi):
        if s:
            loop(lo, hi, lambda c: tail_copy(c).start())

    def send_heads(lo, hi):
        if s and hi > lo:
            loop(lo, hi, lambda c: head_copy(c).start())
    plan = (0,) + HEAD_SENDS.get(s, HEAD_SENDS[0])
    late = s > 0 and plan[2] < nch

    def send_heads_at(point):
        if point < 2:
            send_heads(plan[point], plan[point + 1])
        elif s:
            for c in range(plan[point], plan[point + 1]):
                if c >= AHEAD:
                    head_copy(c - AHEAD).wait_send()
                head_copy(c).start()
    if s:
        tail_in, head_in, dp_in = tail_r, head_r, dp_r
    else:
        tail_in, head_in, dp_in = tail, head, dp_s

    first = GATHER_GROUP
    send_tails(0, TAILS_FIRST)
    neg_pair = remote(neg.at[1 - core], neg_p, one_s.at[0], one_r.at[0], partner)
    neg_pair.start()
    neg_pair.wait_recv()
    neg_half[...] = neg[core] + neg_p[...]

    def rs_neg(k):
        return remote(neg_half.at[lax.rem(chip + k, chips)], neg_buf.at[k], rs_s.at[k], rs_r.at[k], peer(k))
    loop(1, chips, lambda k: rs_neg(k).start())
    send_tails(TAILS_FIRST, first)
    send_heads_at(0)
    neg_acc[...] = neg_half[chip]

    def take_neg(k):
        rs_neg(k).wait_recv()
        neg_acc[...] = neg_acc[...] + neg_buf[k]
    loop(1, chips, take_neg)

    def ag_neg(k):
        return remote(neg_acc, neg_all.at[core, chip], ag_s.at[k], ag_r.at[k], peer(k))
    loop(1, chips, lambda k: ag_neg(k).start())
    send_tails(first, nch)
    send_heads_at(1)
    if s == 0:
        def rel_copy(k):
            rows = pl.ds(pl.multiple_of(k * nch, nch), nch)
            return remote(rel_x.at[rows], rel_x_out.at[rows], x_ss.at[0, k], x_rs.at[0, k], lax.rem(me + k, ent))

        def id_copy(k):
            return remote(tail_x.at[pl.ds(k * dims.edges, dims.edges)], tail_x_out[k - 1], x_ss.at[1, k], x_rs.at[1, k], lax.rem(me + k, ent))
        loop(1, dims.rounds, lambda k: rel_copy(k).start())
        for k in range(1, dims.rounds):
            id_copy(k).start()
        rel_x_out[pl.ds(0, nch), :] = rel_x[pl.ds(0, nch), :]
    for i, part in enumerate(split3(rel_t[...])):
        splits[pl.ds(i * dc, dc), :] = part
    chunks(QUERY_GROUP, rel_query)
    chunks(QUERY_GROUP, head_query)
    neg_all[core, chip] = neg_acc[...]
    loop(1, chips, lambda k: ag_neg(k).wait_recv())
    neg_pair2 = remote(neg_all.at[core], neg_all.at[core], one_s.at[1], one_r.at[1], partner)
    neg_pair2.start()
    neg_pair2.wait_recv()
    neg_t[...] = nt_dot(eye(2 * LANES), neg_all[...].reshape(dims.negp, 2 * LANES)).astype(BF16)

    main = dims.neg // 16 * 16

    def score(cs):
        for c in cs:
            scores = nn_dot(neg_all[...].reshape(dims.negp, 2 * LANES), qb[c])
            body = scores[:main]
            top = jnp.max(body, axis=0, keepdims=True)
            if main < dims.negp:
                rest = jnp.where(iota((dims.negp - main, CHUNK), 0) < dims.neg - main, scores[main:], -1e30)
                top = jnp.maximum(top, jnp.max(rest, axis=0, keepdims=True))
            e_body = jnp.exp(body - top)
            ex[c, pl.ds(0, main), :] = e_body
            total = jnp.sum(e_body, axis=0, keepdims=True)
            if main < dims.negp:
                e_rest = jnp.exp(rest - top)
                ex[c, pl.ds(main, dims.negp - main), :] = e_rest
                total = total + jnp.sum(e_rest, axis=0, keepdims=True)
            top_s[pl.ds(c, 1), :] = top
            sum_s[pl.ds(c, 1), :] = total
    chunks(SCORE_GROUP, score)

    def head_side(cs):
        if s:
            for c in cs:
                tail_copy(c).wait_recv()
        lost, neg_q, neg_d, rel_parts, rel_hot = [], [], [], [], []
        for c in cs:
            t = tail_in[c].astype(F32)
            pos = jnp.sum(q_all[c] * t, axis=0, keepdims=True)
            neg_top = top_s[pl.ds(c, 1), :]
            top = jnp.maximum(pos, neg_top)
            pos_exp = jnp.exp(pos - top)
            scale = jnp.exp(neg_top - top)
            norm = pos_exp + scale * sum_s[pl.ds(c, 1), :]
            w = weight[pl.ds(s * nch + c, 1), :]
            lost.append(w * (top + jnp.log(norm) - pos))
            dp = w * (pos_exp / norm - 1.0)
            dp_s[pl.ds(c, 1), :] = dp
            ds = (ex[c] * (w * scale / norm)).astype(BF16)
            g = dp * t + nn_dot(neg_t[pl.ds(0, dc), :], ds)
            neg_q.append(qb[c, pl.ds(0, dc), :])
            neg_d.append(ds)
            g_re, g_im = g[:hp], g[hp:]
            r = r_all[c]
            r_re, r_im = r[:hp], r[hp:]
            head_c[c] = jnp.concatenate([g_re * r_re + g_im * r_im, g_im * r_re - g_re * r_im], axis=0)
            h = head[c].astype(F32)
            h_re, h_im = h[:hp], h[hp:]
            rel_g = jnp.concatenate([g_re * h_re + g_im * h_im, g_im * h_re - g_re * h_im], axis=0)
            rel_parts.append(jnp.concatenate(split3(rel_g), axis=0))
            rel_hot.append(one_hot(rel_ids, c))
        loss[pl.ds(0, 1), :] += sum(lost)
        acc_neg[...] += nt_dot(jnp.concatenate(neg_q, axis=1), jnp.concatenate(neg_d, axis=1))
        part = nt_dot(jnp.concatenate(rel_parts, axis=1), jnp.concatenate(rel_hot, axis=1))
        acc_rel[...] += (part[:dc] + part[dc:2 * dc]) + part[2 * dc:]
    chunks(HEAD_GROUP, head_side)

    if s:
        dp_copy = remote(dp_s, dp_r, one_s.at[2], one_r.at[2], dst_h)
        dp_copy.start()

    def tile_place(t):
        d, j = t // dims.tpd, t % dims.tpd
        return d // chips, d % chips, j
    rel_cols = dims.relp // LANES
    for t in range(dims.tpd * ent):
        i, j = t // dims.cols, t % dims.cols
        if t >= dims.tiles:
            x_ar[tile_place(t)] = jnp.zeros((8, LANES), F32)
        elif j < rel_cols:
            x_ar[tile_place(t)] = acc_rel[pl.ds(8 * i, 8), pl.ds(j * LANES, LANES)]
        else:
            x_ar[tile_place(t)] = acc_neg[pl.ds(8 * i, 8), pl.ds((j - rel_cols) * LANES, LANES)]

    ar_pair = remote(x_ar.at[1 - core], p_ar, one_s.at[3], one_r.at[3], partner)
    ar_pair.start()
    send_heads_at(2)

    def rows_of(cols):
        gap = jnp.zeros((LANES - hp, CHUNK), F32)
        x = jnp.concatenate([cols[:hp], gap, cols[hp:], gap], axis=0)
        return nt_dot(jnp.concatenate([ident] * 3, axis=1), jnp.concatenate(split3(x), axis=1))

    def put_rows(out, c, rows):
        base = pl.multiple_of(c * 2 * CHUNK, 2 * CHUNK)
        out[pl.ds(base, CHUNK, stride=2), :] = rows[:, :LANES]
        out[pl.ds(base + 1, CHUNK, stride=2), :] = rows[:, LANES:]

    def head_rows(cs):
        for c in cs:
            put_rows(head_g, c, rows_of(head_c[c]))

    def tail_side(cs):
        if s:
            for c in cs:
                head_copy(c).wait_recv()
        for c in cs:
            q = queries(head_in[c], rel_rows(one_hot(rel_ids_p, c)))
            put_rows(tail_g, c, rows_of(dp_in[pl.ds(c, 1), :] * q))

    ar_pair.wait_recv()
    half_ar[...] = x_ar[core] + p_ar[...]

    def rs_ar(k):
        return remote(half_ar.at[lax.rem(chip + k, chips)], buf_ar.at[k], rs2_s.at[k], rs2_r.at[k], peer(k))
    loop(1, chips, lambda k: rs_ar(k).start())
    send_heads_at(3)
    chunks(ROWS_GROUP, head_rows)
    send_heads_at(4)
    acc_ar[...] = half_ar[chip]

    def take_ar(k):
        rs_ar(k).wait_recv()
        acc_ar[...] += buf_ar[k]
    loop(1, chips, take_ar)

    def ag_ar(k):
        return remote(acc_ar, o_ar.at[core, chip], ag2_s.at[k], ag2_r.at[k], peer(k))
    loop(1, chips, lambda k: ag_ar(k).start())
    send_heads_at(5)
    o_ar[core, chip] = acc_ar[...]
    def tail_gradients():
        if s:
            dp_copy.wait_recv()
        chunks(TAIL_GROUP, tail_side)
    if not late:
        tail_gradients()
    loop(1, chips, lambda k: ag_ar(k).wait_recv())
    ar_pair2 = remote(o_ar.at[core], o_ar.at[core], one_s.at[4], one_r.at[4], partner)
    ar_pair2.start()
    send_heads_at(6)
    ar_pair2.wait_recv()

    for t in range(dims.tiles):
        i, j = t // dims.cols, t % dims.cols
        if j < rel_cols:
            acc_rel[pl.ds(8 * i, 8), pl.ds(j * LANES, LANES)] = o_ar[tile_place(t)]
        else:
            acc_neg[pl.ds(8 * i, 8), pl.ds((j - rel_cols) * LANES, LANES)] = o_ar[tile_place(t)]
    g = acc_rel[...]
    state = rel_state[...] + jnp.sum(g * g, axis=0, keepdims=True) * (1.0 / dims.dim)
    rel_state_out[...] = state
    rel_t_out[...] = rel_t[...] - LEARN_RATE * g / jnp.sqrt(state[:1] + ADA_EPS)
    for c in range(dims.negp // CHUNK):
        put_rows(neg_g, c, rows_of(acc_neg[:, pl.ds(c * CHUNK, CHUNK)]))
    if late:
        tail_gradients()

    neg_pair.wait_send()
    neg_pair2.wait_send()
    ar_pair.wait_send()
    ar_pair2.wait_send()
    if s:
        dp_copy.wait_send()

        loop(0, nch, lambda c: tail_copy(c).wait_send())
        for c in range(nch):
            if plan[2] == nch or c >= nch - AHEAD or c < plan[2] - AHEAD:
                head_copy(c).wait_send()

    if s == 0:
        def moved(k):
            rel_copy(k).wait()
        loop(1, dims.rounds, moved)
        for k in range(1, dims.rounds):
            id_copy(k).wait()

    def sent_peers(k):
        rs_neg(k).wait_send()
        ag_neg(k).wait_send()
        rs_ar(k).wait_send()
        ag_ar(k).wait_send()
    loop(1, chips, sent_peers)


def bucket_step(dims, s, rows_in, rel_t, rel_state, rel_ids, rel_ids_p, weight, extra):
    d = dims
    vm = pl.BlockSpec(memory_space=VMEM)
    sds = jax.ShapeDtypeStruct
    dma = pltpu.SemaphoreType.DMA
    outs = [sds((2 * d.edges, LANES), F32), sds((2 * d.edges, LANES), F32), sds((2 * d.negp, LANES), F32),
            sds((d.dc, d.relp), F32), sds((8, d.relp), F32), sds((8, CHUNK), F32)]
    if extra:
        outs += [sds(extra[1].shape, I32)] + [sds((d.edges,), I32)] * (d.rounds - 1)
    tail, head, neg = rows_in
    rows = VMEM((d.nch, d.dc, CHUNK), BF16)
    wide = VMEM((d.nch, d.dc, CHUNK), F32)
    line = VMEM((d.nch, CHUNK), F32)
    neg_part = VMEM((d.chips, d.negc, 2 * LANES), BF16)
    ar_part = VMEM((d.chips, d.tpd, 8, LANES), F32)
    scratch = [dma((2, d.rounds))] * 2 if extra else []
    scratch += [rows, rows, line, line,
                VMEM((3 * d.dc, d.relp), BF16), wide, wide, VMEM((d.nch, 2 * LANES, CHUNK), BF16),
                VMEM((d.nch, d.negp, CHUNK), F32), line, line,
                neg_part, neg_part, neg_part, VMEM((d.negc, 2 * LANES), BF16),
                VMEM((2, d.chips, d.negc, 2 * LANES), BF16), VMEM((2 * LANES, d.negp), BF16),
                VMEM((d.dc, d.relp), F32), VMEM((d.dc, d.negp), F32), wide,
                VMEM((2, d.chips, d.tpd, 8, LANES), F32), ar_part, ar_part, ar_part,
                VMEM((d.tpd, 8, LANES), F32), VMEM((2, d.chips, d.tpd, 8, LANES), F32),
                dma((d.nch,)), dma((d.nch,)), dma((d.nch,)), dma((d.nch,)), dma((5,)), dma((5,))]
    scratch += [dma((d.chips,))] * 8
    return pl.pallas_call(
        functools.partial(bucket_kernel, d, s), out_shape=outs,
        in_specs=[vm] * (8 + len(extra)), out_specs=[vm] * len(outs),
        scratch_shapes=scratch, name=f'bucket_{s}',
        compiler_params=pltpu.CompilerParams(collective_id=s, has_side_effects=True, vmem_limit_bytes=36 << 20),
    )(head, tail, neg.reshape(2, d.chips, d.negc, 2 * LANES), rel_t, rel_state, rel_ids, rel_ids_p, weight, *extra)


def solution(mesh):
    row_spec = P(('sweep', 'ent'), None)
    flat_spec = P(('sweep', 'ent'))
    rel_spec = P('sweep', None)
    state_spec = P('sweep')
    edge_spec = P(('sweep', 'ent'), None, None)

    def device_fn(ent_emb, ent_ada, rel_emb, rel_ada, head_idx, tail_idx, rel_idx, edge_mask, neg_idx):
        d = Dims(mesh, ent_emb, rel_emb, head_idx, neg_idx)
        me = lax.axis_index('ent')
        table = pack(d, ent_emb, ent_ada)
        rel = jnp.pad(rel_emb.reshape(d.num_rel, 2, d.half), ((0, d.relp - d.num_rel), (0, 0), (0, d.hp - d.half)))
        rel_t = rel.reshape(d.relp, d.dc).T
        rel_state = jnp.broadcast_to(jnp.pad(rel_ada, (0, d.relp - d.num_rel), constant_values=1.0), (8, d.relp))

        head_ids = (head_idx[0] * 2).reshape(-1)
        own_tail_ids = (tail_idx[0] * 2).reshape(-1)
        local = neg_idx - me * d.rows
        owned = (local >= 0) & (local < d.rows)
        neg_all = jnp.pad(jnp.where(owned, local, d.rows) * 2, ((0, 0), (0, d.negp - d.neg)), constant_values=2 * d.rows)
        place = lax.broadcasted_iota(I32, neg_all.shape, 1)
        key = jnp.where(neg_all < 2 * d.rows, place, place + d.negp)
        key, neg_rows = lax.sort((key, neg_all), dimension=1, num_keys=1)
        neg_src = key % d.negp * 2
        counts = jnp.sum(owned.astype(I32), axis=1)
        rel_ids = rel_idx[0].reshape(d.rounds * d.nch, CHUNK)
        weight = edge_mask[0].astype(F32).reshape(d.rounds * d.nch, CHUNK)
        def per_round(x):
            size = x.size // d.rounds
            return [x.reshape(-1)[k * size:(k + 1) * size] for k in range(d.rounds)]
        heads, counts, neg_rows, neg_src = (per_round(x) for x in (head_ids, counts, neg_rows, neg_src))
        first_tails = own_tail_ids[:d.edges]
        table, heads, counts, neg_rows, neg_src, first_tails = lax.optimization_barrier((table, heads, counts, neg_rows, neg_src, first_tails))

        def lists(k):
            return [counts[k], heads[k], tails[k], neg_rows[k], neg_src[k]]
        tails = [first_tails]
        rows_in = table_step(d, None, lists(0), None, table)
        losses = []
        for s in range(d.rounds):
            if s == 0:
                res = bucket_step(d, s, rows_in, rel_t, rel_state, rel_ids, rel_ids, weight, (own_tail_ids, rel_ids))
                rel_ids_p = res[6]
                tails += res[7:]
            else:
                res = bucket_step(d, s, rows_in, rel_t, rel_state, rel_ids, rel_ids_p, weight, ())
            hg, tg, ng, rel_t, rel_state, loss = res[:6]
            losses.append(loss)
            table, *rows_in = table_step(d, lists(s), lists(s + 1) if s + 1 < d.rounds else None, (hg, tg, ng), table)
        loss = jnp.sum(jnp.stack(losses), axis=(1, 2)) / d.edges
        emb, ada = unpack(d, table)
        rel_out = rel_t.T.reshape(d.relp, 2, d.hp)[:d.num_rel, :, :d.half].reshape(d.num_rel, d.dim)
        return emb, ada, rel_out, rel_state[0, :d.num_rel], loss[None, :]

    return jax.shard_map(device_fn, mesh=mesh,
                         in_specs=(row_spec, flat_spec, rel_spec, state_spec, edge_spec, edge_spec, edge_spec, edge_spec, rel_spec),
                         out_specs=(row_spec, flat_spec, rel_spec, state_spec, row_spec), check_vma=False)
```

time: 1780 us -> 1260 us (0.71)
  Pallas kernels: 1730 us -> 1210 us
    pallas_call x18 -> x17, Pallas kernels: 575 us -> 292 us  [table_step(): pl.pallas_call(functools.partial(table_kernel, dims, old is not None, new...]
    pallas_call x16, Pallas kernels: 1130 us -> 908 us  [bucket_step(): pl.pallas_call(functools.partial(bucket_kernel, d, s), out_shape=outs, in...]
where the time goes in v2:
time: 1260 us; the launch traced here: 1240 us
  Pallas kernels  1210 us (96%)
  between operations  15 us (1%)
  local copies, waits for them, and re-layouts  14.8 us (1%)
    pallas_call x16, Pallas kernels, bucket_step(): pl.pallas_call(functools.partial(bucket_kernel, d, s), out_shape=outs, in...  908 us
    pallas_call x17, Pallas kernels, table_step(): pl.pallas_call(functools.partial(table_kernel, dims, old is not None, new...  292 us

profile of v2, /device:TPU:97, one launch (start us, length us, event | category | flops | bytes accessed | tf_op | source)
XLA Modules:
  0.0 1244.9 jit_solution(14853710816866839870)
XLA Ops:
  7.2 0.0 copy-start.4
  7.2 0.1 sort.17.cloned.1.call-start
  7.3 0.9 select_multiply_fusion
  8.2 0.6 fusion.6
  8.8 0.1 sort.17.cloned.1.call-update
  8.9 0.9 broadcast_multiply_fusion.1
  9.8 0.1 fusion.3
  9.9 0.9 fusion.2
  10.8 0.7 fusion.7
  11.5 1.0 reshape.214
  12.5 0.9 reshape_squeeze.3.refs_5_.refs_6_.refs_9_
  13.4 0.9 convert_element_type.13
  14.4 0.0 copy-done.4
  14.4 0.0 copy-start.3
  14.4 2.9 copy-done.3
  17.3 0.0 copy-start.5
  17.3 4.2 pack.1.refs_5_.refs_13_
  21.5 0.0 copy-start
  21.5 3.3 copy-done
  24.8 0.0 copy-done.5
  24.8 0.0 sort.17.cloned.1.call-done
  24.8 1.1 fusion.5
  25.9 0.8 fusion.1
  26.7 0.0 copy-start.1
  26.7 3.4 copy-done.1
  30.1 6.9 table.17
  37.0 44.1 %bucket_0.1 = (f32[4096,128]{1,0:T(8,128)S(1)}, f32[4096,128]{1,0:T(8,128)S(1)}, f32[1024,128]{1,0:T(8,128)S(1)}, f32[208,256]{1,0:T(8,128)S(1)}, f32[8,256]{1,0...) custom-call(bf16[8,208,256]{2,1,0:T(8,128)(2,1)S(1)} %get-tuple-elem, ...), custom_call_target="tpu_custom_call" | custom-call | tf_op jit(solution)/shard_map/bucket_0/pallas_call | solution.py:685
  81.1 0.0 copy-done.2
  81.1 18.1 %table.18 = (f32[16400,128]{1,0:T(8,128)S(1)}, bf16[8,208,256]{2,1,0:T(8,128)(2,1)S(1)}, bf16[8,208,256]{2,1,0:T(8,128)(2,1)S(1)}, bf16[512,256]{1,0:T(8,128)(2,1)S(1)}) custom-call(s32[1]{0:T(128)} %get-tuple-element.254.refs_0_, s32[2048]{0:T(1024)S(1)} %bitcast.141, s32[2048]{0:T(1024)S(1)} %bitcast.143, ...), custom_call_target="tpu_custom_call", output_to_operand_aliasing={{0}: (13, {})} | custom-call | tf_op jit(solution)/shard_map/table/pallas_call | solution.py:320
  99.2 41.9 %bucket_1.1 = (f32[4096,128]{1,0:T(8,128)S(1)}, f32[4096,128]{1,0:T(8,128)S(1)}, f32[1024,128]{1,0:T(8,128)S(1)}, f32[208,256]{1,0:T(8,128)S(1)}, f32[8,256]{1,0:T(8,128)S(1)}, /*index=5*/f32[8,256]{1,0:T(8,128)S(1)}) custom-call(bf16[8,208,256]{2,1,0:T(8,128)(2,1)S(1)} %get-tuple-element.339.refs_0_, bf16[8,208,256]{2,1,0:T(8,128)(2,1)S(1)} %get-tuple-element.340.refs_1_, ...), custom_call_target="tpu_custom_call" | custom-call | tf_op jit(solution)/shard_map/bucket_1/pallas_call | solution.py:685
  141.2 18.5 %table.19 = (f32[16400,128]{1,0:T(8,128)S(1)}, bf16[8,208,256]{2,1,0:T(8,128)(2,1)S(1)}, bf16[8,208,256]{2,1,0:T(8,128)(2,1)S(1)}, bf16[512,256]{1,0:T(8,128)(2,1)S(1)}) custom-call(s32[1]{0:T(128)} %get-tuple-element.331.refs_5_.refs_0_, s32[2048]{0:T(1024)S(1)} %bitcast.171, ...), custom_call_target="tpu_custom_call", output_to_operand_aliasing={{0}: (13, {})} | custom-call | tf_op jit(solution)/shard_map/table/pallas_call | solution.py:320
  159.7 46.4 %bucket_2.1 = (f32[4096,128]{1,0:T(8,128)S(1)}, f32[4096,128]{1,0:T(8,128)S(1)}, f32[1024,128]{1,0:T(8,128)S(1)}, f32[208,256]{1,0:T(8,128)S(1)}, f32[8,256]{1,0:T(8,128)S(1)}, /*index=5*/f32[8,256]{1,0:T(8,128)S(1)}) custom-call(bf16[8,208,256]{2,1,0:T(8,128)(2,1)S(1)} %get-tuple-element.349.refs_0_, bf16[8,208,256]{2,1,0:T(8,128)(2,1)S(1)} %get-tuple-element.350.refs_1_, ...), custom_call_target="tpu_custom_call" | custom-call | tf_op jit(solution)/shard_map/bucket_2/pallas_call | solution.py:685
  206.1 18.1 %table.20 = (f32[16400,128]{1,0:T(8,128)S(1)}, bf16[8,208,256]{2,1,0:T(8,128)(2,1)S(1)}, bf16[8,208,256]{2,1,0:T(8,128)(2,1)S(1)}, bf16[512,256]{1,0:T(8,128)(2,1)S(1)}) custom-call(s32[1]{0:T(128)} %get-tuple-element.326.refs_5_.refs_0_, s32[2048]{0:T(1024)S(1)} %bitcast.169, ...), custom_call_target="tpu_custom_call", output_to_operand_aliasing={{0}: (13, {})} | custom-call | tf_op jit(solution)/shard_map/table/pallas_call | solution.py:320
  224.2 56.8 %bucket_3.1 = (f32[4096,128]{1,0:T(8,128)S(1)}, f32[4096,128]{1,0:T(8,128)S(1)}, f32[1024,128]{1,0:T(8,128)S(1)}, f32[208,256]{1,0:T(8,128)S(1)}, f32[8,256]{1,0:T(8,128)S(1)}, /*index=5*/f32[8,256]{1,0:T(8,128)S(1)}) custom-call(bf16[8,208,256]{2,1,0:T(8,128)(2,1)S(1)} %get-tuple-element.358.refs_0_, bf16[8,208,256]{2,1,0:T(8,128)(2,1)S(1)} %get-tuple-element.359.refs_1_, ...), custom_call_target="tpu_custom_call" | custom-call | tf_op jit(solution)/shard_map/bucket_3/pallas_call | solution.py:685
  281.1 18.3 %table.21 = (f32[16400,128]{1,0:T(8,128)S(1)}, bf16[8,208,256]{2,1,0:T(8,128)(2,1)S(1)}, bf16[8,208,256]{2,1,0:T(8,128)(2,1)S(1)}, bf16[512,256]{1,0:T(8,128)(2,1)S(1)}) custom-call(s32[1]{0:T(128)} %get-tuple-element.321.refs_5_.refs_0_, s32[2048]{0:T(1024)S(1)} %bitcast.167, ...), custom_call_target="tpu_custom_call", output_to_operand_aliasing={{0}: (13, {})} | custom-call | tf_op jit(solution)/shard_map/table/pallas_call | solution.py:320
  299.3 68.8 %bucket_4.1 = (f32[4096,128]{1,0:T(8,128)S(1)}, f32[4096,128]{1,0:T(8,128)S(1)}, f32[1024,128]{1,0:T(8,128)S(1)}, f32[208,256]{1,0:T(8,128)S(1)}, f32[8,256]{1,0:T(8,128)S(1)}, /*index=5*/f32[8,256]{1,0:T(8,128)S(1)}) custom-call(bf16[8,208,256]{2,1,0:T(8,128)(2,1)S(1)} %get-tuple-element.367.refs_0_, bf16[8,208,256]{2,1,0:T(8,128)(2,1)S(1)} %get-tuple-element.368.refs_1_, ...), custom_call_target="tpu_custom_call" | custom-call | tf_op jit(solution)/shard_map/bucket_4/pallas_call | solution.py:685
  368.2 18.0 %table.22 = (f32[16400,128]{1,0:T(8,128)S(1)}, bf16[8,208,256]{2,1,0:T(8,128)(2,1)S(1)}, bf16[8,208,256]{2,1,0:T(8,128)(2,1)S(1)}, bf16[512,256]{1,0:T(8,128)(2,1)S(1)}) custom-call(s32[1]{0:T(128)} %get-tuple-element.316.refs_5_.refs_0_, s32[2048]{0:T(1024)S(1)} %bitcast.165, ...), custom_call_target="tpu_custom_call", output_to_operand_aliasing={{0}: (13, {})} | custom-call | tf_op jit(solution)/shard_map/table/pallas_call | solution.py:320
  386.2 61.7 %bucket_5.1 = (f32[4096,128]{1,0:T(8,128)S(1)}, f32[4096,128]{1,0:T(8,128)S(1)}, f32[1024,128]{1,0:T(8,128)S(1)}, f32[208,256]{1,0:T(8,128)S(1)}, f32[8,256]{1,0:T(8,128)S(1)}, /*index=5*/f32[8,256]{1,0:T(8,128)S(1)}) custom-call(bf16[8,208,256]{2,1,0:T(8,128)(2,1)S(1)} %get-tuple-element.376.refs_0_, bf16[8,208,256]{2,1,0:T(8,128)(2,1)S(1)} %get-tuple-element.377.refs_1_, ...), custom_call_target="tpu_custom_call" | custom-call | tf_op jit(solution)/shard_map/bucket_5/pallas_call | solution.py:685
  447.9 18.1 %table.23 = (f32[16400,128]{1,0:T(8,128)S(1)}, bf16[8,208,256]{2,1,0:T(8,128)(2,1)S(1)}, bf16[8,208,256]{2,1,0:T(8,128)(2,1)S(1)}, bf16[512,256]{1,0:T(8,128)(2,1)S(1)}) custom-call(s32[1]{0:T(128)} %get-tuple-element.311.refs_5_.refs_0_, s32[2048]{0:T(1024)S(1)} %bitcast.163, ...), custom_call_target="tpu_custom_call", output_to_operand_aliasing={{0}: (13, {})} | custom-call | tf_op jit(solution)/shard_map/table/pallas_call | solution.py:320
  466.1 50.8 %bucket_6.1 = (f32[4096,128]{1,0:T(8,128)S(1)}, f32[4096,128]{1,0:T(8,128)S(1)}, f32[1024,128]{1,0:T(8,128)S(1)}, f32[208,256]{1,0:T(8,128)S(1)}, f32[8,256]{1,0:T(8,128)S(1)}, /*index=5*/f32[8,256]{1,0:T(8,128)S(1)}) custom-call(bf16[8,208,256]{2,1,0:T(8,128)(2,1)S(1)} %get-tuple-element.385.refs_0_, bf16[8,208,256]{2,1,0:T(8,128)(2,1)S(1)} %get-tuple-element.386.refs_1_, ...), custom_call_target="tpu_custom_call" | custom-call | tf_op jit(solution)/shard_map/bucket_6/pallas_call | solution.py:685
  516.9 18.0 %table.24 = (f32[16400,128]{1,0:T(8,128)S(1)}, bf16[8,208,256]{2,1,0:T(8,128)(2,1)S(1)}, bf16[8,208,256]{2,1,0:T(8,128)(2,1)S(1)}, bf16[512,256]{1,0:T(8,128)(2,1)S(1)}) custom-call(s32[1]{0:T(128)} %get-tuple-element.306.refs_5_.refs_0_, s32[2048]{0:T(1024)S(1)} %bitcast.161, ...), custom_call_target="tpu_custom_call", output_to_operand_aliasing={{0}: (13, {})} | custom-call | tf_op jit(solution)/shard_map/table/pallas_call | solution.py:320
  535.0 49.9 %bucket_7.1 = (f32[4096,128]{1,0:T(8,128)S(1)}, f32[4096,128]{1,0:T(8,128)S(1)}, f32[1024,128]{1,0:T(8,128)S(1)}, f32[208,256]{1,0:T(8,128)S(1)}, f32[8,256]{1,0:T(8,128)S(1)}, /*index=5*/f32[8,256]{1,0:T(8,128)S(1)}) custom-call(bf16[8,208,256]{2,1,0:T(8,128)(2,1)S(1)} %get-tuple-element.394.refs_0_, bf16[8,208,256]{2,1,0:T(8,128)(2,1)S(1)} %get-tuple-element.395.refs_1_, ...), custom_call_target="tpu_custom_call" | custom-call | tf_op jit(solution)/shard_map/bucket_7/pallas_call | solution.py:685
  584.9 18.5 %table.25 = (f32[16400,128]{1,0:T(8,128)S(1)}, bf16[8,208,256]{2,1,0:T(8,128)(2,1)S(1)}, bf16[8,208,256]{2,1,0:T(8,128)(2,1)S(1)}, bf16[512,256]{1,0:T(8,128)(2,1)S(1)}) custom-call(s32[1]{0:T(128)} %get-tuple-element.301.refs_5_.refs_0_, s32[2048]{0:T(1024)S(1)} %bitcast.159, ...), custom_call_target="tpu_custom_call", output_to_operand_aliasing={{0}: (13, {})} | custom-call | tf_op jit(solution)/shard_map/table/pallas_call | solution.py:320
  603.4 47.0 %bucket_8.1 = (f32[4096,128]{1,0:T(8,128)S(1)}, f32[4096,128]{1,0:T(8,128)S(1)}, f32[1024,128]{1,0:T(8,128)S(1)}, f32[208,256]{1,0:T(8,128)S(1)}, f32[8,256]{1,0:T(8,128)S(1)}, /*index=5*/f32[8,256]{1,0:T(8,128)S(1)}) custom-call(bf16[8,208,256]{2,1,0:T(8,128)(2,1)S(1)} %get-tuple-element.403.refs_0_, bf16[8,208,256]{2,1,0:T(8,128)(2,1)S(1)} %get-tuple-element.404.refs_1_, ...), custom_call_target="tpu_custom_call" | custom-call | tf_op jit(solution)/shard_map/bucket_8/pallas_call | solution.py:685
  650.4 18.0 %table.26 = (f32[16400,128]{1,0:T(8,128)S(1)}, bf16[8,208,256]{2,1,0:T(8,128)(2,1)S(1)}, bf16[8,208,256]{2,1,0:T(8,128)(2,1)S(1)}, bf16[512,256]{1,0:T(8,128)(2,1)S(1)}) custom-call(s32[1]{0:T(128)} %get-tuple-element.296.refs_5_.refs_0_, s32[2048]{0:T(1024)S(1)} %bitcast.157, ...), custom_call_target="tpu_custom_call", output_to_operand_aliasing={{0}: (13, {})} | custom-call | tf_op jit(solution)/shard_map/table/pallas_call | solution.py:320
  668.4 55.7 %bucket_9.1 = (f32[4096,128]{1,0:T(8,128)S(1)}, f32[4096,128]{1,0:T(8,128)S(1)}, f32[1024,128]{1,0:T(8,128)S(1)}, f32[208,256]{1,0:T(8,128)S(1)}, f32[8,256]{1,0:T(8,128)S(1)}, /*index=5*/f32[8,256]{1,0:T(8,128)S(1)}) custom-call(bf16[8,208,256]{2,1,0:T(8,128)(2,1)S(1)} %get-tuple-element.412.refs_0_, bf16[8,208,256]{2,1,0:T(8,128)(2,1)S(1)} %get-tuple-element.413.refs_1_, ...), custom_call_target="tpu_custom_call" | custom-call | tf_op jit(solution)/shard_map/bucket_9/pallas_call | solution.py:685
  724.1 18.2 %table.27 = (f32[16400,128]{1,0:T(8,128)S(1)}, bf16[8,208,256]{2,1,0:T(8,128)(2,1)S(1)}, bf16[8,208,256]{2,1,0:T(8,128)(2,1)S(1)}, bf16[512,256]{1,0:T(8,128)(2,1)S(1)}) custom-call(s32[1]{0:T(128)} %get-tuple-element.291.refs_5_.refs_0_, s32[2048]{0:T(1024)S(1)} %bitcast.155, ...), custom_call_target="tpu_custom_call", output_to_operand_aliasing={{0}: (13, {})} | custom-call | tf_op jit(solution)/shard_map/table/pallas_call | solution.py:320
  742.2 63.8 %bucket_10.1 = (f32[4096,128]{1,0:T(8,128)S(1)}, f32[4096,128]{1,0:T(8,128)S(1)}, f32[1024,128]{1,0:T(8,128)S(1)}, f32[208,256]{1,0:T(8,128)S(1)}, f32[8,256]{1,0:T(8,128)S(1)}, /*index=5*/f32[8,256]{1,0:T(8,128)S(1)}) custom-call(bf16[8,208,256]{2,1,0:T(8,128)(2,1)S(1)} %get-tuple-element.421.refs_0_, bf16[8,208,256]{2,1,0:T(8,128)(2,1)S(1)} %get-tuple-element.422.refs_1_, ...), custom_call_target="tpu_custom_call" | custom-call | tf_op jit(solution)/shard_map/bucket_10/pallas_call | solution.py:685
  806.1 18.0 %table.28 = (f32[16400,128]{1,0:T(8,128)S(1)}, bf16[8,208,256]{2,1,0:T(8,128)(2,1)S(1)}, bf16[8,208,256]{2,1,0:T(8,128)(2,1)S(1)}, bf16[512,256]{1,0:T(8,128)(2,1)S(1)}) custom-call(s32[1]{0:T(128)} %get-tuple-element.286.refs_5_.refs_0_, s32[2048]{0:T(1024)S(1)} %bitcast.153, ...), custom_call_target="tpu_custom_call", output_to_operand_aliasing={{0}: (13, {})} | custom-call | tf_op jit(solution)/shard_map/table/pallas_call | solution.py:320
  824.0 62.9 %bucket_11.1 = (f32[4096,128]{1,0:T(8,128)S(1)}, f32[4096,128]{1,0:T(8,128)S(1)}, f32[1024,128]{1,0:T(8,128)S(1)}, f32[208,256]{1,0:T(8,128)S(1)}, f32[8,256]{1,0:T(8,128)S(1)}, /*index=5*/f32[8,256]{1,0:T(8,128)S(1)}) custom-call(bf16[8,208,256]{2,1,0:T(8,128)(2,1)S(1)} %get-tuple-element.430.refs_0_, bf16[8,208,256]{2,1,0:T(8,128)(2,1)S(1)} %get-tuple-element.431.refs_1_, ...), custom_call_target="tpu_custom_call" | custom-call | tf_op jit(solution)/shard_map/bucket_11/pallas_call | solution.py:685
  886.9 18.2 %table.29 = (f32[16400,128]{1,0:T(8,128)S(1)}, bf16[8,208,256]{2,1,0:T(8,128)(2,1)S(1)}, bf16[8,208,256]{2,1,0:T(8,128)(2,1)S(1)}, bf16[512,256]{1,0:T(8,128)(2,1)S(1)}) custom-call(s32[1]{0:T(128)} %get-tuple-element.281.refs_5_.refs_0_, s32[2048]{0:T(1024)S(1)} %bitcast.151, ...), custom_call_target="tpu_custom_call", output_to_operand_aliasing={{0}: (13, {})} | custom-call | tf_op jit(solution)/shard_map/table/pallas_call | solution.py:320
  905.1 66.8 %bucket_12.1 = (f32[4096,128]{1,0:T(8,128)S(1)}, f32[4096,128]{1,0:T(8,128)S(1)}, f32[1024,128]{1,0:T(8,128)S(1)}, f32[208,256]{1,0:T(8,128)S(1)}, f32[8,256]{1,0:T(8,128)S(1)}, /*index=5*/f32[8,256]{1,0:T(8,128)S(1)}) custom-call(bf16[8,208,256]{2,1,0:T(8,128)(2,1)S(1)} %get-tuple-element.439.refs_0_, bf16[8,208,256]{2,1,0:T(8,128)(2,1)S(1)} %get-tuple-element.440.refs_1_, ...), custom_call_target="tpu_custom_call" | custom-call | tf_op jit(solution)/shard_map/bucket_12/pallas_call | solution.py:685
  971.9 18.1 %table.30 = (f32[16400,128]{1,0:T(8,128)S(1)}, bf16[8,208,256]{2,1,0:T(8,128)(2,1)S(1)}, bf16[8,208,256]{2,1,0:T(8,128)(2,1)S(1)}, bf16[512,256]{1,0:T(8,128)(2,1)S(1)}) custom-call(s32[1]{0:T(128)} %get-tuple-element.276.refs_5_.refs_0_, s32[2048]{0:T(1024)S(1)} %bitcast.149, ...), custom_call_target="tpu_custom_call", output_to_operand_aliasing={{0}: (13, {})} | custom-call | tf_op jit(solution)/shard_map/table/pallas_call | solution.py:320
  990.0 64.5 %bucket_13.1 = (f32[4096,128]{1,0:T(8,128)S(1)}, f32[4096,128]{1,0:T(8,128)S(1)}, f32[1024,128]{1,0:T(8,128)S(1)}, f32[208,256]{1,0:T(8,128)S(1)}, f32[8,256]{1,0:T(8,128)S(1)}, /*index=5*/f32[8,256]{1,0:T(8,128)S(1)}) custom-call(bf16[8,208,256]{2,1,0:T(8,128)(2,1)S(1)} %get-tuple-element.448.refs_0_, bf16[8,208,256]{2,1,0:T(8,128)(2,1)S(1)} %get-tuple-element.449.refs_1_, ...), custom_call_target="tpu_custom_call" | custom-call | tf_op jit(solution)/shard_map/bucket_13/pallas_call | solution.py:685
  1054.5 18.4 %table.31 = (f32[16400,128]{1,0:T(8,128)S(1)}, bf16[8,208,256]{2,1,0:T(8,128)(2,1)S(1)}, bf16[8,208,256]{2,1,0:T(8,128)(2,1)S(1)}, bf16[512,256]{1,0:T(8,128)(2,1)S(1)}) custom-call(s32[1]{0:T(128)} %get-tuple-element.271.refs_5_.refs_0_, s32[2048]{0:T(1024)S(1)} %bitcast.147, ...), custom_call_target="tpu_custom_call", output_to_operand_aliasing={{0}: (13, {})} | custom-call | tf_op jit(solution)/shard_map/table/pallas_call | solution.py:320
  1072.9 64.0 %bucket_14.1 = (f32[4096,128]{1,0:T(8,128)S(1)}, f32[4096,128]{1,0:T(8,128)S(1)}, f32[1024,128]{1,0:T(8,128)S(1)}, f32[208,256]{1,0:T(8,128)S(1)}, f32[8,256]{1,0:T(8,128)S(1)}, /*index=5*/f32[8,256]{1,0:T(8,128)S(1)}) custom-call(bf16[8,208,256]{2,1,0:T(8,128)(2,1)S(1)} %get-tuple-element.457.refs_0_, bf16[8,208,256]{2,1,0:T(8,128)(2,1)S(1)} %get-tuple-element.458.refs_1_, ...), custom_call_target="tpu_custom_call" | custom-call | tf_op jit(solution)/shard_map/bucket_14/pallas_call | solution.py:685
  1136.8 18.1 %table.32 = (f32[16400,128]{1,0:T(8,128)S(1)}, bf16[8,208,256]{2,1,0:T(8,128)(2,1)S(1)}, bf16[8,208,256]{2,1,0:T(8,128)(2,1)S(1)}, bf16[512,256]{1,0:T(8,128)(2,1)S(1)}) custom-call(s32[1]{0:T(128)} %get-tuple-element.266.refs_5_.refs_0_, s32[2048]{0:T(1024)S(1)} %bitcast.145, ...), custom_call_target="tpu_custom_call", output_to_operand_aliasing={{0}: (13, {})} | custom-call | tf_op jit(solution)/shard_map/table/pallas_call | solution.py:320
  1154.9 63.1 %bucket_15.1 = (f32[4096,128]{1,0:T(8,128)S(1)}, f32[4096,128]{1,0:T(8,128)S(1)}, f32[1024,128]{1,0:T(8,128)S(1)}, f32[208,256]{1,0:T(8,128)S(1)}, f32[8,256]{1,0:T(8,128)S(1)}, /*index=5*/f32[8,256]{1,0:T(8,128)S(1)}) custom-call(bf16[8,208,256]{2,1,0:T(8,128)(2,1)S(1)} %get-tuple-element.466.refs_0_, bf16[8,208,256]{2,1,0:T(8,128)(2,1)S(1)} %get-tuple-element.467.refs_1_, ...), custom_call_target="tpu_custom_call" | custom-call | tf_op jit(solution)/shard_map/bucket_15/pallas_call | solution.py:685
  1218.0 12.1 table.33.t_ref
  1230.2 5.3 unpack.1
  1235.5 0.7 reshape.233
  1236.2 0.6 slice.480
  1236.9 0.2 reduce_sum.19
  1237.1 0.5 multiply_bitcast_fusion
  (25 shorter events, 0.2 us)
Async XLA Ops:
  7.2 7.2 copy-start.4
  7.2 17.6 %sort.17.cloned.1.call-start = ((), (), s32[]{:S(2)}) async-start(), calls=%async_computation | async-start | bytes 196640 | tf_op jit(solution)/shard_map/sort | solution.py:715
  14.4 2.9 copy-start.3
  17.3 7.5 copy-start.5
  21.5 3.3 copy-start
  26.7 3.4 copy-start.1
  30.1 51.0 %copy-start.2 = (f32[16400,128]{1,0:T(8,128)S(1)}, f32[16400,128]{1,0:T(8,128)}, u32[]{:S(2)}) copy-start(f32[16400,128]{1,0:T(8,128)} %copy-done) | copy-start | bytes 25190404
Sparse Core Ops, SparseCore 0:
  11.0 3.1 sort.19.cloned.1.call-done
  (1 shorter events, 0.0 us)

commit v3 on v2

--- a/solution.py
+++ b/solution.py
@@ -13,9 +13,9 @@
 CHUNK = 256
 PACK_ROWS = 1024
 QUERY_GROUP, SCORE_GROUP, HEAD_GROUP, ROWS_GROUP, TAIL_GROUP = 2, 2, 2, 4, 2
-TAILS_FIRST = 2
+TAILS_FIRST, TAILS_SECOND = 0, 2
 AHEAD = 2
-HEAD_SENDS = {0: (0, 2, 3, 4, 5, 7, 8), **{k: (4, 8, 8, 8, 8, 8, 8) for k in (1, 2, 3, 6, 7, 8)}}
+HEAD_SENDS = {0: (0, 2, 3, 4, 5, 7, 8), **{k: (2, 8, 8, 8, 8, 8, 8) for k in (1, 2, 3, 6, 7, 8)}}
 F32, BF16, I32 = jnp.float32, jnp.bfloat16, jnp.int32
 MESH = pl.DeviceIdType.MESH
 VMEM = pltpu.VMEM
@@ -150,12 +150,13 @@
 UNROLL_SCATTER = 16
 UNROLL_GATHER = 64
 UNROLL_NEG = 8
-GATHER_GROUP = 4
+CONVERT_GROUP = 4
 UPDATE_ROWS = 512
 
 
-def table_kernel(dims, update_rows, gather_next, *refs):
+def table_kernel(dims, old, new, *refs):
     refs = list(refs)
+    update_rows, gather_next = old is not None, new is not None
 
     def take(n):
         taken = refs[:n]
@@ -179,52 +180,35 @@
     sem, = take(1)
     if update_rows:
         acc_a, acc_b = take(2)
-    if gather_next:
-        stage, = take(1)
-    copies = [pltpu.make_async_copy(src, dst, sem.at[k]) for k, (src, dst) in enumerate(zip(sources, lists))]
+    steps = [old] * 4 * (old is not None) + [new] * 4 * (new is not None)
+    copies = [pltpu.make_async_copy(src.at[pl.ds(step * dst.shape[0], dst.shape[0])], dst, sem.at[k])
+              for k, (src, dst, step) in enumerate(zip(sources, lists, steps))]
     for copy in copies:
         copy.start()
     if update_rows:
         head_i, tail_i, neg_i, src_i = lists[:4]
-        table_update(dims, copies, old_count, head_i, tail_i, neg_i, src_i, head_g, tail_g, neg_g, table_in, table, acc_a, acc_b)
+        table_update(dims, copies, old_count[old], head_i, tail_i, neg_i, src_i, head_g, tail_g, neg_g, table_in, table, acc_a, acc_b)
     else:
         for copy in copies:
             copy.wait()
     if gather_next:
         head_i, tail_i, neg_i, src_i = lists[-4:]
-        sel = compact_sel(dims, 2 * LANES)
-
-        def staged(c):
-            base = pl.multiple_of(c * 2 * CHUNK, 2 * CHUNK)
-            re = stage[pl.ds(base, CHUNK, stride=2), :]
-            im = stage[pl.ds(base + 1, CHUNK, stride=2), :]
-            return jnp.concatenate([re.astype(BF16), im.astype(BF16)], axis=1)
-
         for ids, out in ((tail_i, tail_out), (head_i, head_out)):
             def gather(c, _):
                 for u in range(UNROLL_GATHER):
                     k = c * UNROLL_GATHER + u
-                    stage[pair(k), :] = table[at(ids, k), :]
+                    out[pair(k), :] = table[at(ids, k), :]
                 return 0
             lax.fori_loop(0, edges // UNROLL_GATHER, gather, 0)
 
-            def convert(c, _):
-                for u in range(GATHER_GROUP):
-                    k = c * GATHER_GROUP + u
-                    out[k] = nt_dot(sel[:dims.dc], staged(k)).astype(BF16)
-                return 0
-            lax.fori_loop(0, dims.nch // GATHER_GROUP, convert, 0)
-
-        stage[pl.ds(0, 2 * negp), :] = jnp.zeros((2 * negp, LANES), F32)
+        neg_out[...] = jnp.zeros_like(neg_out)
 
         def gather_neg(c, _):
             rows = [table[at(neg_i, c * UNROLL_NEG + u), :] for u in range(UNROLL_NEG)]
             for u in range(UNROLL_NEG):
-                stage[at(src_i, c * UNROLL_NEG + u), :] = rows[u]
+                neg_out[at(src_i, c * UNROLL_NEG + u), :] = rows[u]
             return 0
-        lax.fori_loop(0, (new_count[0] + UNROLL_NEG - 1) // UNROLL_NEG, gather_neg, 0)
-        for c in range(negp // CHUNK):
-            neg_out[pl.ds(c * CHUNK, CHUNK), :] = nt_dot(staged(c), sel).astype(BF16)
+        lax.fori_loop(0, (new_count[new] + UNROLL_NEG - 1) // UNROLL_NEG, gather_neg, 0)
 
 
 def table_update(dims, copies, count, head_i, tail_i, neg_i, src_i, head_g, tail_g, neg_g, table_in, table, acc_a, acc_b):
@@ -263,7 +247,7 @@
             acc_a[h, :] = new_a
             acc_b[t, :] = new_b
         return 0
-    lax.fori_loop(0, (count[0] + UNROLL_NEG - 1) // UNROLL_NEG, scatter_neg, 0)
+    lax.fori_loop(0, (count + UNROLL_NEG - 1) // UNROLL_NEG, scatter_neg, 0)
 
     lane = iota((UPDATE_ROWS, LANES), 1)
 
@@ -293,14 +277,14 @@
     return pl.ds(pl.multiple_of(ref[k], 2), 2)
 
 
-def table_step(dims, old, new, grads, table):
+def table_step(dims, old, new, old_lists, new_lists, grads, table):
     vm = pl.BlockSpec(memory_space=VMEM)
     smem = pl.BlockSpec(memory_space=pltpu.SMEM)
     anys = pl.BlockSpec(memory_space=pl.ANY)
     sizes = (dims.edges, dims.edges, dims.negp, dims.negp)
     operands, in_specs, outs, scratch, aliases = [], [], [], [], {}
-    for lists in (old, new):
-        if lists is not None:
+    for step, lists in ((old, old_lists), (new, new_lists)):
+        if step is not None:
             operands += lists
             in_specs += [smem] + [anys] * 4
             scratch += [pltpu.SMEM((n,), I32) for n in sizes]
@@ -314,26 +298,23 @@
     operands.append(table)
     in_specs.append(vm)
     if new is not None:
-        outs += [jax.ShapeDtypeStruct((dims.nch, dims.dc, CHUNK), BF16)] * 2
-        outs.append(jax.ShapeDtypeStruct((dims.negp, 2 * LANES), BF16))
-        scratch.append(VMEM((2 * dims.edges, LANES), F32))
+        outs += [jax.ShapeDtypeStruct((2 * n, LANES), F32) for n in (dims.edges, dims.edges, dims.negp)]
     return pl.pallas_call(
-        functools.partial(table_kernel, dims, old is not None, new is not None),
+        functools.partial(table_kernel, dims, old, new),
         out_shape=outs, in_specs=in_specs, out_specs=[vm] * len(outs), scratch_shapes=scratch,
         input_output_aliases=aliases, name='table',
         compiler_params=pltpu.CompilerParams(vmem_limit_bytes=24 << 20))(*operands)
 
 
 def bucket_kernel(dims, s, *refs):
-    (head, tail, neg, rel_t, rel_state, rel_ids, rel_ids_p, weight), refs = refs[:8], refs[8:]
+    (head_rows_in, tail_rows_in, neg_rows_in, rel_t, rel_state, rel_ids, rel_ids_p, weight), refs = refs[:8], refs[8:]
     if s == 0:
         (tail_x, rel_x), refs = refs[:2], refs[2:]
     (head_g, tail_g, neg_g, rel_t_out, rel_state_out, loss), refs = refs[:6], refs[6:]
     if s == 0:
-        rel_x_out, tail_x_out = refs[0], refs[1:dims.rounds]
-        refs = refs[dims.rounds:]
+        (rel_x_out, tail_x_out), refs = refs[:2], refs[2:]
         (x_ss, x_rs), refs = refs[:2], refs[2:]
-    (tail_r, head_r, dp_s, dp_r, splits, q_all, r_all, qb, ex, top_s, sum_s, neg_p, neg_half, neg_buf, neg_acc, neg_all, neg_t,
+    (head, tail, neg, tail_r, head_r, dp_s, dp_r, splits, q_all, r_all, qb, ex, top_s, sum_s, neg_p, neg_half, neg_buf, neg_acc, neg_all, neg_t,
      acc_rel, acc_neg, head_c, x_ar, p_ar, half_ar, buf_ar, acc_ar, o_ar,
      tail_ss, tail_rs, head_ss, head_rs, one_s, one_r, rs_s, rs_r, ag_s, ag_r, rs2_s, rs2_r, ag2_s, ag2_r) = refs
     ent, chips, hp, dc, nch = dims.ent, dims.chips, dims.hp, dims.dc, dims.nch
@@ -404,6 +385,24 @@
     acc_rel[...] = jnp.zeros_like(acc_rel)
     acc_neg[...] = jnp.zeros_like(acc_neg)
     loss[...] = jnp.zeros_like(loss)
+    sel = compact_sel(dims, 2 * LANES)
+
+    def edge_rows(ref, c):
+        base = pl.multiple_of(c * 2 * CHUNK, 2 * CHUNK)
+        re = ref[pl.ds(base, CHUNK, stride=2), :]
+        im = ref[pl.ds(base + 1, CHUNK, stride=2), :]
+        return jnp.concatenate([re.astype(BF16), im.astype(BF16)], axis=1)
+
+    def convert(ref, out):
+        def group(cs):
+            for c in cs:
+                out[c] = nt_dot(sel[:dc], edge_rows(ref, c)).astype(BF16)
+        chunks(CONVERT_GROUP, group)
+    per = CHUNK // dims.negc
+    for c in range(dims.negp // CHUNK):
+        neg[c * per // chips, pl.ds(c * per % chips, per)] = nt_dot(edge_rows(neg_rows_in, c), sel).astype(BF16).reshape(per, dims.negc, 2 * LANES)
+    convert(tail_rows_in, tail)
+
     pl.semaphore_wait(barrier, chips + others)
 
     def tail_copy(c):
@@ -435,7 +434,6 @@
     else:
         tail_in, head_in, dp_in = tail, head, dp_s
 
-    first = GATHER_GROUP
     send_tails(0, TAILS_FIRST)
     neg_pair = remote(neg.at[1 - core], neg_p, one_s.at[0], one_r.at[0], partner)
     neg_pair.start()
@@ -445,7 +443,8 @@
     def rs_neg(k):
         return remote(neg_half.at[lax.rem(chip + k, chips)], neg_buf.at[k], rs_s.at[k], rs_r.at[k], peer(k))
     loop(1, chips, lambda k: rs_neg(k).start())
-    send_tails(TAILS_FIRST, first)
+    send_tails(TAILS_FIRST, TAILS_SECOND)
+    convert(head_rows_in, head)
     send_heads_at(0)
     neg_acc[...] = neg_half[chip]
 
@@ -457,7 +456,7 @@
     def ag_neg(k):
         return remote(neg_acc, neg_all.at[core, chip], ag_s.at[k], ag_r.at[k], peer(k))
     loop(1, chips, lambda k: ag_neg(k).start())
-    send_tails(first, nch)
+    send_tails(TAILS_SECOND, nch)
     send_heads_at(1)
     if s == 0:
         def rel_copy(k):
@@ -465,11 +464,13 @@
             return remote(rel_x.at[rows], rel_x_out.at[rows], x_ss.at[0, k], x_rs.at[0, k], lax.rem(me + k, ent))
 
         def id_copy(k):
-            return remote(tail_x.at[pl.ds(k * dims.edges, dims.edges)], tail_x_out[k - 1], x_ss.at[1, k], x_rs.at[1, k], lax.rem(me + k, ent))
+            rows = pl.ds(k * dims.edges, dims.edges)
+            return remote(tail_x.at[rows], tail_x_out.at[rows], x_ss.at[1, k], x_rs.at[1, k], lax.rem(me + k, ent))
         loop(1, dims.rounds, lambda k: rel_copy(k).start())
         for k in range(1, dims.rounds):
             id_copy(k).start()
         rel_x_out[pl.ds(0, nch), :] = rel_x[pl.ds(0, nch), :]
+        tail_x_out[pl.ds(0, dims.edges)] = tail_x[pl.ds(0, dims.edges)]
     for i, part in enumerate(split3(rel_t[...])):
         splits[pl.ds(i * dc, dc), :] = part
     chunks(QUERY_GROUP, rel_query)
@@ -664,7 +665,7 @@
     outs = [sds((2 * d.edges, LANES), F32), sds((2 * d.edges, LANES), F32), sds((2 * d.negp, LANES), F32),
             sds((d.dc, d.relp), F32), sds((8, d.relp), F32), sds((8, CHUNK), F32)]
     if extra:
-        outs += [sds(extra[1].shape, I32)] + [sds((d.edges,), I32)] * (d.rounds - 1)
+        outs += [sds(extra[1].shape, I32), sds(extra[0].shape, I32)]
     tail, head, neg = rows_in
     rows = VMEM((d.nch, d.dc, CHUNK), BF16)
     wide = VMEM((d.nch, d.dc, CHUNK), F32)
@@ -672,7 +673,7 @@
     neg_part = VMEM((d.chips, d.negc, 2 * LANES), BF16)
     ar_part = VMEM((d.chips, d.tpd, 8, LANES), F32)
     scratch = [dma((2, d.rounds))] * 2 if extra else []
-    scratch += [rows, rows, line, line,
+    scratch += [rows, rows, VMEM((2, d.chips, d.negc, 2 * LANES), BF16), rows, rows, line, line,
                 VMEM((3 * d.dc, d.relp), BF16), wide, wide, VMEM((d.nch, 2 * LANES, CHUNK), BF16),
                 VMEM((d.nch, d.negp, CHUNK), F32), line, line,
                 neg_part, neg_part, neg_part, VMEM((d.negc, 2 * LANES), BF16),
@@ -687,7 +688,7 @@
         in_specs=[vm] * (8 + len(extra)), out_specs=[vm] * len(outs),
         scratch_shapes=scratch, name=f'bucket_{s}',
         compiler_params=pltpu.CompilerParams(collective_id=s, has_side_effects=True, vmem_limit_bytes=36 << 20),
-    )(head, tail, neg.reshape(2, d.chips, d.negc, 2 * LANES), rel_t, rel_state, rel_ids, rel_ids_p, weight, *extra)
+    )(head, tail, neg, rel_t, rel_state, rel_ids, rel_ids_p, weight, *extra)
 
 
 def solution(mesh):
@@ -717,28 +718,24 @@
         counts = jnp.sum(owned.astype(I32), axis=1)
         rel_ids = rel_idx[0].reshape(d.rounds * d.nch, CHUNK)
         weight = edge_mask[0].astype(F32).reshape(d.rounds * d.nch, CHUNK)
-        def per_round(x):
-            size = x.size // d.rounds
-            return [x.reshape(-1)[k * size:(k + 1) * size] for k in range(d.rounds)]
-        heads, counts, neg_rows, neg_src = (per_round(x) for x in (head_ids, counts, neg_rows, neg_src))
-        first_tails = own_tail_ids[:d.edges]
-        table, heads, counts, neg_rows, neg_src, first_tails = lax.optimization_barrier((table, heads, counts, neg_rows, neg_src, first_tails))
-
-        def lists(k):
-            return [counts[k], heads[k], tails[k], neg_rows[k], neg_src[k]]
-        tails = [first_tails]
-        rows_in = table_step(d, None, lists(0), None, table)
+        neg_rows, neg_src = neg_rows.reshape(-1), neg_src.reshape(-1)
+        table, head_ids, counts, neg_rows, neg_src, own_tail_ids = lax.optimization_barrier(
+            (table, head_ids, counts, neg_rows, neg_src, own_tail_ids))
+
+        own_lists = [counts, head_ids, own_tail_ids, neg_rows, neg_src]
+        rows_in = table_step(d, None, 0, None, own_lists, None, table)
         losses = []
         for s in range(d.rounds):
             if s == 0:
                 res = bucket_step(d, s, rows_in, rel_t, rel_state, rel_ids, rel_ids, weight, (own_tail_ids, rel_ids))
-                rel_ids_p = res[6]
-                tails += res[7:]
+                rel_ids_p, tail_ids = res[6:]
+                lists = [counts, head_ids, tail_ids, neg_rows, neg_src]
             else:
                 res = bucket_step(d, s, rows_in, rel_t, rel_state, rel_ids, rel_ids_p, weight, ())
             hg, tg, ng, rel_t, rel_state, loss = res[:6]
             losses.append(loss)
-            table, *rows_in = table_step(d, lists(s), lists(s + 1) if s + 1 < d.rounds else None, (hg, tg, ng), table)
+            new = s + 1 if s + 1 < d.rounds else None
+            table, *rows_in = table_step(d, s, new, own_lists if s == 0 else lists, lists, (hg, tg, ng), table)
         loss = jnp.sum(jnp.stack(losses), axis=(1, 2)) / d.edges
         emb, ada = unpack(d, table)
         rel_out = rel_t.T.reshape(d.relp, 2, d.hp)[:d.num_rel, :, :d.half].reshape(d.num_rel, d.dim)

time: 1260 us -> 1220 us (0.968)
  Pallas kernels: 1210 us -> 1170 us
    pallas_call x17, Pallas kernels: 292 us -> 255 us  [table_step(): pl.pallas_call(functools.partial(table_kernel, dims, old, new), out_shape...]
where the time goes in v3:
time: 1220 us; the launch traced here: 1200 us
  Pallas kernels  1170 us (96%)
  between operations  15 us (1%)
  local copies, waits for them, and re-layouts  12.8 us (1%)
    pallas_call x16, Pallas kernels, bucket_step(): pl.pallas_call(functools.partial(bucket_kernel, d, s), out_shape=outs, in...  905 us
    pallas_call x17, Pallas kernels, table_step(): pl.pallas_call(functools.partial(table_kernel, dims, old, new), out_shape...  255 us

profile of v3, /device:TPU:97, one launch (start us, length us, event | category | flops | bytes accessed | tf_op | source)
XLA Modules:
  0.0 1203.3 jit_solution(4350247294678778546)
XLA Ops:
  7.2 0.0 copy-start.5
  7.2 0.0 copy-start.6
  7.2 0.0 copy-start.4
  7.2 0.1 sort.17.cloned.1.call-start
  7.3 0.9 select_multiply_fusion
  8.2 0.6 fusion.3
  8.8 0.1 sort.17.cloned.1.call-update
  8.9 0.9 multiply_bitcast_fusion.1
  9.8 0.9 multiply_bitcast_fusion
  10.7 0.9 reshape_squeeze.3.refs_5_.refs_6_.refs_9_
  11.7 0.9 convert_element_type.13
  12.7 0.0 copy-done.5
  12.7 0.0 copy-done.6
  12.8 0.0 copy-done.4
  12.8 0.0 copy-start.3
  12.8 2.9 copy-done.3
  15.6 4.2 pack.1.refs_5_.refs_13_
  19.8 0.0 copy-start
  19.8 3.3 copy-done
  23.1 0.0 sort.17.cloned.1.call-done
  23.1 0.8 copy.31
  23.9 0.8 fusion.2
  24.7 0.0 copy-start.1
  24.7 3.4 copy-done.1
  28.0 0.0 copy-start.2
  28.0 5.1 table.17
  33.1 44.0 %bucket_0.1 = (f32[4096,128]{1,0:T(8,128)S(1)}, f32[4096,128]{1,0:T(8,128)S(1)}, f32[1024,128]{1,0:T(8,128)S(1)}, f32[208,256]{1,0:T(8,128)S(1)}, f32[8,256]{1,0...) custom-call(f32[4096,128]{1,0:T(8,128)S(1)} %get-tuple-element.184.refs_0_, ...), custom_call_target="tpu_custom_call" | custom-call | tf_op jit(solution)/shard_map/bucket_0/pallas_call | solution.py:686
  77.2 0.0 copy-done.2
  77.2 15.7 %table.18 = (f32[16400,128]{1,0:T(8,128)S(1)}, f32[4096,128]{1,0:T(8,128)S(1)}, f32[4096,128]{1,0:T(8,128)S(1)}, f32[1024,128]{1,0:T(8,128)S(1)}) custom-call(s32[16]{0:T(128)S(1)} %get-tuple-element.178.refs_0_.refs_5_, s32[32768]{0:T(1024)S(1)} %bitcast.62, s32[32768]{0:T(1024)S(1)} %bitcast.160, ...), custom_call_target="tpu_custom_call", output_to_operand_aliasing={{0}: (13, {})} | custom-call | tf_op jit(solution)/shard_map/table/pallas_call | solution.py:302
  92.9 37.8 %bucket_1.1 = (f32[4096,128]{1,0:T(8,128)S(1)}, f32[4096,128]{1,0:T(8,128)S(1)}, f32[1024,128]{1,0:T(8,128)S(1)}, f32[208,256]{1,0:T(8,128)S(1)}, f32[8,256]{1,0:T(8,128)S(1)}, /*index=5*/f32[8,256]{1,0:T(8,128)S(1)}) custom-call(f32[4096,128]{1,0:T(8,128)S(1)} %get-tuple-element.191.refs_0_, f32[4096,128]{1,0:T(8,128)S(1)} %get-tuple-element.192.refs_1_, ...), custom_call_target="tpu_custom_call" | custom-call | tf_op jit(solution)/shard_map/bucket_1/pallas_call | solution.py:686
  130.8 16.2 %table.19 = (f32[16400,128]{1,0:T(8,128)S(1)}, f32[4096,128]{1,0:T(8,128)S(1)}, f32[4096,128]{1,0:T(8,128)S(1)}, f32[1024,128]{1,0:T(8,128)S(1)}) custom-call(s32[16]{0:T(128)S(1)} %get-tuple-element.178.refs_0_.refs_5_, s32[32768]{0:T(1024)S(1)} %bitcast.64, s32[32768]{0:T(1024)S(1)} %get-tuple-element.187.refs_7_.refs_2_, ...), custom_call_target="tpu_custom_call", output_to_operand_aliasing={{0}: (13, {})} | custom-call | tf_op jit(solution)/shard_map/table/pallas_call | solution.py:302
  147.0 46.9 %bucket_2.1 = (f32[4096,128]{1,0:T(8,128)S(1)}, f32[4096,128]{1,0:T(8,128)S(1)}, f32[1024,128]{1,0:T(8,128)S(1)}, f32[208,256]{1,0:T(8,128)S(1)}, f32[8,256]{1,0:T(8,128)S(1)}, /*index=5*/f32[8,256]{1,0:T(8,128)S(1)}) custom-call(f32[4096,128]{1,0:T(8,128)S(1)} %get-tuple-element.201.refs_0_, f32[4096,128]{1,0:T(8,128)S(1)} %get-tuple-element.202.refs_1_, ...), custom_call_target="tpu_custom_call" | custom-call | tf_op jit(solution)/shard_map/bucket_2/pallas_call | solution.py:686
  193.8 15.7 %table.20 = (f32[16400,128]{1,0:T(8,128)S(1)}, f32[4096,128]{1,0:T(8,128)S(1)}, f32[4096,128]{1,0:T(8,128)S(1)}, f32[1024,128]{1,0:T(8,128)S(1)}) custom-call(s32[16]{0:T(128)S(1)} %get-tuple-element.178.refs_0_.refs_5_, s32[32768]{0:T(1024)S(1)} %bitcast.66, s32[32768]{0:T(1024)S(1)} %get-tuple-element.187.refs_7_.refs_2_, ...), custom_call_target="tpu_custom_call", output_to_operand_aliasing={{0}: (13, {})} | custom-call | tf_op jit(solution)/shard_map/table/pallas_call | solution.py:302
  209.6 55.7 %bucket_3.1 = (f32[4096,128]{1,0:T(8,128)S(1)}, f32[4096,128]{1,0:T(8,128)S(1)}, f32[1024,128]{1,0:T(8,128)S(1)}, f32[208,256]{1,0:T(8,128)S(1)}, f32[8,256]{1,0:T(8,128)S(1)}, /*index=5*/f32[8,256]{1,0:T(8,128)S(1)}) custom-call(f32[4096,128]{1,0:T(8,128)S(1)} %get-tuple-element.210.refs_0_, f32[4096,128]{1,0:T(8,128)S(1)} %get-tuple-element.211.refs_1_, ...), custom_call_target="tpu_custom_call" | custom-call | tf_op jit(solution)/shard_map/bucket_3/pallas_call | solution.py:686
  265.3 15.9 %table.21 = (f32[16400,128]{1,0:T(8,128)S(1)}, f32[4096,128]{1,0:T(8,128)S(1)}, f32[4096,128]{1,0:T(8,128)S(1)}, f32[1024,128]{1,0:T(8,128)S(1)}) custom-call(s32[16]{0:T(128)S(1)} %get-tuple-element.178.refs_0_.refs_5_, s32[32768]{0:T(1024)S(1)} %bitcast.68, s32[32768]{0:T(1024)S(1)} %get-tuple-element.187.refs_7_.refs_2_, ...), custom_call_target="tpu_custom_call", output_to_operand_aliasing={{0}: (13, {})} | custom-call | tf_op jit(solution)/shard_map/table/pallas_call | solution.py:302
  281.2 63.4 %bucket_4.1 = (f32[4096,128]{1,0:T(8,128)S(1)}, f32[4096,128]{1,0:T(8,128)S(1)}, f32[1024,128]{1,0:T(8,128)S(1)}, f32[208,256]{1,0:T(8,128)S(1)}, f32[8,256]{1,0:T(8,128)S(1)}, /*index=5*/f32[8,256]{1,0:T(8,128)S(1)}) custom-call(f32[4096,128]{1,0:T(8,128)S(1)} %get-tuple-element.219.refs_0_, f32[4096,128]{1,0:T(8,128)S(1)} %get-tuple-element.220.refs_1_, ...), custom_call_target="tpu_custom_call" | custom-call | tf_op jit(solution)/shard_map/bucket_4/pallas_call | solution.py:686
  344.7 15.7 %table.22 = (f32[16400,128]{1,0:T(8,128)S(1)}, f32[4096,128]{1,0:T(8,128)S(1)}, f32[4096,128]{1,0:T(8,128)S(1)}, f32[1024,128]{1,0:T(8,128)S(1)}) custom-call(s32[16]{0:T(128)S(1)} %get-tuple-element.178.refs_0_.refs_5_, s32[32768]{0:T(1024)S(1)} %bitcast.70, s32[32768]{0:T(1024)S(1)} %get-tuple-element.187.refs_7_.refs_2_, ...), custom_call_target="tpu_custom_call", output_to_operand_aliasing={{0}: (13, {})} | custom-call | tf_op jit(solution)/shard_map/table/pallas_call | solution.py:302
  360.4 63.7 %bucket_5.1 = (f32[4096,128]{1,0:T(8,128)S(1)}, f32[4096,128]{1,0:T(8,128)S(1)}, f32[1024,128]{1,0:T(8,128)S(1)}, f32[208,256]{1,0:T(8,128)S(1)}, f32[8,256]{1,0:T(8,128)S(1)}, /*index=5*/f32[8,256]{1,0:T(8,128)S(1)}) custom-call(f32[4096,128]{1,0:T(8,128)S(1)} %get-tuple-element.228.refs_0_, f32[4096,128]{1,0:T(8,128)S(1)} %get-tuple-element.229.refs_1_, ...), custom_call_target="tpu_custom_call" | custom-call | tf_op jit(solution)/shard_map/bucket_5/pallas_call | solution.py:686
  424.1 15.9 %table.23 = (f32[16400,128]{1,0:T(8,128)S(1)}, f32[4096,128]{1,0:T(8,128)S(1)}, f32[4096,128]{1,0:T(8,128)S(1)}, f32[1024,128]{1,0:T(8,128)S(1)}) custom-call(s32[16]{0:T(128)S(1)} %get-tuple-element.178.refs_0_.refs_5_, s32[32768]{0:T(1024)S(1)} %bitcast.72, s32[32768]{0:T(1024)S(1)} %get-tuple-element.187.refs_7_.refs_2_, ...), custom_call_target="tpu_custom_call", output_to_operand_aliasing={{0}: (13, {})} | custom-call | tf_op jit(solution)/shard_map/table/pallas_call | solution.py:302
  440.0 50.8 %bucket_6.1 = (f32[4096,128]{1,0:T(8,128)S(1)}, f32[4096,128]{1,0:T(8,128)S(1)}, f32[1024,128]{1,0:T(8,128)S(1)}, f32[208,256]{1,0:T(8,128)S(1)}, f32[8,256]{1,0:T(8,128)S(1)}, /*index=5*/f32[8,256]{1,0:T(8,128)S(1)}) custom-call(f32[4096,128]{1,0:T(8,128)S(1)} %get-tuple-element.237.refs_0_, f32[4096,128]{1,0:T(8,128)S(1)} %get-tuple-element.238.refs_1_, ...), custom_call_target="tpu_custom_call" | custom-call | tf_op jit(solution)/shard_map/bucket_6/pallas_call | solution.py:686
  490.8 15.7 %table.24 = (f32[16400,128]{1,0:T(8,128)S(1)}, f32[4096,128]{1,0:T(8,128)S(1)}, f32[4096,128]{1,0:T(8,128)S(1)}, f32[1024,128]{1,0:T(8,128)S(1)}) custom-call(s32[16]{0:T(128)S(1)} %get-tuple-element.178.refs_0_.refs_5_, s32[32768]{0:T(1024)S(1)} %bitcast.74, s32[32768]{0:T(1024)S(1)} %get-tuple-element.187.refs_7_.refs_2_, ...), custom_call_target="tpu_custom_call", output_to_operand_aliasing={{0}: (13, {})} | custom-call | tf_op jit(solution)/shard_map/table/pallas_call | solution.py:302
  506.5 44.7 %bucket_7.1 = (f32[4096,128]{1,0:T(8,128)S(1)}, f32[4096,128]{1,0:T(8,128)S(1)}, f32[1024,128]{1,0:T(8,128)S(1)}, f32[208,256]{1,0:T(8,128)S(1)}, f32[8,256]{1,0:T(8,128)S(1)}, /*index=5*/f32[8,256]{1,0:T(8,128)S(1)}) custom-call(f32[4096,128]{1,0:T(8,128)S(1)} %get-tuple-element.246.refs_0_, f32[4096,128]{1,0:T(8,128)S(1)} %get-tuple-element.247.refs_1_, ...), custom_call_target="tpu_custom_call" | custom-call | tf_op jit(solution)/shard_map/bucket_7/pallas_call | solution.py:686
  551.2 16.1 %table.25 = (f32[16400,128]{1,0:T(8,128)S(1)}, f32[4096,128]{1,0:T(8,128)S(1)}, f32[4096,128]{1,0:T(8,128)S(1)}, f32[1024,128]{1,0:T(8,128)S(1)}) custom-call(s32[16]{0:T(128)S(1)} %get-tuple-element.178.refs_0_.refs_5_, s32[32768]{0:T(1024)S(1)} %bitcast.76, s32[32768]{0:T(1024)S(1)} %get-tuple-element.187.refs_7_.refs_2_, ...), custom_call_target="tpu_custom_call", output_to_operand_aliasing={{0}: (13, {})} | custom-call | tf_op jit(solution)/shard_map/table/pallas_call | solution.py:302
  567.3 46.5 %bucket_8.1 = (f32[4096,128]{1,0:T(8,128)S(1)}, f32[4096,128]{1,0:T(8,128)S(1)}, f32[1024,128]{1,0:T(8,128)S(1)}, f32[208,256]{1,0:T(8,128)S(1)}, f32[8,256]{1,0:T(8,128)S(1)}, /*index=5*/f32[8,256]{1,0:T(8,128)S(1)}) custom-call(f32[4096,128]{1,0:T(8,128)S(1)} %get-tuple-element.255.refs_0_, f32[4096,128]{1,0:T(8,128)S(1)} %get-tuple-element.256.refs_1_, ...), custom_call_target="tpu_custom_call" | custom-call | tf_op jit(solution)/shard_map/bucket_8/pallas_call | solution.py:686
  613.8 15.7 %table.26 = (f32[16400,128]{1,0:T(8,128)S(1)}, f32[4096,128]{1,0:T(8,128)S(1)}, f32[4096,128]{1,0:T(8,128)S(1)}, f32[1024,128]{1,0:T(8,128)S(1)}) custom-call(s32[16]{0:T(128)S(1)} %get-tuple-element.178.refs_0_.refs_5_, s32[32768]{0:T(1024)S(1)} %bitcast.78, s32[32768]{0:T(1024)S(1)} %get-tuple-element.187.refs_7_.refs_2_, ...), custom_call_target="tpu_custom_call", output_to_operand_aliasing={{0}: (13, {})} | custom-call | tf_op jit(solution)/shard_map/table/pallas_call | solution.py:302
  629.6 55.4 %bucket_9.1 = (f32[4096,128]{1,0:T(8,128)S(1)}, f32[4096,128]{1,0:T(8,128)S(1)}, f32[1024,128]{1,0:T(8,128)S(1)}, f32[208,256]{1,0:T(8,128)S(1)}, f32[8,256]{1,0:T(8,128)S(1)}, /*index=5*/f32[8,256]{1,0:T(8,128)S(1)}) custom-call(f32[4096,128]{1,0:T(8,128)S(1)} %get-tuple-element.264.refs_0_, f32[4096,128]{1,0:T(8,128)S(1)} %get-tuple-element.265.refs_1_, ...), custom_call_target="tpu_custom_call" | custom-call | tf_op jit(solution)/shard_map/bucket_9/pallas_call | solution.py:686
  685.0 15.9 %table.27 = (f32[16400,128]{1,0:T(8,128)S(1)}, f32[4096,128]{1,0:T(8,128)S(1)}, f32[4096,128]{1,0:T(8,128)S(1)}, f32[1024,128]{1,0:T(8,128)S(1)}) custom-call(s32[16]{0:T(128)S(1)} %get-tuple-element.178.refs_0_.refs_5_, s32[32768]{0:T(1024)S(1)} %bitcast.80, s32[32768]{0:T(1024)S(1)} %get-tuple-element.187.refs_7_.refs_2_, ...), custom_call_target="tpu_custom_call", output_to_operand_aliasing={{0}: (13, {})} | custom-call | tf_op jit(solution)/shard_map/table/pallas_call | solution.py:302
  700.8 62.5 %bucket_10.1 = (f32[4096,128]{1,0:T(8,128)S(1)}, f32[4096,128]{1,0:T(8,128)S(1)}, f32[1024,128]{1,0:T(8,128)S(1)}, f32[208,256]{1,0:T(8,128)S(1)}, f32[8,256]{1,0:T(8,128)S(1)}, /*index=5*/f32[8,256]{1,0:T(8,128)S(1)}) custom-call(f32[4096,128]{1,0:T(8,128)S(1)} %get-tuple-element.273.refs_0_, f32[4096,128]{1,0:T(8,128)S(1)} %get-tuple-element.274.refs_1_, ...), custom_call_target="tpu_custom_call" | custom-call | tf_op jit(solution)/shard_map/bucket_10/pallas_call | solution.py:686
  763.3 15.7 %table.28 = (f32[16400,128]{1,0:T(8,128)S(1)}, f32[4096,128]{1,0:T(8,128)S(1)}, f32[4096,128]{1,0:T(8,128)S(1)}, f32[1024,128]{1,0:T(8,128)S(1)}) custom-call(s32[16]{0:T(128)S(1)} %get-tuple-element.178.refs_0_.refs_5_, s32[32768]{0:T(1024)S(1)} %bitcast.82, s32[32768]{0:T(1024)S(1)} %get-tuple-element.187.refs_7_.refs_2_, ...), custom_call_target="tpu_custom_call", output_to_operand_aliasing={{0}: (13, {})} | custom-call | tf_op jit(solution)/shard_map/table/pallas_call | solution.py:302
  779.1 66.3 %bucket_11.1 = (f32[4096,128]{1,0:T(8,128)S(1)}, f32[4096,128]{1,0:T(8,128)S(1)}, f32[1024,128]{1,0:T(8,128)S(1)}, f32[208,256]{1,0:T(8,128)S(1)}, f32[8,256]{1,0:T(8,128)S(1)}, /*index=5*/f32[8,256]{1,0:T(8,128)S(1)}) custom-call(f32[4096,128]{1,0:T(8,128)S(1)} %get-tuple-element.282.refs_0_, f32[4096,128]{1,0:T(8,128)S(1)} %get-tuple-element.283.refs_1_, ...), custom_call_target="tpu_custom_call" | custom-call | tf_op jit(solution)/shard_map/bucket_11/pallas_call | solution.py:686
  845.4 16.0 %table.29 = (f32[16400,128]{1,0:T(8,128)S(1)}, f32[4096,128]{1,0:T(8,128)S(1)}, f32[4096,128]{1,0:T(8,128)S(1)}, f32[1024,128]{1,0:T(8,128)S(1)}) custom-call(s32[16]{0:T(128)S(1)} %get-tuple-element.178.refs_0_.refs_5_, s32[32768]{0:T(1024)S(1)} %bitcast.84, s32[32768]{0:T(1024)S(1)} %get-tuple-element.187.refs_7_.refs_2_, ...), custom_call_target="tpu_custom_call", output_to_operand_aliasing={{0}: (13, {})} | custom-call | tf_op jit(solution)/shard_map/table/pallas_call | solution.py:302
  861.4 69.6 %bucket_12.1 = (f32[4096,128]{1,0:T(8,128)S(1)}, f32[4096,128]{1,0:T(8,128)S(1)}, f32[1024,128]{1,0:T(8,128)S(1)}, f32[208,256]{1,0:T(8,128)S(1)}, f32[8,256]{1,0:T(8,128)S(1)}, /*index=5*/f32[8,256]{1,0:T(8,128)S(1)}) custom-call(f32[4096,128]{1,0:T(8,128)S(1)} %get-tuple-element.291.refs_0_, f32[4096,128]{1,0:T(8,128)S(1)} %get-tuple-element.292.refs_1_, ...), custom_call_target="tpu_custom_call" | custom-call | tf_op jit(solution)/shard_map/bucket_12/pallas_call | solution.py:686
  931.0 15.7 %table.30 = (f32[16400,128]{1,0:T(8,128)S(1)}, f32[4096,128]{1,0:T(8,128)S(1)}, f32[4096,128]{1,0:T(8,128)S(1)}, f32[1024,128]{1,0:T(8,128)S(1)}) custom-call(s32[16]{0:T(128)S(1)} %get-tuple-element.178.refs_0_.refs_5_, s32[32768]{0:T(1024)S(1)} %bitcast.86, s32[32768]{0:T(1024)S(1)} %get-tuple-element.187.refs_7_.refs_2_, ...), custom_call_target="tpu_custom_call", output_to_operand_aliasing={{0}: (13, {})} | custom-call | tf_op jit(solution)/shard_map/table/pallas_call | solution.py:302
  946.8 67.7 %bucket_13.1 = (f32[4096,128]{1,0:T(8,128)S(1)}, f32[4096,128]{1,0:T(8,128)S(1)}, f32[1024,128]{1,0:T(8,128)S(1)}, f32[208,256]{1,0:T(8,128)S(1)}, f32[8,256]{1,0:T(8,128)S(1)}, /*index=5*/f32[8,256]{1,0:T(8,128)S(1)}) custom-call(f32[4096,128]{1,0:T(8,128)S(1)} %get-tuple-element.300.refs_0_, f32[4096,128]{1,0:T(8,128)S(1)} %get-tuple-element.301.refs_1_, ...), custom_call_target="tpu_custom_call" | custom-call | tf_op jit(solution)/shard_map/bucket_13/pallas_call | solution.py:686
  1014.5 16.0 %table.31 = (f32[16400,128]{1,0:T(8,128)S(1)}, f32[4096,128]{1,0:T(8,128)S(1)}, f32[4096,128]{1,0:T(8,128)S(1)}, f32[1024,128]{1,0:T(8,128)S(1)}) custom-call(s32[16]{0:T(128)S(1)} %get-tuple-element.178.refs_0_.refs_5_, s32[32768]{0:T(1024)S(1)} %bitcast.88, s32[32768]{0:T(1024)S(1)} %get-tuple-element.187.refs_7_.refs_2_, ...), custom_call_target="tpu_custom_call", output_to_operand_aliasing={{0}: (13, {})} | custom-call | tf_op jit(solution)/shard_map/table/pallas_call | solution.py:302
  1030.4 66.1 %bucket_14.1 = (f32[4096,128]{1,0:T(8,128)S(1)}, f32[4096,128]{1,0:T(8,128)S(1)}, f32[1024,128]{1,0:T(8,128)S(1)}, f32[208,256]{1,0:T(8,128)S(1)}, f32[8,256]{1,0:T(8,128)S(1)}, /*index=5*/f32[8,256]{1,0:T(8,128)S(1)}) custom-call(f32[4096,128]{1,0:T(8,128)S(1)} %get-tuple-element.309.refs_0_, f32[4096,128]{1,0:T(8,128)S(1)} %get-tuple-element.310.refs_1_, ...), custom_call_target="tpu_custom_call" | custom-call | tf_op jit(solution)/shard_map/bucket_14/pallas_call | solution.py:686
  1096.5 15.8 %table.32 = (f32[16400,128]{1,0:T(8,128)S(1)}, f32[4096,128]{1,0:T(8,128)S(1)}, f32[4096,128]{1,0:T(8,128)S(1)}, f32[1024,128]{1,0:T(8,128)S(1)}) custom-call(s32[16]{0:T(128)S(1)} %get-tuple-element.178.refs_0_.refs_5_, s32[32768]{0:T(1024)S(1)} %bitcast.90, s32[32768]{0:T(1024)S(1)} %get-tuple-element.187.refs_7_.refs_2_, ...), custom_call_target="tpu_custom_call", output_to_operand_aliasing={{0}: (13, {})} | custom-call | tf_op jit(solution)/shard_map/table/pallas_call | solution.py:302
  1112.3 64.3 %bucket_15.1 = (f32[4096,128]{1,0:T(8,128)S(1)}, f32[4096,128]{1,0:T(8,128)S(1)}, f32[1024,128]{1,0:T(8,128)S(1)}, f32[208,256]{1,0:T(8,128)S(1)}, f32[8,256]{1,0:T(8,128)S(1)}, /*index=5*/f32[8,256]{1,0:T(8,128)S(1)}) custom-call(f32[4096,128]{1,0:T(8,128)S(1)} %get-tuple-element.318.refs_0_, f32[4096,128]{1,0:T(8,128)S(1)} %get-tuple-element.319.refs_1_, ...), custom_call_target="tpu_custom_call" | custom-call | tf_op jit(solution)/shard_map/bucket_15/pallas_call | solution.py:686
  1176.6 12.0 table.33.t_ref
  1188.6 5.3 unpack.1
  1193.9 0.6 slice.7
  1194.6 0.2 reduce_sum.19
  1194.8 0.5 multiply_bitcast_fusion.2
  1195.3 0.7 reshape.61
  (25 shorter events, 0.2 us)
Async XLA Ops:
  7.2 5.5 copy-start.5
  7.2 5.5 copy-start.6
  7.2 5.6 copy-start.4
  7.2 15.9 %sort.17.cloned.1.call-start = ((), (), s32[]{:S(2)}) async-start(), calls=%async_computation | async-start | bytes 196640 | tf_op jit(solution)/shard_map/sort | solution.py:716
  12.8 2.9 copy-start.3
  19.8 3.3 copy-start
  24.7 3.4 copy-start.1
  28.0 49.1 %copy-start.2 = (f32[16400,128]{1,0:T(8,128)S(1)}, f32[16400,128]{1,0:T(8,128)}, u32[]{:S(2)}) copy-start(f32[16400,128]{1,0:T(8,128)} %copy-done) | copy-start | bytes 25190404
Sparse Core Ops, SparseCore 0:
  11.0 3.0 sort.19.cloned.1.call-done
  (1 shorter events, 0.0 us)

commit v4 on v3

--- a/solution.py
+++ b/solution.py
@@ -29,6 +29,9 @@
     def __init__(self, mesh, ent_emb, rel_emb, head_idx, neg_idx):
         self.ent = mesh.shape['ent']
         self.chips = self.ent // 2
+        side = max(round(self.chips ** 0.5), 1)
+        hops = lambda k: min(k % side, side - k % side) + min(k // side, side - k // side)
+        self.far_first = sorted(range(1, self.chips), key=lambda k: -hops(k))
         self.rows, self.dim = ent_emb.shape
         self.half = self.dim // 2
         self.hp = round_up(self.half, 8)
@@ -442,7 +445,8 @@
 
     def rs_neg(k):
         return remote(neg_half.at[lax.rem(chip + k, chips)], neg_buf.at[k], rs_s.at[k], rs_r.at[k], peer(k))
-    loop(1, chips, lambda k: rs_neg(k).start())
+    for k in dims.far_first:
+        rs_neg(k).start()
     send_tails(TAILS_FIRST, TAILS_SECOND)
     convert(head_rows_in, head)
     send_heads_at(0)
@@ -455,7 +459,8 @@
 
     def ag_neg(k):
         return remote(neg_acc, neg_all.at[core, chip], ag_s.at[k], ag_r.at[k], peer(k))
-    loop(1, chips, lambda k: ag_neg(k).start())
+    for k in dims.far_first:
+        ag_neg(k).start()
     send_tails(TAILS_SECOND, nch)
     send_heads_at(1)
     if s == 0:
@@ -587,7 +592,8 @@
 
     def rs_ar(k):
         return remote(half_ar.at[lax.rem(chip + k, chips)], buf_ar.at[k], rs2_s.at[k], rs2_r.at[k], peer(k))
-    loop(1, chips, lambda k: rs_ar(k).start())
+    for k in dims.far_first:
+        rs_ar(k).start()
     send_heads_at(3)
     chunks(ROWS_GROUP, head_rows)
     send_heads_at(4)
@@ -600,7 +606,8 @@
 
     def ag_ar(k):
         return remote(acc_ar, o_ar.at[core, chip], ag2_s.at[k], ag2_r.at[k], peer(k))
-    loop(1, chips, lambda k: ag_ar(k).start())
+    for k in dims.far_first:
+        ag_ar(k).start()
     send_heads_at(5)
     o_ar[core, chip] = acc_ar[...]
     def tail_gradients():

time: 1220 us -> 1220 us (level); the launches traced: 1200 us -> 1220 us
  Pallas kernels: 1170 us -> 1190 us
    pallas_call x16, Pallas kernels: 905 us -> 922 us  [bucket_step(): pl.pallas_call(functools.partial(bucket_kernel, d, s), out_shape=outs, in...]
where the time goes in v4:
time: 1220 us
  Pallas kernels  1190 us (98%)
  between operations  15 us (1%)
  local copies, waits for them, and re-layouts  12.8 us (1%)
    pallas_call x16, Pallas kernels, bucket_step(): pl.pallas_call(functools.partial(bucket_kernel, d, s), out_shape=outs, in...  922 us
    pallas_call x17, Pallas kernels, table_step(): pl.pallas_call(functools.partial(table_kernel, dims, old, new), out_shape...  255 us

profile of v4, /device:TPU:97, one launch (start us, length us, event | category | flops | bytes accessed | tf_op | source)
XLA Modules:
  0.0 1219.5 jit_solution(6693146429681076961)
XLA Ops:
  7.2 0.0 copy-start.5
  7.2 0.0 copy-start.6
  7.2 0.0 copy-start.4
  7.2 0.1 sort.17.cloned.1.call-start
  7.3 0.9 select_multiply_fusion
  8.2 0.6 fusion.3
  8.8 0.1 sort.17.cloned.1.call-update
  8.9 0.9 multiply_bitcast_fusion.1
  9.8 0.9 multiply_bitcast_fusion
  10.7 0.9 reshape_squeeze.3.refs_5_.refs_6_.refs_9_
  11.7 0.9 convert_element_type.13
  12.7 0.0 copy-done.5
  12.7 0.0 copy-done.6
  12.8 0.0 copy-done.4
  12.8 0.0 copy-start.3
  12.8 2.9 copy-done.3
  15.6 4.2 pack.1.refs_5_.refs_13_
  19.8 0.0 copy-start
  19.8 3.3 copy-done
  23.1 0.0 sort.17.cloned.1.call-done
  23.1 0.8 copy.31
  23.9 0.8 fusion.2
  24.7 0.0 copy-start.1
  24.7 3.4 copy-done.1
  28.0 0.0 copy-start.2
  28.0 5.1 table.17
  33.1 44.4 %bucket_0.1 = (f32[4096,128]{1,0:T(8,128)S(1)}, f32[4096,128]{1,0:T(8,128)S(1)}, f32[1024,128]{1,0:T(8,128)S(1)}, f32[208,256]{1,0:T(8,128)S(1)}, f32[8,256]{1,0...) custom-call(f32[4096,128]{1,0:T(8,128)S(1)} %get-tuple-element.184.refs_0_, ...), custom_call_target="tpu_custom_call" | custom-call | tf_op jit(solution)/shard_map/bucket_0/pallas_call | solution.py:693
  77.6 0.0 copy-done.2
  77.6 15.9 %table.18 = (f32[16400,128]{1,0:T(8,128)S(1)}, f32[4096,128]{1,0:T(8,128)S(1)}, f32[4096,128]{1,0:T(8,128)S(1)}, f32[1024,128]{1,0:T(8,128)S(1)}) custom-call(s32[16]{0:T(128)S(1)} %get-tuple-element.178.refs_0_.refs_5_, s32[32768]{0:T(1024)S(1)} %bitcast.62, s32[32768]{0:T(1024)S(1)} %bitcast.160, ...), custom_call_target="tpu_custom_call", output_to_operand_aliasing={{0}: (13, {})} | custom-call | tf_op jit(solution)/shard_map/table/pallas_call | solution.py:305
  93.5 43.4 %bucket_1.1 = (f32[4096,128]{1,0:T(8,128)S(1)}, f32[4096,128]{1,0:T(8,128)S(1)}, f32[1024,128]{1,0:T(8,128)S(1)}, f32[208,256]{1,0:T(8,128)S(1)}, f32[8,256]{1,0:T(8,128)S(1)}, /*index=5*/f32[8,256]{1,0:T(8,128)S(1)}) custom-call(f32[4096,128]{1,0:T(8,128)S(1)} %get-tuple-element.191.refs_0_, f32[4096,128]{1,0:T(8,128)S(1)} %get-tuple-element.192.refs_1_, ...), custom_call_target="tpu_custom_call" | custom-call | tf_op jit(solution)/shard_map/bucket_1/pallas_call | solution.py:693
  136.9 15.7 %table.19 = (f32[16400,128]{1,0:T(8,128)S(1)}, f32[4096,128]{1,0:T(8,128)S(1)}, f32[4096,128]{1,0:T(8,128)S(1)}, f32[1024,128]{1,0:T(8,128)S(1)}) custom-call(s32[16]{0:T(128)S(1)} %get-tuple-element.178.refs_0_.refs_5_, s32[32768]{0:T(1024)S(1)} %bitcast.64, s32[32768]{0:T(1024)S(1)} %get-tuple-element.187.refs_7_.refs_2_, ...), custom_call_target="tpu_custom_call", output_to_operand_aliasing={{0}: (13, {})} | custom-call | tf_op jit(solution)/shard_map/table/pallas_call | solution.py:305
  152.6 46.8 %bucket_2.1 = (f32[4096,128]{1,0:T(8,128)S(1)}, f32[4096,128]{1,0:T(8,128)S(1)}, f32[1024,128]{1,0:T(8,128)S(1)}, f32[208,256]{1,0:T(8,128)S(1)}, f32[8,256]{1,0:T(8,128)S(1)}, /*index=5*/f32[8,256]{1,0:T(8,128)S(1)}) custom-call(f32[4096,128]{1,0:T(8,128)S(1)} %get-tuple-element.201.refs_0_, f32[4096,128]{1,0:T(8,128)S(1)} %get-tuple-element.202.refs_1_, ...), custom_call_target="tpu_custom_call" | custom-call | tf_op jit(solution)/shard_map/bucket_2/pallas_call | solution.py:693
  199.4 16.1 %table.20 = (f32[16400,128]{1,0:T(8,128)S(1)}, f32[4096,128]{1,0:T(8,128)S(1)}, f32[4096,128]{1,0:T(8,128)S(1)}, f32[1024,128]{1,0:T(8,128)S(1)}) custom-call(s32[16]{0:T(128)S(1)} %get-tuple-element.178.refs_0_.refs_5_, s32[32768]{0:T(1024)S(1)} %bitcast.66, s32[32768]{0:T(1024)S(1)} %get-tuple-element.187.refs_7_.refs_2_, ...), custom_call_target="tpu_custom_call", output_to_operand_aliasing={{0}: (13, {})} | custom-call | tf_op jit(solution)/shard_map/table/pallas_call | solution.py:305
  215.6 54.0 %bucket_3.1 = (f32[4096,128]{1,0:T(8,128)S(1)}, f32[4096,128]{1,0:T(8,128)S(1)}, f32[1024,128]{1,0:T(8,128)S(1)}, f32[208,256]{1,0:T(8,128)S(1)}, f32[8,256]{1,0:T(8,128)S(1)}, /*index=5*/f32[8,256]{1,0:T(8,128)S(1)}) custom-call(f32[4096,128]{1,0:T(8,128)S(1)} %get-tuple-element.210.refs_0_, f32[4096,128]{1,0:T(8,128)S(1)} %get-tuple-element.211.refs_1_, ...), custom_call_target="tpu_custom_call" | custom-call | tf_op jit(solution)/shard_map/bucket_3/pallas_call | solution.py:693
  269.5 15.7 %table.21 = (f32[16400,128]{1,0:T(8,128)S(1)}, f32[4096,128]{1,0:T(8,128)S(1)}, f32[4096,128]{1,0:T(8,128)S(1)}, f32[1024,128]{1,0:T(8,128)S(1)}) custom-call(s32[16]{0:T(128)S(1)} %get-tuple-element.178.refs_0_.refs_5_, s32[32768]{0:T(1024)S(1)} %bitcast.68, s32[32768]{0:T(1024)S(1)} %get-tuple-element.187.refs_7_.refs_2_, ...), custom_call_target="tpu_custom_call", output_to_operand_aliasing={{0}: (13, {})} | custom-call | tf_op jit(solution)/shard_map/table/pallas_call | solution.py:305
  285.3 69.7 %bucket_4.1 = (f32[4096,128]{1,0:T(8,128)S(1)}, f32[4096,128]{1,0:T(8,128)S(1)}, f32[1024,128]{1,0:T(8,128)S(1)}, f32[208,256]{1,0:T(8,128)S(1)}, f32[8,256]{1,0:T(8,128)S(1)}, /*index=5*/f32[8,256]{1,0:T(8,128)S(1)}) custom-call(f32[4096,128]{1,0:T(8,128)S(1)} %get-tuple-element.219.refs_0_, f32[4096,128]{1,0:T(8,128)S(1)} %get-tuple-element.220.refs_1_, ...), custom_call_target="tpu_custom_call" | custom-call | tf_op jit(solution)/shard_map/bucket_4/pallas_call | solution.py:693
  355.0 15.9 %table.22 = (f32[16400,128]{1,0:T(8,128)S(1)}, f32[4096,128]{1,0:T(8,128)S(1)}, f32[4096,128]{1,0:T(8,128)S(1)}, f32[1024,128]{1,0:T(8,128)S(1)}) custom-call(s32[16]{0:T(128)S(1)} %get-tuple-element.178.refs_0_.refs_5_, s32[32768]{0:T(1024)S(1)} %bitcast.70, s32[32768]{0:T(1024)S(1)} %get-tuple-element.187.refs_7_.refs_2_, ...), custom_call_target="tpu_custom_call", output_to_operand_aliasing={{0}: (13, {})} | custom-call | tf_op jit(solution)/shard_map/table/pallas_call | solution.py:305
  370.9 62.9 %bucket_5.1 = (f32[4096,128]{1,0:T(8,128)S(1)}, f32[4096,128]{1,0:T(8,128)S(1)}, f32[1024,128]{1,0:T(8,128)S(1)}, f32[208,256]{1,0:T(8,128)S(1)}, f32[8,256]{1,0:T(8,128)S(1)}, /*index=5*/f32[8,256]{1,0:T(8,128)S(1)}) custom-call(f32[4096,128]{1,0:T(8,128)S(1)} %get-tuple-element.228.refs_0_, f32[4096,128]{1,0:T(8,128)S(1)} %get-tuple-element.229.refs_1_, ...), custom_call_target="tpu_custom_call" | custom-call | tf_op jit(solution)/shard_map/bucket_5/pallas_call | solution.py:693
  433.8 15.7 %table.23 = (f32[16400,128]{1,0:T(8,128)S(1)}, f32[4096,128]{1,0:T(8,128)S(1)}, f32[4096,128]{1,0:T(8,128)S(1)}, f32[1024,128]{1,0:T(8,128)S(1)}) custom-call(s32[16]{0:T(128)S(1)} %get-tuple-element.178.refs_0_.refs_5_, s32[32768]{0:T(1024)S(1)} %bitcast.72, s32[32768]{0:T(1024)S(1)} %get-tuple-element.187.refs_7_.refs_2_, ...), custom_call_target="tpu_custom_call", output_to_operand_aliasing={{0}: (13, {})} | custom-call | tf_op jit(solution)/shard_map/table/pallas_call | solution.py:305
  449.5 54.0 %bucket_6.1 = (f32[4096,128]{1,0:T(8,128)S(1)}, f32[4096,128]{1,0:T(8,128)S(1)}, f32[1024,128]{1,0:T(8,128)S(1)}, f32[208,256]{1,0:T(8,128)S(1)}, f32[8,256]{1,0:T(8,128)S(1)}, /*index=5*/f32[8,256]{1,0:T(8,128)S(1)}) custom-call(f32[4096,128]{1,0:T(8,128)S(1)} %get-tuple-element.237.refs_0_, f32[4096,128]{1,0:T(8,128)S(1)} %get-tuple-element.238.refs_1_, ...), custom_call_target="tpu_custom_call" | custom-call | tf_op jit(solution)/shard_map/bucket_6/pallas_call | solution.py:693
  503.6 15.9 %table.24 = (f32[16400,128]{1,0:T(8,128)S(1)}, f32[4096,128]{1,0:T(8,128)S(1)}, f32[4096,128]{1,0:T(8,128)S(1)}, f32[1024,128]{1,0:T(8,128)S(1)}) custom-call(s32[16]{0:T(128)S(1)} %get-tuple-element.178.refs_0_.refs_5_, s32[32768]{0:T(1024)S(1)} %bitcast.74, s32[32768]{0:T(1024)S(1)} %get-tuple-element.187.refs_7_.refs_2_, ...), custom_call_target="tpu_custom_call", output_to_operand_aliasing={{0}: (13, {})} | custom-call | tf_op jit(solution)/shard_map/table/pallas_call | solution.py:305
  519.5 45.6 %bucket_7.1 = (f32[4096,128]{1,0:T(8,128)S(1)}, f32[4096,128]{1,0:T(8,128)S(1)}, f32[1024,128]{1,0:T(8,128)S(1)}, f32[208,256]{1,0:T(8,128)S(1)}, f32[8,256]{1,0:T(8,128)S(1)}, /*index=5*/f32[8,256]{1,0:T(8,128)S(1)}) custom-call(f32[4096,128]{1,0:T(8,128)S(1)} %get-tuple-element.246.refs_0_, f32[4096,128]{1,0:T(8,128)S(1)} %get-tuple-element.247.refs_1_, ...), custom_call_target="tpu_custom_call" | custom-call | tf_op jit(solution)/shard_map/bucket_7/pallas_call | solution.py:693
  565.1 15.7 %table.25 = (f32[16400,128]{1,0:T(8,128)S(1)}, f32[4096,128]{1,0:T(8,128)S(1)}, f32[4096,128]{1,0:T(8,128)S(1)}, f32[1024,128]{1,0:T(8,128)S(1)}) custom-call(s32[16]{0:T(128)S(1)} %get-tuple-element.178.refs_0_.refs_5_, s32[32768]{0:T(1024)S(1)} %bitcast.76, s32[32768]{0:T(1024)S(1)} %get-tuple-element.187.refs_7_.refs_2_, ...), custom_call_target="tpu_custom_call", output_to_operand_aliasing={{0}: (13, {})} | custom-call | tf_op jit(solution)/shard_map/table/pallas_call | solution.py:305
  580.8 47.0 %bucket_8.1 = (f32[4096,128]{1,0:T(8,128)S(1)}, f32[4096,128]{1,0:T(8,128)S(1)}, f32[1024,128]{1,0:T(8,128)S(1)}, f32[208,256]{1,0:T(8,128)S(1)}, f32[8,256]{1,0:T(8,128)S(1)}, /*index=5*/f32[8,256]{1,0:T(8,128)S(1)}) custom-call(f32[4096,128]{1,0:T(8,128)S(1)} %get-tuple-element.255.refs_0_, f32[4096,128]{1,0:T(8,128)S(1)} %get-tuple-element.256.refs_1_, ...), custom_call_target="tpu_custom_call" | custom-call | tf_op jit(solution)/shard_map/bucket_8/pallas_call | solution.py:693
  627.9 16.1 %table.26 = (f32[16400,128]{1,0:T(8,128)S(1)}, f32[4096,128]{1,0:T(8,128)S(1)}, f32[4096,128]{1,0:T(8,128)S(1)}, f32[1024,128]{1,0:T(8,128)S(1)}) custom-call(s32[16]{0:T(128)S(1)} %get-tuple-element.178.refs_0_.refs_5_, s32[32768]{0:T(1024)S(1)} %bitcast.78, s32[32768]{0:T(1024)S(1)} %get-tuple-element.187.refs_7_.refs_2_, ...), custom_call_target="tpu_custom_call", output_to_operand_aliasing={{0}: (13, {})} | custom-call | tf_op jit(solution)/shard_map/table/pallas_call | solution.py:305
  644.0 54.6 %bucket_9.1 = (f32[4096,128]{1,0:T(8,128)S(1)}, f32[4096,128]{1,0:T(8,128)S(1)}, f32[1024,128]{1,0:T(8,128)S(1)}, f32[208,256]{1,0:T(8,128)S(1)}, f32[8,256]{1,0:T(8,128)S(1)}, /*index=5*/f32[8,256]{1,0:T(8,128)S(1)}) custom-call(f32[4096,128]{1,0:T(8,128)S(1)} %get-tuple-element.264.refs_0_, f32[4096,128]{1,0:T(8,128)S(1)} %get-tuple-element.265.refs_1_, ...), custom_call_target="tpu_custom_call" | custom-call | tf_op jit(solution)/shard_map/bucket_9/pallas_call | solution.py:693
  698.6 15.7 %table.27 = (f32[16400,128]{1,0:T(8,128)S(1)}, f32[4096,128]{1,0:T(8,128)S(1)}, f32[4096,128]{1,0:T(8,128)S(1)}, f32[1024,128]{1,0:T(8,128)S(1)}) custom-call(s32[16]{0:T(128)S(1)} %get-tuple-element.178.refs_0_.refs_5_, s32[32768]{0:T(1024)S(1)} %bitcast.80, s32[32768]{0:T(1024)S(1)} %get-tuple-element.187.refs_7_.refs_2_, ...), custom_call_target="tpu_custom_call", output_to_operand_aliasing={{0}: (13, {})} | custom-call | tf_op jit(solution)/shard_map/table/pallas_call | solution.py:305
  714.3 64.9 %bucket_10.1 = (f32[4096,128]{1,0:T(8,128)S(1)}, f32[4096,128]{1,0:T(8,128)S(1)}, f32[1024,128]{1,0:T(8,128)S(1)}, f32[208,256]{1,0:T(8,128)S(1)}, f32[8,256]{1,0:T(8,128)S(1)}, /*index=5*/f32[8,256]{1,0:T(8,128)S(1)}) custom-call(f32[4096,128]{1,0:T(8,128)S(1)} %get-tuple-element.273.refs_0_, f32[4096,128]{1,0:T(8,128)S(1)} %get-tuple-element.274.refs_1_, ...), custom_call_target="tpu_custom_call" | custom-call | tf_op jit(solution)/shard_map/bucket_10/pallas_call | solution.py:693
  779.2 15.9 %table.28 = (f32[16400,128]{1,0:T(8,128)S(1)}, f32[4096,128]{1,0:T(8,128)S(1)}, f32[4096,128]{1,0:T(8,128)S(1)}, f32[1024,128]{1,0:T(8,128)S(1)}) custom-call(s32[16]{0:T(128)S(1)} %get-tuple-element.178.refs_0_.refs_5_, s32[32768]{0:T(1024)S(1)} %bitcast.82, s32[32768]{0:T(1024)S(1)} %get-tuple-element.187.refs_7_.refs_2_, ...), custom_call_target="tpu_custom_call", output_to_operand_aliasing={{0}: (13, {})} | custom-call | tf_op jit(solution)/shard_map/table/pallas_call | solution.py:305
  795.1 64.0 %bucket_11.1 = (f32[4096,128]{1,0:T(8,128)S(1)}, f32[4096,128]{1,0:T(8,128)S(1)}, f32[1024,128]{1,0:T(8,128)S(1)}, f32[208,256]{1,0:T(8,128)S(1)}, f32[8,256]{1,0:T(8,128)S(1)}, /*index=5*/f32[8,256]{1,0:T(8,128)S(1)}) custom-call(f32[4096,128]{1,0:T(8,128)S(1)} %get-tuple-element.282.refs_0_, f32[4096,128]{1,0:T(8,128)S(1)} %get-tuple-element.283.refs_1_, ...), custom_call_target="tpu_custom_call" | custom-call | tf_op jit(solution)/shard_map/bucket_11/pallas_call | solution.py:693
  859.1 15.7 %table.29 = (f32[16400,128]{1,0:T(8,128)S(1)}, f32[4096,128]{1,0:T(8,128)S(1)}, f32[4096,128]{1,0:T(8,128)S(1)}, f32[1024,128]{1,0:T(8,128)S(1)}) custom-call(s32[16]{0:T(128)S(1)} %get-tuple-element.178.refs_0_.refs_5_, s32[32768]{0:T(1024)S(1)} %bitcast.84, s32[32768]{0:T(1024)S(1)} %get-tuple-element.187.refs_7_.refs_2_, ...), custom_call_target="tpu_custom_call", output_to_operand_aliasing={{0}: (13, {})} | custom-call | tf_op jit(solution)/shard_map/table/pallas_call | solution.py:305
  874.8 74.8 %bucket_12.1 = (f32[4096,128]{1,0:T(8,128)S(1)}, f32[4096,128]{1,0:T(8,128)S(1)}, f32[1024,128]{1,0:T(8,128)S(1)}, f32[208,256]{1,0:T(8,128)S(1)}, f32[8,256]{1,0:T(8,128)S(1)}, /*index=5*/f32[8,256]{1,0:T(8,128)S(1)}) custom-call(f32[4096,128]{1,0:T(8,128)S(1)} %get-tuple-element.291.refs_0_, f32[4096,128]{1,0:T(8,128)S(1)} %get-tuple-element.292.refs_1_, ...), custom_call_target="tpu_custom_call" | custom-call | tf_op jit(solution)/shard_map/bucket_12/pallas_call | solution.py:693
  949.6 15.9 %table.30 = (f32[16400,128]{1,0:T(8,128)S(1)}, f32[4096,128]{1,0:T(8,128)S(1)}, f32[4096,128]{1,0:T(8,128)S(1)}, f32[1024,128]{1,0:T(8,128)S(1)}) custom-call(s32[16]{0:T(128)S(1)} %get-tuple-element.178.refs_0_.refs_5_, s32[32768]{0:T(1024)S(1)} %bitcast.86, s32[32768]{0:T(1024)S(1)} %get-tuple-element.187.refs_7_.refs_2_, ...), custom_call_target="tpu_custom_call", output_to_operand_aliasing={{0}: (13, {})} | custom-call | tf_op jit(solution)/shard_map/table/pallas_call | solution.py:305
  965.5 63.1 %bucket_13.1 = (f32[4096,128]{1,0:T(8,128)S(1)}, f32[4096,128]{1,0:T(8,128)S(1)}, f32[1024,128]{1,0:T(8,128)S(1)}, f32[208,256]{1,0:T(8,128)S(1)}, f32[8,256]{1,0:T(8,128)S(1)}, /*index=5*/f32[8,256]{1,0:T(8,128)S(1)}) custom-call(f32[4096,128]{1,0:T(8,128)S(1)} %get-tuple-element.300.refs_0_, f32[4096,128]{1,0:T(8,128)S(1)} %get-tuple-element.301.refs_1_, ...), custom_call_target="tpu_custom_call" | custom-call | tf_op jit(solution)/shard_map/bucket_13/pallas_call | solution.py:693
  1028.6 15.7 %table.31 = (f32[16400,128]{1,0:T(8,128)S(1)}, f32[4096,128]{1,0:T(8,128)S(1)}, f32[4096,128]{1,0:T(8,128)S(1)}, f32[1024,128]{1,0:T(8,128)S(1)}) custom-call(s32[16]{0:T(128)S(1)} %get-tuple-element.178.refs_0_.refs_5_, s32[32768]{0:T(1024)S(1)} %bitcast.88, s32[32768]{0:T(1024)S(1)} %get-tuple-element.187.refs_7_.refs_2_, ...), custom_call_target="tpu_custom_call", output_to_operand_aliasing={{0}: (13, {})} | custom-call | tf_op jit(solution)/shard_map/table/pallas_call | solution.py:305
  1044.3 66.5 %bucket_14.1 = (f32[4096,128]{1,0:T(8,128)S(1)}, f32[4096,128]{1,0:T(8,128)S(1)}, f32[1024,128]{1,0:T(8,128)S(1)}, f32[208,256]{1,0:T(8,128)S(1)}, f32[8,256]{1,0:T(8,128)S(1)}, /*index=5*/f32[8,256]{1,0:T(8,128)S(1)}) custom-call(f32[4096,128]{1,0:T(8,128)S(1)} %get-tuple-element.309.refs_0_, f32[4096,128]{1,0:T(8,128)S(1)} %get-tuple-element.310.refs_1_, ...), custom_call_target="tpu_custom_call" | custom-call | tf_op jit(solution)/shard_map/bucket_14/pallas_call | solution.py:693
  1110.8 16.0 %table.32 = (f32[16400,128]{1,0:T(8,128)S(1)}, f32[4096,128]{1,0:T(8,128)S(1)}, f32[4096,128]{1,0:T(8,128)S(1)}, f32[1024,128]{1,0:T(8,128)S(1)}) custom-call(s32[16]{0:T(128)S(1)} %get-tuple-element.178.refs_0_.refs_5_, s32[32768]{0:T(1024)S(1)} %bitcast.90, s32[32768]{0:T(1024)S(1)} %get-tuple-element.187.refs_7_.refs_2_, ...), custom_call_target="tpu_custom_call", output_to_operand_aliasing={{0}: (13, {})} | custom-call | tf_op jit(solution)/shard_map/table/pallas_call | solution.py:305
  1126.8 66.0 %bucket_15.1 = (f32[4096,128]{1,0:T(8,128)S(1)}, f32[4096,128]{1,0:T(8,128)S(1)}, f32[1024,128]{1,0:T(8,128)S(1)}, f32[208,256]{1,0:T(8,128)S(1)}, f32[8,256]{1,0:T(8,128)S(1)}, /*index=5*/f32[8,256]{1,0:T(8,128)S(1)}) custom-call(f32[4096,128]{1,0:T(8,128)S(1)} %get-tuple-element.318.refs_0_, f32[4096,128]{1,0:T(8,128)S(1)} %get-tuple-element.319.refs_1_, ...), custom_call_target="tpu_custom_call" | custom-call | tf_op jit(solution)/shard_map/bucket_15/pallas_call | solution.py:693
  1192.8 12.0 table.33.t_ref
  1204.8 5.3 unpack.1
  1210.1 0.6 slice.7
  1210.8 0.2 reduce_sum.19
  1211.0 0.5 multiply_bitcast_fusion.2
  1211.5 0.7 reshape.61
  (25 shorter events, 0.2 us)
Async XLA Ops:
  7.2 5.5 copy-start.5
  7.2 5.5 copy-start.6
  7.2 5.6 copy-start.4
  7.2 15.9 %sort.17.cloned.1.call-start = ((), (), s32[]{:S(2)}) async-start(), calls=%async_computation | async-start | bytes 196640 | tf_op jit(solution)/shard_map/sort | solution.py:723
  12.8 2.9 copy-start.3
  19.8 3.3 copy-start
  24.7 3.4 copy-start.1
  28.0 49.5 %copy-start.2 = (f32[16400,128]{1,0:T(8,128)S(1)}, f32[16400,128]{1,0:T(8,128)}, u32[]{:S(2)}) copy-start(f32[16400,128]{1,0:T(8,128)} %copy-done) | copy-start | bytes 25190404
Sparse Core Ops, SparseCore 0:
  11.0 3.0 sort.19.cloned.1.call-done
  (1 shorter events, 0.0 us)
